TPU v7x, 256 devices: a whole 4x4x8 slice. The times are simulated.
256 devices in a mesh: dp: 16 (over y, x_lo, core), seq: 16 (over x_hi, z).
Axes of the slice: x: 4 (x_hi: 2, x_lo: 2; x = x_hi * 2 + x_lo), y: 4, z: 8, core: 2. Of those that a mesh axis runs over, the one named last changes fastest.
Arguments:
- queries: bfloat16 [65536, 1664], P(('dp', 'seq')), parts along dimension 0, may hold values from -6 to 6
- key_rows: bfloat16 [65536, 1664], P(('dp', 'seq')), parts along dimension 0, may hold values from -6 to 6
- value_rows: bfloat16 [65536, 1664], P(('dp', 'seq')), parts along dimension 0, may hold values from -6 to 6
Outputs:
- merged_tokens: bfloat16 [16384, 6656], P('dp', 'seq'), parts along dimension 0
There are 16 independent parts, one for each index of `dp`. A program takes and returns all parts, laid end to end along the dimension named above; each array names one. Nothing has to cross between parts.
All inputs are finite; a program needn't handle non-finite values.
Results may differ from a plain program's by a relative error of at most 0.005.
Values may be sent and summed in bfloat16 or wider, within the bound.
No kernel may reach another device: no remote copies, remote signals or barrier semaphores. Data moves between devices by JAX's collectives and lax.ppermute only.
A program may use at most 128 MiB of HBM per device.

v0:
```python
import math

import jax
import jax.numpy as jnp
from jax import lax
from jax.sharding import PartitionSpec as P

HEAD_DIM = 128
GRID_W = 64


def by_heads(queries, key_rows, value_rows, score_scale):
    tok_rows, width = queries.shape
    heads = width // HEAD_DIM
    groups = lax.axis_size("seq")
    padded_heads = -(-heads // groups) * groups

    def spread(source):
        shaped = source.reshape(tok_rows, heads, HEAD_DIM)
        shaped = jnp.pad(shaped, ((0, 0), (0, padded_heads - heads), (0, 0)))
        return shaped.reshape(tok_rows, groups, padded_heads // groups, HEAD_DIM)

    head_query = lax.all_to_all(spread(queries), "seq", split_axis=1, concat_axis=0, tiled=True)
    head_key = lax.all_to_all(spread(key_rows), "seq", split_axis=1, concat_axis=0, tiled=True)
    head_value = lax.all_to_all(spread(value_rows), "seq", split_axis=1, concat_axis=0, tiled=True)
    total_rows = head_query.shape[0]
    head_count = head_query.shape[2]
    flat_key = head_key.reshape(total_rows, head_count, HEAD_DIM)
    flat_value = head_value.reshape(total_rows, head_count, HEAD_DIM)
    step_rows = math.gcd(total_rows, 512)
    blocks = head_query.reshape(total_rows // step_rows, step_rows, head_count, HEAD_DIM)

    def one_block(query_block):
        scores = (
            jnp.einsum("qhd,khd->hqk", query_block, flat_key, preferred_element_type=jnp.float32)
            * score_scale
        )
        row_max = jnp.max(scores, axis=-1, keepdims=True)
        weights = jnp.exp(scores - row_max)
        totals = jnp.sum(weights, axis=-1, keepdims=True)
        weighted = jnp.einsum(
            "hqk,khd->qhd",
            weights.astype(jnp.bfloat16),
            flat_value,
            preferred_element_type=jnp.float32,
        )
        return (weighted / totals.transpose(1, 0, 2)).astype(jnp.bfloat16)

    result = lax.map(one_block, blocks).reshape(total_rows, 1, head_count, HEAD_DIM)
    result = lax.all_to_all(result, "seq", split_axis=0, concat_axis=1, tiled=True)
    return result.reshape(tok_rows, padded_heads, HEAD_DIM)[:, :heads].reshape(tok_rows, width)


def on_device(queries, key_rows, value_rows):
    score_scale = 1.0 / math.sqrt(HEAD_DIM)
    attended = by_heads(queries, key_rows, value_rows, score_scale)
    tok_rows, width = attended.shape
    grid_rows = tok_rows // GRID_W
    shuffled = attended.reshape(grid_rows // 2, 2, GRID_W // 2, 2, width).transpose(0, 2, 1, 3, 4)
    shuffled = shuffled.reshape(grid_rows // 2 * (GRID_W // 2), 4 * width)
    return lax.all_to_all(shuffled, "seq", split_axis=1, concat_axis=0, tiled=True)


def solution(mesh):
    placed = (P(("dp", "seq"), None), P(("dp", "seq"), None), P(("dp", "seq"), None))
    return jax.shard_map(
        on_device, mesh=mesh, in_specs=placed, out_specs=P("dp", "seq"), check_vma=False
    )
```

profile of v0, /device:TPU:16, one launch (start us, length us, event | category | flops | bytes accessed | tf_op | source)
XLA Modules:
  0.0 230.8 jit_solution(4403984086742618941)
XLA Ops:
  0.0 1.5 copy.42
  2.7 11.0 %all-to-all-start = ((bf16[256,16,1,128]{0,3,2,1:T(8,128)(2,1)}), bf16[256,16,1,128]{0,3,2,1:T(8,128)(2,1)S(1)}, u32[]{:S(2)}, u32[]{:S(2)}) async-start(bf16[256,16,1,128]{0,3,2,1:T(8,128)(2,1)} %pad_bitcast_fusion.2), calls=%async_computation | async-start | bytes 2097152 | tf_op jit(solution)/shard_map/all_to_all | solution.py:23
  13.7 1.5 copy.45
  16.4 26.0 %all-to-all-done = bf16[256,16,1,128]{0,3,2,1:T(8,128)(2,1)S(1)} async-done(((bf16[256,16,1,128]{0,3,2,1:T(8,128)(2,1)}), bf16[256,16,1,128]{0,3,2,1:T(8,128)(2,1)S(1)}, u32[]{:S(2)}, u32[]{:S(2)}) %all-to-all-start) | async-done | bytes 1048608 | tf_op jit(solution)/shard_map/all_to_all | solution.py:23
  42.4 4.4 %all-to-all-start.1 = ((bf16[256,16,1,128]{0,3,2,1:T(8,128)(2,1)}), bf16[256,16,1,128]{0,3,2,1:T(8,128)(2,1)S(1)}, u32[]{:S(2)}, u32[]{:S(2)}) async-start(bf16[256,16,1,128]{0,3,2,1:T(8,128)(2,1)} %pad_bitcast_fusion.1), calls=%async_computation.1 | async-start | bytes 2097152 | tf_op jit(solution)/shard_map/all_to_all | solution.py:24
  46.7 1.5 copy.48
  49.3 26.2 %all-to-all-done.1 = bf16[256,16,1,128]{0,3,2,1:T(8,128)(2,1)S(1)} async-done(((bf16[256,16,1,128]{0,3,2,1:T(8,128)(2,1)}), bf16[256,16,1,128]{0,3,2,1:T(8,128)(2,1)S(1)}, u32[]{:S(2)}, u32[]{:S(2)}) %all-to-all-start.1) | async-done | bytes 1048608 | tf_op jit(solution)/shard_map/all_to_all | solution.py:24
  75.5 4.4 %all-to-all-start.2 = ((bf16[256,16,1,128]{0,3,2,1:T(8,128)(2,1)}), bf16[256,16,1,128]{0,3,2,1:T(8,128)(2,1)S(1)}, u32[]{:S(2)}, u32[]{:S(2)}) async-start(bf16[256,16,1,128]{0,3,2,1:T(8,128)(2,1)} %pad_bitcast_fusion), calls=%async_computation.2 | async-start | bytes 2097152 | tf_op jit(solution)/shard_map/all_to_all | solution.py:25
  81.9 26.8 %all-to-all-done.2 = bf16[256,16,1,128]{0,3,2,1:T(8,128)(2,1)S(1)} async-done(((bf16[256,16,1,128]{0,3,2,1:T(8,128)(2,1)}), bf16[256,16,1,128]{0,3,2,1:T(8,128)(2,1)S(1)}, u32[]{:S(2)}, u32[]{:S(2)}) %all-to-all-start.2) | async-done | bytes 1048608 | tf_op jit(solution)/shard_map/all_to_all | solution.py:25
  109.4 47.1 %while.10 = (s32[]{:T(128)}, bf16[8,512,1,128]{3,1,2,0:T(8,128)(2,1)}, bf16[8,512,1,128]{3,1,2,0:T(8,128)(2,1)}, bf16[4096,1,128]{2,0,1:T(8,128)(2,1)S(1)}, bf16[4096,1,128]{2,0,1:T(8,128)(2,1)S(1)}, /*index=5*/s32[]{:T(128)}) while((s32[]{:T(128)}, bf16[8,512,1,128]{3,1,2,0:T(8,128)(2,1)}, bf16[8,512,1,128]{3,1,2,0:T(8,128)(2,1)}, ...), condition=%wide.region_3.4_spmd, body=%wide.region_0.3_spmd.sunk | while | flops 1090649088 | bytes 27536452 | solution.py:49
  109.4 2.2 multiply_reduce_fusion.2
  111.6 1.5 fusion.32
  113.1 2.1 fusion.33
  115.3 2.2 multiply_reduce_fusion.2
  119.0 2.1 fusion.33
  121.1 2.2 multiply_reduce_fusion.2
  124.9 2.1 fusion.33
  127.0 2.2 multiply_reduce_fusion.2
  129.3 1.5 fusion.32
  130.8 2.1 fusion.33
  132.9 2.2 multiply_reduce_fusion.2
  136.6 2.1 fusion.33
  138.8 2.2 multiply_reduce_fusion.2
  141.0 1.5 fusion.32
  142.5 2.1 fusion.33
  144.7 2.2 multiply_reduce_fusion.2
  148.4 2.1 fusion.33
  150.5 2.2 multiply_reduce_fusion.2
  154.3 2.1 fusion.33
  156.9 2.7 %reduce.4 = bf16[4096,128]{1,0:T(8,128)(2,1)S(1)} reduce(bf16[4096,1,1,128]{3,0,2,1:T(8,128)(2,1)} %bitcast.91, bf16[]{:T(256)} %broadcast.30), dimensions={1,2}, to_apply=%copy.52.reduce_sub_computation | reduce | bytes 2097154 | tf_op jit(solution)/shard_map/reshape | solution.py:49
  159.9 32.5 %all_to_all.79 = bf16[16,2,16384]{2,1,0:T(2,128)(2,1)S(1)} all-to-all(bf16[16,2,16384]{2,1,0:T(2,128)(2,1)S(1)} %reshape.81), channel_id=1, replica_groups=mesh['dp'=16,'seq'=16] {'seq'}, dimensions={0} | all-to-all | bytes 2097152 | tf_op jit(solution)/shard_map/all_to_all | solution.py:50
  197.0 32.6 %all_to_all.80 = bf16[64,16,416]{2,0,1:T(8,128)(2,1)S(1)} all-to-all(bf16[64,16,416]{2,0,1:T(8,128)(2,1)S(1)} %copy.55), channel_id=1, replica_groups=mesh['dp'=16,'seq'=16] {'seq'}, dimensions={1} | all-to-all | bytes 1703936 | tf_op jit(solution)/shard_map/all_to_all | solution.py:61
  (23 shorter events, 20.1 us)
Async XLA Ops:
  2.7 39.7 %all-to-all-start = ((bf16[256,16,1,128]{0,3,2,1:T(8,128)(2,1)}), bf16[256,16,1,128]{0,3,2,1:T(8,128)(2,1)S(1)}, u32[]{:S(2)}, u32[]{:S(2)}) async-start(bf16[256,16,1,128]{0,3,2,1:T(8,128)(2,1)} %pad_bitcast_fusion.2), calls=%async_computation | async-start | bytes 2097152 | tf_op jit(solution)/shard_map/all_to_all | solution.py:23
  42.4 33.2 %all-to-all-start.1 = ((bf16[256,16,1,128]{0,3,2,1:T(8,128)(2,1)}), bf16[256,16,1,128]{0,3,2,1:T(8,128)(2,1)S(1)}, u32[]{:S(2)}, u32[]{:S(2)}) async-start(bf16[256,16,1,128]{0,3,2,1:T(8,128)(2,1)} %pad_bitcast_fusion.1), calls=%async_computation.1 | async-start | bytes 2097152 | tf_op jit(solution)/shard_map/all_to_all | solution.py:24
  75.5 33.2 %all-to-all-start.2 = ((bf16[256,16,1,128]{0,3,2,1:T(8,128)(2,1)}), bf16[256,16,1,128]{0,3,2,1:T(8,128)(2,1)S(1)}, u32[]{:S(2)}, u32[]{:S(2)}) async-start(bf16[256,16,1,128]{0,3,2,1:T(8,128)(2,1)} %pad_bitcast_fusion), calls=%async_computation.2 | async-start | bytes 2097152 | tf_op jit(solution)/shard_map/all_to_all | solution.py:25
where the time goes:
time: 231 us
  waiting for transfers between devices  79 us (34%)
  blocking collectives  65.1 us (28%)
  matrix products  35 us (15%)
  starting transfers between devices  19.8 us (9%)
  local copies, waits for them, and re-layouts  17.1 us (7%)
  other arithmetic  14.7 us (6%)
    all_to_all x1, blocking collectives, on_device(): lax.all_to_all(shuffled, 'seq', split_axis=1, concat_axis=0, tiled=True)  32.6 us
    all_to_all x1, blocking collectives, by_heads(): lax.all_to_all(result, 'seq', split_axis=0, concat_axis=1, tiled=True)  32.5 us
    all_to_all x1, waiting for transfers between devices, by_heads(): lax.all_to_all(spread(value_rows), 'seq', split_axis=1, concat_axis=0, ti...  26.8 us
    all_to_all x1, waiting for transfers between devices, by_heads(): lax.all_to_all(spread(key_rows), 'seq', split_axis=1, concat_axis=0, tile...  26.2 us
    all_to_all x1, waiting for transfers between devices, by_heads(): lax.all_to_all(spread(queries), 'seq', split_axis=1, concat_axis=0, tiled...  26 us
    dot_general x8, matrix products, one_block(): jnp.einsum('qhd,khd->hqk', query_block, flat_key, preferred_element_type=...  17.9 us
    dot_general x8, matrix products, one_block(): jnp.einsum('hqk,khd->qhd', weights.astype(jnp.bfloat16), flat_value, pref...  17.1 us
    reduce_sum x8, other arithmetic, one_block(): totals = jnp.sum(weights, axis=-1, keepdims=True)  12.1 us
  transfers between devices with their start and end apart: 3, of which 3 were waited for; matrix products, arithmetic and copies ran while one was open for 3% of the time, Pallas kernels for 0%

commit v1 on v0

v1 whole, which is shorter than its diff:
```python
import math

import jax
import jax.numpy as jnp
import numpy as np
from jax import lax
from jax.experimental import pallas as pl
from jax.experimental.pallas import tpu as pltpu
from jax.sharding import PartitionSpec as P


HEAD_DIM = 128
HEADS = 13
SEQ = 16
TOK = 256
LOC = 64
OUT_COLS = 416
FAR = 1 << 20
LOG2_SCALE = math.log2(math.e) / math.sqrt(HEAD_DIM)


IDLE = (((), (0,), (1,), (3,)), ((), (3,), (2,), (0,)))
CHUNK_HEADS = ((0, 1, 2, 3), (4, 5, 6), (7, 8, 9), (10, 11, 12))

ROTATIONS = ((0, 0), (0, 4), (1, 4), (0, 3), (0, 5), (1, 3), (1, 5), (0, 2), (0, 6), (1, 2), (1, 6), (0, 1), (0, 7),
             (1, 1), (1, 7), (1, 0))
XORS = (3, 1, 2, 0)


def place_heads():
    head_of = np.full((2, SEQ), -1, np.int32)
    for core in range(2):
        for chunk in range(4):
            places = [p for p in range(4) if p not in IDLE[core][chunk]]
            for place, head in zip(places, CHUNK_HEADS[chunk]):
                head_of[core, place * 4 + chunk] = head
    return head_of


HEAD_OF = place_heads()


def turn(seq, rotation, sign=1):
    dx, dz = rotation
    return ((seq // 8) ^ dx) * 8 + (seq % 8 + sign * dz) % 8


def tables():
    send = np.zeros((2, SEQ, 16), np.int32)
    source = np.zeros((2, SEQ, 16), np.int32)
    shift = np.full((2, SEQ, 5), FAR, np.int32)
    for core in range(2):
        for seq in range(SEQ):
            for r, rotation in enumerate(ROTATIONS):
                send[core, seq, r] = max(HEAD_OF[core, turn(seq, rotation)], 0)
                source[core, seq, r] = turn(seq, rotation, -1)
            chunk, place = seq % 4, seq // 4
            for j, flip in enumerate(XORS):
                head = HEAD_OF[core, (place ^ flip) * 4 + chunk]
                if head >= 0:
                    shift[core, seq, j] = head * HEAD_DIM - chunk * OUT_COLS
            if chunk > 0:
                shift[core, seq, 4] = CHUNK_HEADS[chunk - 1][-1] * HEAD_DIM - chunk * OUT_COLS
    return send, source, shift


SEND, SOURCE, SHIFT = tables()


def last_index():
    table = np.zeros((2, SEQ), np.int32)
    for core in range(2):
        for seq in range(SEQ):
            chunk, place = seq % 4, seq // 4
            for j, flip in enumerate(XORS):
                if HEAD_OF[core, (place ^ flip) * 4 + chunk] == CHUNK_HEADS[chunk][-1]:
                    table[core, seq] = j
    return table


LAST = last_index()


def pairs(step, active):
    out = []
    for dp in range(16):
        for seq in range(SEQ):
            target = step(seq)
            if target is not None and active(dp % 2, seq, target):
                out.append((dp * SEQ + seq, dp * SEQ + target))
    return out


def pack_kernel(send_ref, q_ref, k_ref, v_ref, *refs):
    outs, q_sorted = refs[:16], refs[16]
    row = lax.broadcasted_iota(jnp.int32, (TOK, TOK), 0)
    col = lax.broadcasted_iota(jnp.int32, (TOK, TOK), 1)
    grid_row, grid_col = col // 64, col % 64
    wanted = ((grid_row % 2) * 2 + grid_col % 2) * LOC + (grid_row // 2) * 32 + grid_col // 2
    order = jnp.where(row == wanted, 1.0, 0.0).astype(jnp.bfloat16)
    q_sorted[...] = jnp.dot(order, q_ref[...], preferred_element_type=jnp.float32).astype(jnp.bfloat16)
    for r in range(16):
        at = pl.ds(pl.multiple_of(send_ref[r] * HEAD_DIM, HEAD_DIM), HEAD_DIM)
        outs[r][0:TOK, :] = q_sorted[:, at]
        outs[r][TOK:2 * TOK, :] = k_ref[:, at]
        outs[r][2 * TOK:, :] = v_ref[:, at]


def pack(send, queries, key_rows, value_rows):
    shape = jax.ShapeDtypeStruct((3 * TOK, HEAD_DIM), jnp.bfloat16)
    full = pl.BlockSpec(memory_space=pltpu.VMEM)
    return pl.pallas_call(
        pack_kernel,
        in_specs=[pl.BlockSpec(memory_space=pltpu.SMEM), full, full, full],
        out_specs=[full] * 16,
        out_shape=[shape] * 16,
        scratch_shapes=[pltpu.VMEM((TOK, HEADS * HEAD_DIM), jnp.bfloat16)],
        compiler_params=pltpu.CompilerParams(vmem_limit_bytes=24 * 2**20),
        name="pack",
    )(send, queries, key_rows, value_rows)


def gather_kernel(*refs):
    got, (q_out, k_out, v_out) = refs[:4], refs[4:]
    for i in range(4):
        for klass in range(4):
            q_out[klass, i * LOC:(i + 1) * LOC, :] = got[i][klass * LOC:(klass + 1) * LOC, :]
        k_out[i * TOK:(i + 1) * TOK, :] = got[i][TOK:2 * TOK, :]
        v_out[:, i * TOK:(i + 1) * TOK] = got[i][2 * TOK:, :].T


def gather_group(messages):
    full = pl.BlockSpec(memory_space=pltpu.VMEM)
    return pl.pallas_call(
        gather_kernel,
        in_specs=[full] * 4,
        out_specs=[full] * 3,
        out_shape=[
            jax.ShapeDtypeStruct((4, 4 * LOC, HEAD_DIM), jnp.bfloat16),
            jax.ShapeDtypeStruct((4 * TOK, HEAD_DIM), jnp.bfloat16),
            jax.ShapeDtypeStruct((HEAD_DIM, 4 * TOK), jnp.bfloat16),
        ],
        compiler_params=pltpu.CompilerParams(vmem_limit_bytes=16 * 2**20),
        name="gather_group",
    )(*messages)


def attend_kernel(klass_ref, source_ref, *refs):
    queries, keys, values, out_ref = refs[:4], refs[4:8], refs[8:12], refs[12]
    half = pl.program_id(0)
    step = 512
    q = jnp.concatenate([jnp.where(half == 0, queries[i][0], queries[i + 2][0]) for i in range(2)], axis=0)
    scaled = q.astype(jnp.float32) * LOG2_SCALE
    high = scaled.astype(jnp.bfloat16)
    low = (scaled - high.astype(jnp.float32)).astype(jnp.bfloat16)
    rhs = jnp.concatenate([high, low], axis=1)
    top = total = acc = None
    for g in range(4):
        for at in range(0, 4 * TOK, step):
            k = keys[g][at:at + step, :]
            scores = lax.dot_general(jnp.concatenate([k, k], axis=1), rhs, (((1,), (1,)), ((), ())),
                                     preferred_element_type=jnp.float32)
            own = jnp.max(scores, axis=0, keepdims=True)
            new_top = own if top is None else jnp.maximum(top, own)
            weights = jnp.exp2(scores - new_top)
            part = jnp.sum(weights, axis=0, keepdims=True)
            out = jnp.dot(values[g][:, at:at + step], weights.astype(jnp.bfloat16),
                          preferred_element_type=jnp.float32)
            if top is None:
                total, acc = part, out
            else:
                fade = jnp.exp2(top - new_top)
                total, acc = total * fade + part, acc * fade + out
            top = new_top
    done = (acc / total).T.astype(jnp.bfloat16)
    for i in range(8):
        row = pl.multiple_of(source_ref[8 * half + i] * LOC, LOC)
        out_ref[pl.ds(row, LOC), :] = done[i * LOC:(i + 1) * LOC, :]


def attend(klass, source, groups):
    full = pl.BlockSpec(memory_space=pltpu.VMEM)
    rows = SEQ * LOC
    grid_spec = pltpu.PrefetchScalarGridSpec(
        num_scalar_prefetch=2,
        grid=(2,),
        in_specs=[pl.BlockSpec((1, 4 * LOC, HEAD_DIM), lambda i, klass, source: (klass[0], 0, 0))] * 4
        + [pl.BlockSpec((4 * TOK, HEAD_DIM), lambda i, klass, source: (0, 0))] * 4
        + [pl.BlockSpec((HEAD_DIM, 4 * TOK), lambda i, klass, source: (0, 0))] * 4,
        out_specs=pl.BlockSpec((rows, HEAD_DIM), lambda i, klass, source: (0, 0)),
    )
    return pl.pallas_call(
        attend_kernel,
        grid_spec=grid_spec,
        out_shape=jax.ShapeDtypeStruct((rows, HEAD_DIM), jnp.bfloat16),
        cost_estimate=pl.CostEstimate(flops=4 * rows * SEQ * TOK * HEAD_DIM, transcendentals=rows * SEQ * TOK,
                                      bytes_accessed=2 * 3 * SEQ * TOK * HEAD_DIM),
        compiler_params=pltpu.CompilerParams(vmem_limit_bytes=32 * 2**20),
        name="attend",
    )(klass, source, *[g[0] for g in groups], *[g[1] for g in groups], *[g[2] for g in groups])


def merge_kernel(shift_ref, *refs):
    blocks, out_ref = refs[:5], refs[5]
    row = lax.broadcasted_iota(jnp.int32, (HEAD_DIM, OUT_COLS), 0)
    col = lax.broadcasted_iota(jnp.int32, (HEAD_DIM, OUT_COLS), 1)
    picks = [jnp.where(col == row + shift_ref[j], 1.0, 0.0).astype(jnp.bfloat16) for j in range(5)]
    block = jnp.concatenate([ref[...] for ref in blocks], axis=1)
    out_ref[...] = jnp.dot(block, jnp.concatenate(picks, axis=0),
                           preferred_element_type=jnp.float32).astype(jnp.bfloat16)


def merge(shift, blocks):
    rows = SEQ * LOC
    full = pl.BlockSpec(memory_space=pltpu.VMEM)
    return pl.pallas_call(
        merge_kernel,
        in_specs=[pl.BlockSpec(memory_space=pltpu.SMEM)] + [full] * 5,
        out_specs=full,
        out_shape=jax.ShapeDtypeStruct((rows, OUT_COLS), jnp.bfloat16),
        compiler_params=pltpu.CompilerParams(vmem_limit_bytes=24 * 2**20),
        name="merge",
    )(shift, *blocks)


def exchange_and_attend(queries, key_rows, value_rows):
    axes = ("dp", "seq")
    core = lax.axis_index("dp") % 2
    seq = lax.axis_index("seq")
    send = jnp.asarray(SEND)[core, seq]
    source = jnp.asarray(SOURCE)[core, seq]
    shift = jnp.asarray(SHIFT)[core, seq]
    last = jnp.asarray(LAST)[core, seq]

    messages = pack(send, queries, key_rows, value_rows)
    got = [messages[0]]
    for r in range(1, 16):
        perm = pairs(lambda s: turn(s, ROTATIONS[r]), lambda core, s, t: HEAD_OF[core, t] >= 0)
        got.append(lax.ppermute(messages[r], axes, perm))
    groups = [gather_group(got[i:i + 4]) for i in range(0, 16, 4)]

    blocks = []
    for flip in XORS:
        klass = ((seq // 4) ^ flip).reshape(1)
        out = attend(klass, source, groups)
        if flip:
            perm = pairs(lambda s: ((s // 4) ^ flip) * 4 + s % 4, lambda core, s, t: HEAD_OF[core, s] >= 0)
            out = lax.ppermute(out, axes, perm)
        blocks.append(out)
    tail = blocks[0]
    for j in range(1, 4):
        tail = jnp.where(last == j, blocks[j], tail)
    perm = pairs(lambda s: s + 1 if s % 4 < 3 else None, lambda core, s, t: True)
    blocks.append(lax.ppermute(tail, axes, perm))
    return merge(shift, blocks)


def solution(mesh):
    placed = (P(("dp", "seq"), None), P(("dp", "seq"), None), P(("dp", "seq"), None))
    return jax.shard_map(exchange_and_attend, mesh=mesh, in_specs=placed, out_specs=P("dp", "seq"), check_vma=False)
```

time: 231 us -> 165 us (0.71)
  the two profiles are of different devices: /device:TPU:16 before, /device:TPU:50 now
where the time goes in v1:
time: 165 us
  starting transfers between devices  70.5 us (43%)
  waiting for transfers between devices  43.5 us (26%)
  Pallas kernels  40.8 us (25%)
  local copies, waits for them, and re-layouts  7.39 us (4%)
  between operations  2.3 us (1%)
    ppermute x15, starting transfers between devices, exchange_and_attend(): got.append(lax.ppermute(messages[r], axes, perm))  64.5 us
    pallas_call x4, Pallas kernels, attend(): pl.pallas_call(attend_kernel, grid_spec=grid_spec, out_shape=jax.ShapeDty...  36.7 us
    ppermute x3, waiting for transfers between devices, exchange_and_attend(): out = lax.ppermute(out, axes, perm)  18.5 us
    ppermute x15, waiting for transfers between devices, exchange_and_attend(): got.append(lax.ppermute(messages[r], axes, perm))  17.4 us
    ppermute x1, waiting for transfers between devices, exchange_and_attend(): blocks.append(lax.ppermute(tail, axes, perm))  7.51 us
    ppermute x3, starting transfers between devices, exchange_and_attend(): out = lax.ppermute(out, axes, perm)  4.06 us
    unnamed x8, local copies, waits for them, and re-layouts  3.47 us
  transfers between devices with their start and end apart: 19, of which 6 were waited for; matrix products, arithmetic and copies ran while one was open for 1% of the time, Pallas kernels for 6%

profile of v1, /device:TPU:50, one launch (start us, length us, event | category | flops | bytes accessed | tf_op | source)
XLA Modules:
  0.0 164.5 jit_solution(10853497598299849011)
XLA Ops:
  0.7 1.2 copy-done
  1.9 1.2 copy-done.1
  3.0 1.2 copy-done.2
  4.2 2.1 %pack.1 = (bf16[768,128]{1,0:T(8,128)(2,1)S(1)}, bf16[768,128]{1,0:T(8,128)(2,1)S(1)}, bf16[768,128]{1,0:T(8,128)(2,1)S(1)}, bf16[768,128]{1,0:T(8,128)(2,1)S(1)...) custom-call(s32[16]{0:T(128)S(1)} %fusion.2.send_ref, ...), custom_call_target="tpu_custom_call" | custom-call | tf_op jit(solution)/shard_map/pack/pallas_call | solution.py:112
  6.3 8.2 %collective-permute-start = (bf16[768,128]{1,0:T(8,128)(2,1)S(1)}, bf16[768,128]{1,0:T(8,128)(2,1)S(1)}, u32[]{:S(2)}, u32[]{:S(2)}) collective-permute-start(bf16[768,128]{1,0:T(8,128)(2,1)S(1)} %get-tuple-element.34), channel_id=1, source_target_pairs={{0,4},{1,5},{3,7},{4,0},{6,2},{7,3},{8,12},{9,13},{10,14},{12,8},{... | collective-permute-start | bytes 589832 | tf_op jit(solution)/shard_map/ppermute | solution.py:239
  14.5 3.5 %collective-permute-start.1 = (bf16[768,128]{1,0:T(8,128)(2,1)S(1)}, bf16[768,128]{1,0:T(8,128)(2,1)S(1)}, u32[]{:S(2)}, u32[]{:S(2)}) collective-permute-start(bf16[768,128]{1,0:T(8,128)(2,1)S(1)} %get-tuple-element.35), channel_id=1, source_target_pairs={{0,12},{1,13},{2,14},{4,8},{5,9},{6,10},{7,11},{8,4},{9,5},{11,7},... | collective-permute-start | bytes 589832 | tf_op jit(solution)/shard_map/ppermute | solution.py:239
  18.0 7.4 %collective-permute-start.2 = (bf16[768,128]{1,0:T(8,128)(2,1)S(1)}, bf16[768,128]{1,0:T(8,128)(2,1)S(1)}, u32[]{:S(2)}, u32[]{:S(2)}) collective-permute-start(bf16[768,128]{1,0:T(8,128)(2,1)S(1)} %get-tuple-element.36), channel_id=1, source_target_pairs={{0,3},{1,4},{2,5},{4,7},{5,0},{7,2},{8,11},{9,12},{10,13},{11,14},... | collective-permute-start | bytes 589832 | tf_op jit(solution)/shard_map/ppermute | solution.py:239
  26.0 9.0 %collective-permute-start.4 = (bf16[768,128]{1,0:T(8,128)(2,1)S(1)}, bf16[768,128]{1,0:T(8,128)(2,1)S(1)}, u32[]{:S(2)}, u32[]{:S(2)}) collective-permute-start(bf16[768,128]{1,0:T(8,128)(2,1)S(1)} %get-tuple-element.39), channel_id=1, source_target_pairs={{0,11},{1,12},{2,13},{3,14},{5,8},{6,9},{7,10},{8,3},{9,4},{10,5},... | collective-permute-start | bytes 589832 | tf_op jit(solution)/shard_map/ppermute | solution.py:239
  35.1 1.3 collective-permute-start.5
  36.4 1.3 collective-permute-start.6
  37.7 7.0 %collective-permute-done.2.refs_3_ = bf16[768,128]{1,0:T(8,128)(2,1)S(1)} collective-permute-done((bf16[768,128]{1,0:T(8,128)(2,1)S(1)}, bf16[768,128]{1,0:T(8,128)(2,1)S(1)}, u32[]{:S(2)}, u32[]{:S(2)}) %collective-permute-start.2) | collective-permute-done | bytes 196640 | tf_op jit(solution)/shard_map/ppermute | solution.py:239
  44.7 7.1 %collective-permute-start.7 = (bf16[768,128]{1,0:T(8,128)(2,1)S(1)}, bf16[768,128]{1,0:T(8,128)(2,1)S(1)}, u32[]{:S(2)}, u32[]{:S(2)}) collective-permute-start(bf16[768,128]{1,0:T(8,128)(2,1)S(1)} %get-tuple-element.43), channel_id=1, source_target_pairs={{1,7},{2,0},{4,2},{5,3},{6,4},{7,5},{8,14},{10,8},{11,9},{12,10},{... | collective-permute-start | bytes 589832 | tf_op jit(solution)/shard_map/ppermute | solution.py:239
  51.8 1.3 collective-permute-start.8
  53.1 5.1 %collective-permute-done.4.refs_1_ = bf16[768,128]{1,0:T(8,128)(2,1)S(1)} collective-permute-done((bf16[768,128]{1,0:T(8,128)(2,1)S(1)}, bf16[768,128]{1,0:T(8,128)(2,1)S(1)}, u32[]{:S(2)}, u32[]{:S(2)}) %collective-permute-start.4) | collective-permute-done | bytes 196640 | tf_op jit(solution)/shard_map/ppermute | solution.py:239
  58.9 8.7 %collective-permute-start.10 = (bf16[768,128]{1,0:T(8,128)(2,1)}, bf16[768,128]{1,0:T(8,128)(2,1)S(1)}, u32[]{:S(2)}, u32[]{:S(2)}) collective-permute-start(bf16[768,128]{1,0:T(8,128)(2,1)} %get-tuple-element.46), channel_id=1, source_target_pairs={{1,2},{2,3},{3,4},{4,5},{6,7},{7,0},{8,9},{9,10},{10,11},{11,12},{... | collective-permute-start | bytes 589832 | tf_op jit(solution)/shard_map/ppermute | solution.py:239
  67.6 1.3 collective-permute-start.11
  68.9 7.3 %collective-permute-start.12 = (bf16[768,128]{1,0:T(8,128)(2,1)}, bf16[768,128]{1,0:T(8,128)(2,1)S(1)}, u32[]{:S(2)}, u32[]{:S(2)}) collective-permute-start(bf16[768,128]{1,0:T(8,128)(2,1)} %get-tuple-element.49), channel_id=1, source_target_pairs={{0,9},{1,10},{2,11},{3,12},{4,13},{5,14},{7,8},{9,2},{10,3},{11,4}... | collective-permute-start | bytes 589832 | tf_op jit(solution)/shard_map/ppermute | solution.py:239
  76.3 1.3 collective-permute-start.13
  77.6 5.5 %collective-permute-start.14 = (bf16[768,128]{1,0:T(8,128)(2,1)S(1)}, bf16[768,128]{1,0:T(8,128)(2,1)S(1)}, u32[]{:S(2)}, u32[]{:S(2)}) collective-permute-start(bf16[768,128]{1,0:T(8,128)(2,1)S(1)} %get-tuple-element.51), channel_id=1, source_target_pairs={{0,8},{1,9},{2,10},{3,11},{4,12},{5,13},{6,14},{8,0},{10,2},{11,3}... | collective-permute-start | bytes 589832 | tf_op jit(solution)/shard_map/ppermute | solution.py:239
  84.2 5.3 %collective-permute-done.14.refs_3_ = bf16[768,128]{1,0:T(8,128)(2,1)S(1)} collective-permute-done((bf16[768,128]{1,0:T(8,128)(2,1)S(1)}, bf16[768,128]{1,0:T(8,128)(2,1)S(1)}, u32[]{:S(2)}, u32[]{:S(2)}) %collective-permute-start.14) | collective-permute-done | bytes 196640 | tf_op jit(solution)/shard_map/ppermute | solution.py:239
  89.7 9.2 %attend.6 = bf16[1024,128]{1,0:T(8,128)(2,1)S(1)} custom-call(s32[1]{0:T(128)} %bitcast.5.klass_ref, s32[16]{0:T(128)S(1)} %fusion.1.source_ref, bf16[4,256,128]{2,1,0:T(8,128)(2,1)S(1)} %get-tuple-element.37.refs_0_, bf16[4,256,128]{2,1,0:T(8,128)(2,1)S(1)} %get-tuple-element.42.refs_1_, bf16[4,256,128]{2,1,0:T(8,128)(2,1)S(1)} %get-tuple-element.47.refs_2_, ...), custom_call_target="tpu_custom_call" | custom-call | flops 2147483648 | bytes 3145728 | tf_op jit(solution)/shard_map/attend/pallas_call | solution.py:192
  98.8 9.2 %attend.5 = bf16[1024,128]{1,0:T(8,128)(2,1)S(1)} custom-call(s32[1]{0:T(128)} %bitcast.4.klass_ref, s32[16]{0:T(128)S(1)} %fusion.1.source_ref, bf16[4,256,128]{2,1,0:T(8,128)(2,1)S(1)} %get-tuple-element.37.refs_0_, bf16[4,256,128]{2,1,0:T(8,128)(2,1)S(1)} %get-tuple-element.42.refs_1_, bf16[4,256,128]{2,1,0:T(8,128)(2,1)S(1)} %get-tuple-element.47.refs_2_, ...), custom_call_target="tpu_custom_call" | custom-call | flops 2147483648 | bytes 3145728 | tf_op jit(solution)/shard_map/attend/pallas_call | solution.py:192
  108.0 9.2 %attend.4 = bf16[1024,128]{1,0:T(8,128)(2,1)S(1)} custom-call(s32[1]{0:T(128)} %bitcast.1.klass_ref, s32[16]{0:T(128)S(1)} %fusion.1.source_ref, bf16[4,256,128]{2,1,0:T(8,128)(2,1)S(1)} %get-tuple-element.37.refs_0_, bf16[4,256,128]{2,1,0:T(8,128)(2,1)S(1)} %get-tuple-element.42.refs_1_, bf16[4,256,128]{2,1,0:T(8,128)(2,1)S(1)} %get-tuple-element.47.refs_2_, ...), custom_call_target="tpu_custom_call" | custom-call | flops 2147483648 | bytes 3145728 | tf_op jit(solution)/shard_map/attend/pallas_call | solution.py:192
  117.2 1.3 collective-permute-start.15
  118.5 1.3 collective-permute-start.16
  119.8 1.5 collective-permute-start.17
  123.8 9.2 %attend.7.refs_3_ = bf16[1024,128]{1,0:T(8,128)(2,1)S(1)} custom-call(s32[1]{0:T(128)} %bitcast.6.klass_ref, s32[16]{0:T(128)S(1)} %fusion.1.source_ref, bf16[4,256,128]{2,1,0:T(8,128)(2,1)S(1)} %get-tuple-element.37.refs_0_, bf16[4,256,128]{2,1,0:T(8,128)(2,1)S(1)} %get-tuple-element.42.refs_1_, bf16[4,256,128]{2,1,0:T(8,128)(2,1)S(1)} %get-tuple-element.47.refs_2_, ...), custom_call_target="tpu_custom_call" | custom-call | flops 2147483648 | bytes 3145728 | tf_op jit(solution)/shard_map/attend/pallas_call | solution.py:192
  134.0 17.6 %collective-permute-done.16.refs_1_ = bf16[1024,128]{1,0:T(8,128)(2,1)S(1)} collective-permute-done((bf16[1024,128]{1,0:T(8,128)(2,1)S(1)}, bf16[1024,128]{1,0:T(8,128)(2,1)S(1)}, u32[]{:S(2)}, u32[]{:S(2)}) %collective-permute-start.16) | collective-permute-done | bytes 262176 | tf_op jit(solution)/shard_map/ppermute | solution.py:248
  151.6 1.9 %collective-permute-start.18 = (bf16[1024,128]{1,0:T(8,128)(2,1)S(1)}, bf16[1024,128]{1,0:T(8,128)(2,1)S(1)}, u32[]{:S(2)}, u32[]{:S(2)}) collective-permute-start(bf16[1024,128]{1,0:T(8,128)(2,1)S(1)} %select_select_fusion), channel_id=1, source_target_pairs={{0,1},{1,2},{2,3},{4,5},{5,6},{6,7},{8,9},{9,10},{10,11},{12,13},{... | collective-permute-start | bytes 786440 | tf_op jit(solution)/shard_map/ppermute | solution.py:254
  154.3 7.5 %collective-permute-done.18.refs_4_ = bf16[1024,128]{1,0:T(8,128)(2,1)S(1)} collective-permute-done((bf16[1024,128]{1,0:T(8,128)(2,1)S(1)}, bf16[1024,128]{1,0:T(8,128)(2,1)S(1)}, u32[]{:S(2)}, u32[]{:S(2)}) %collective-permute-start.18) | collective-permute-done | bytes 262176 | tf_op jit(solution)/shard_map/ppermute | solution.py:254
  161.8 1.5 merge.1
  163.3 1.2 copy.8
  (30 shorter events, 5.6 us)
Async XLA Ops:
  0.7 1.2 copy-start
  1.8 1.2 copy-start.1
  3.0 1.2 copy-start.2
  6.3 28.8 %collective-permute-start = (bf16[768,128]{1,0:T(8,128)(2,1)S(1)}, bf16[768,128]{1,0:T(8,128)(2,1)S(1)}, u32[]{:S(2)}, u32[]{:S(2)}) collective-permute-start(bf16[768,128]{1,0:T(8,128)(2,1)S(1)} %get-tuple-element.34), channel_id=1, source_target_pairs={{0,4},{1,5},{3,7},{4,0},{6,2},{7,3},{8,12},{9,13},{10,14},{12,8},{... | collective-permute-start | bytes 589832 | tf_op jit(solution)/shard_map/ppermute | solution.py:239
  14.5 21.9 %collective-permute-start.1 = (bf16[768,128]{1,0:T(8,128)(2,1)S(1)}, bf16[768,128]{1,0:T(8,128)(2,1)S(1)}, u32[]{:S(2)}, u32[]{:S(2)}) collective-permute-start(bf16[768,128]{1,0:T(8,128)(2,1)S(1)} %get-tuple-element.35), channel_id=1, source_target_pairs={{0,12},{1,13},{2,14},{4,8},{5,9},{6,10},{7,11},{8,4},{9,5},{11,7},... | collective-permute-start | bytes 589832 | tf_op jit(solution)/shard_map/ppermute | solution.py:239
  18.0 26.7 %collective-permute-start.2 = (bf16[768,128]{1,0:T(8,128)(2,1)S(1)}, bf16[768,128]{1,0:T(8,128)(2,1)S(1)}, u32[]{:S(2)}, u32[]{:S(2)}) collective-permute-start(bf16[768,128]{1,0:T(8,128)(2,1)S(1)} %get-tuple-element.36), channel_id=1, source_target_pairs={{0,3},{1,4},{2,5},{4,7},{5,0},{7,2},{8,11},{9,12},{10,13},{11,14},... | collective-permute-start | bytes 589832 | tf_op jit(solution)/shard_map/ppermute | solution.py:239
  25.4 26.4 %collective-permute-start.3 = (bf16[768,128]{1,0:T(8,128)(2,1)S(1)}, bf16[768,128]{1,0:T(8,128)(2,1)S(1)}, u32[]{:S(2)}, u32[]{:S(2)}) collective-permute-start(bf16[768,128]{1,0:T(8,128)(2,1)S(1)} %get-tuple-element.38), channel_id=1, source_target_pairs={{0,5},{2,7},{3,0},{5,2},{6,3},{7,4},{8,13},{9,14},{11,8},{12,9},{1... | collective-permute-start | bytes 589832 | tf_op jit(solution)/shard_map/ppermute | solution.py:239
  26.0 32.2 %collective-permute-start.4 = (bf16[768,128]{1,0:T(8,128)(2,1)S(1)}, bf16[768,128]{1,0:T(8,128)(2,1)S(1)}, u32[]{:S(2)}, u32[]{:S(2)}) collective-permute-start(bf16[768,128]{1,0:T(8,128)(2,1)S(1)} %get-tuple-element.39), channel_id=1, source_target_pairs={{0,11},{1,12},{2,13},{3,14},{5,8},{6,9},{7,10},{8,3},{9,4},{10,5},... | collective-permute-start | bytes 589832 | tf_op jit(solution)/shard_map/ppermute | solution.py:239
  35.1 23.8 %collective-permute-start.5 = (bf16[768,128]{1,0:T(8,128)(2,1)S(1)}, bf16[768,128]{1,0:T(8,128)(2,1)S(1)}, u32[]{:S(2)}, u32[]{:S(2)}) collective-permute-start(bf16[768,128]{1,0:T(8,128)(2,1)S(1)} %get-tuple-element.40), channel_id=1, source_target_pairs={{0,13},{1,14},{3,8},{4,9},{5,10},{6,11},{7,12},{8,5},{10,7},{11,0}... | collective-permute-start | bytes 589832 | tf_op jit(solution)/shard_map/ppermute | solution.py:239
  36.4 31.2 %collective-permute-start.6 = (bf16[768,128]{1,0:T(8,128)(2,1)S(1)}, bf16[768,128]{1,0:T(8,128)(2,1)S(1)}, u32[]{:S(2)}, u32[]{:S(2)}) collective-permute-start(bf16[768,128]{1,0:T(8,128)(2,1)S(1)} %get-tuple-element.41), channel_id=1, source_target_pairs={{0,2},{1,3},{2,4},{3,5},{5,7},{6,0},{8,10},{9,11},{10,12},{11,13},... | collective-permute-start | bytes 589832 | tf_op jit(solution)/shard_map/ppermute | solution.py:239
  44.7 24.2 %collective-permute-start.7 = (bf16[768,128]{1,0:T(8,128)(2,1)S(1)}, bf16[768,128]{1,0:T(8,128)(2,1)S(1)}, u32[]{:S(2)}, u32[]{:S(2)}) collective-permute-start(bf16[768,128]{1,0:T(8,128)(2,1)S(1)} %get-tuple-element.43), channel_id=1, source_target_pairs={{1,7},{2,0},{4,2},{5,3},{6,4},{7,5},{8,14},{10,8},{11,9},{12,10},{... | collective-permute-start | bytes 589832 | tf_op jit(solution)/shard_map/ppermute | solution.py:239
  51.8 24.5 %collective-permute-start.8 = (bf16[768,128]{1,0:T(8,128)(2,1)S(1)}, bf16[768,128]{1,0:T(8,128)(2,1)S(1)}, u32[]{:S(2)}, u32[]{:S(2)}) collective-permute-start(bf16[768,128]{1,0:T(8,128)(2,1)S(1)} %get-tuple-element.44), channel_id=1, source_target_pairs={{0,10},{1,11},{2,12},{3,13},{4,14},{6,8},{7,9},{8,2},{9,3},{10,4},... | collective-permute-start | bytes 589832 | tf_op jit(solution)/shard_map/ppermute | solution.py:239
  58.2 19.4 %collective-permute-start.9 = (bf16[768,128]{1,0:T(8,128)(2,1)S(1)}, bf16[768,128]{1,0:T(8,128)(2,1)S(1)}, u32[]{:S(2)}, u32[]{:S(2)}) collective-permute-start(bf16[768,128]{1,0:T(8,128)(2,1)S(1)} %get-tuple-element.45), channel_id=1, source_target_pairs={{0,14},{2,8},{3,9},{4,10},{5,11},{6,12},{7,13},{9,7},{10,0},{12,2}... | collective-permute-start | bytes 589832 | tf_op jit(solution)/shard_map/ppermute | solution.py:239
  58.9 25.2 %collective-permute-start.10 = (bf16[768,128]{1,0:T(8,128)(2,1)}, bf16[768,128]{1,0:T(8,128)(2,1)S(1)}, u32[]{:S(2)}, u32[]{:S(2)}) collective-permute-start(bf16[768,128]{1,0:T(8,128)(2,1)} %get-tuple-element.46), channel_id=1, source_target_pairs={{1,2},{2,3},{3,4},{4,5},{6,7},{7,0},{8,9},{9,10},{10,11},{11,12},{... | collective-permute-start | bytes 589832 | tf_op jit(solution)/shard_map/ppermute | solution.py:239
  67.6 16.6 %collective-permute-start.11 = (bf16[768,128]{1,0:T(8,128)(2,1)}, bf16[768,128]{1,0:T(8,128)(2,1)S(1)}, u32[]{:S(2)}, u32[]{:S(2)}) collective-permute-start(bf16[768,128]{1,0:T(8,128)(2,1)} %get-tuple-element.48), channel_id=1, source_target_pairs={{0,7},{1,0},{3,2},{4,3},{5,4},{6,5},{9,8},{10,9},{11,10},{12,11},{... | collective-permute-start | bytes 589832 | tf_op jit(solution)/shard_map/ppermute | solution.py:239
  68.9 15.3 %collective-permute-start.12 = (bf16[768,128]{1,0:T(8,128)(2,1)}, bf16[768,128]{1,0:T(8,128)(2,1)S(1)}, u32[]{:S(2)}, u32[]{:S(2)}) collective-permute-start(bf16[768,128]{1,0:T(8,128)(2,1)} %get-tuple-element.49), channel_id=1, source_target_pairs={{0,9},{1,10},{2,11},{3,12},{4,13},{5,14},{7,8},{9,2},{10,3},{11,4}... | collective-permute-start | bytes 589832 | tf_op jit(solution)/shard_map/ppermute | solution.py:239
  76.3 8.0 %collective-permute-start.13 = (bf16[768,128]{1,0:T(8,128)(2,1)S(1)}, bf16[768,128]{1,0:T(8,128)(2,1)S(1)}, u32[]{:S(2)}, u32[]{:S(2)}) collective-permute-start(bf16[768,128]{1,0:T(8,128)(2,1)S(1)} %get-tuple-element.50), channel_id=1, source_target_pairs={{1,8},{2,9},{3,10},{4,11},{5,12},{6,13},{7,14},{8,7},{9,0},{11,2},... | collective-permute-start | bytes 589832 | tf_op jit(solution)/shard_map/ppermute | solution.py:239
  77.6 11.9 %collective-permute-start.14 = (bf16[768,128]{1,0:T(8,128)(2,1)S(1)}, bf16[768,128]{1,0:T(8,128)(2,1)S(1)}, u32[]{:S(2)}, u32[]{:S(2)}) collective-permute-start(bf16[768,128]{1,0:T(8,128)(2,1)S(1)} %get-tuple-element.51), channel_id=1, source_target_pairs={{0,8},{1,9},{2,10},{3,11},{4,12},{5,13},{6,14},{8,0},{10,2},{11,3}... | collective-permute-start | bytes 589832 | tf_op jit(solution)/shard_map/ppermute | solution.py:239
  108.0 13.3 %copy-start.3 = (s32[2,16]{1,0:T(2,128)S(1)}, s32[2,16]{1,0:T(2,128)}, u32[]{:S(2)}) copy-start(s32[2,16]{1,0:T(2,128)} %constant.61.clone) | copy-start | bytes 388
  117.2 16.8 %collective-permute-start.15 = (bf16[1024,128]{1,0:T(8,128)(2,1)S(1)}, bf16[1024,128]{1,0:T(8,128)(2,1)S(1)}, u32[]{:S(2)}, u32[]{:S(2)}) collective-permute-start(bf16[1024,128]{1,0:T(8,128)(2,1)S(1)} %attend.4), channel_id=1, source_target_pairs={{0,12},{2,14},{3,15},{4,8},{5,9},{7,11},{8,4},{9,5},{10,6},{11,7},... | collective-permute-start | bytes 786440 | tf_op jit(solution)/shard_map/ppermute | solution.py:248
  118.5 33.0 %collective-permute-start.16 = (bf16[1024,128]{1,0:T(8,128)(2,1)S(1)}, bf16[1024,128]{1,0:T(8,128)(2,1)S(1)}, u32[]{:S(2)}, u32[]{:S(2)}) collective-permute-start(bf16[1024,128]{1,0:T(8,128)(2,1)S(1)} %attend.5), channel_id=1, source_target_pairs={{0,4},{2,6},{3,7},{4,0},{5,1},{7,3},{8,12},{9,13},{10,14},{11,15},... | collective-permute-start | bytes 786440 | tf_op jit(solution)/shard_map/ppermute | solution.py:248
  119.8 31.7 %collective-permute-start.17 = (bf16[1024,128]{1,0:T(8,128)(2,1)S(1)}, bf16[1024,128]{1,0:T(8,128)(2,1)S(1)}, u32[]{:S(2)}, u32[]{:S(2)}) collective-permute-start(bf16[1024,128]{1,0:T(8,128)(2,1)S(1)} %attend.6), channel_id=1, source_target_pairs={{0,8},{2,10},{3,11},{4,12},{5,13},{7,15},{8,0},{9,1},{10,2},{11,3}... | collective-permute-start | bytes 786440 | tf_op jit(solution)/shard_map/ppermute | solution.py:248
  151.6 10.1 %collective-permute-start.18 = (bf16[1024,128]{1,0:T(8,128)(2,1)S(1)}, bf16[1024,128]{1,0:T(8,128)(2,1)S(1)}, u32[]{:S(2)}, u32[]{:S(2)}) collective-permute-start(bf16[1024,128]{1,0:T(8,128)(2,1)S(1)} %select_select_fusion), channel_id=1, source_target_pairs={{0,1},{1,2},{2,3},{4,5},{5,6},{6,7},{8,9},{9,10},{10,11},{12,13},{... | collective-permute-start | bytes 786440 | tf_op jit(solution)/shard_map/ppermute | solution.py:254

commit v2 on v1

--- a/solution.py
+++ b/solution.py
@@ -22,8 +22,8 @@
 IDLE = (((), (0,), (1,), (3,)), ((), (3,), (2,), (0,)))
 CHUNK_HEADS = ((0, 1, 2, 3), (4, 5, 6), (7, 8, 9), (10, 11, 12))
 
-ROTATIONS = ((0, 0), (0, 4), (1, 4), (0, 3), (0, 5), (1, 3), (1, 5), (0, 2), (0, 6), (1, 2), (1, 6), (0, 1), (0, 7),
-             (1, 1), (1, 7), (1, 0))
+ROTATIONS = ((0, 0), (1, 0), (0, 1), (0, 7), (1, 1), (1, 7), (0, 2), (0, 6), (1, 2), (1, 6), (0, 3), (0, 5), (1, 3),
+             (1, 5), (0, 4), (1, 4))
 XORS = (3, 1, 2, 0)
 
 
@@ -146,48 +146,56 @@
 
 
 def attend_kernel(klass_ref, source_ref, *refs):
-    queries, keys, values, out_ref = refs[:4], refs[4:8], refs[8:12], refs[12]
-    half = pl.program_id(0)
-    step = 512
-    q = jnp.concatenate([jnp.where(half == 0, queries[i][0], queries[i + 2][0]) for i in range(2)], axis=0)
-    scaled = q.astype(jnp.float32) * LOG2_SCALE
-    high = scaled.astype(jnp.bfloat16)
-    low = (scaled - high.astype(jnp.float32)).astype(jnp.bfloat16)
-    rhs = jnp.concatenate([high, low], axis=1)
-    top = total = acc = None
-    for g in range(4):
-        for at in range(0, 4 * TOK, step):
-            k = keys[g][at:at + step, :]
-            scores = lax.dot_general(jnp.concatenate([k, k], axis=1), rhs, (((1,), (1,)), ((), ())),
-                                     preferred_element_type=jnp.float32)
-            own = jnp.max(scores, axis=0, keepdims=True)
-            new_top = own if top is None else jnp.maximum(top, own)
-            weights = jnp.exp2(scores - new_top)
-            part = jnp.sum(weights, axis=0, keepdims=True)
-            out = jnp.dot(values[g][:, at:at + step], weights.astype(jnp.bfloat16),
-                          preferred_element_type=jnp.float32)
-            if top is None:
-                total, acc = part, out
-            else:
-                fade = jnp.exp2(top - new_top)
-                total, acc = total * fade + part, acc * fade + out
-            top = new_top
-    done = (acc / total).T.astype(jnp.bfloat16)
-    for i in range(8):
-        row = pl.multiple_of(source_ref[8 * half + i] * LOC, LOC)
-        out_ref[pl.ds(row, LOC), :] = done[i * LOC:(i + 1) * LOC, :]
+    queries, keys, values, out_ref, stores = refs[:4], refs[4:8], refs[8:12], refs[12], refs[13:]
+    width, step = 4 * LOC, 512
+
+    def score(block, g, at, rhs, top):
+        k = keys[g][at:at + step, :]
+        scores = lax.dot_general(jnp.concatenate([k, k], axis=1), rhs, (((1,), (1,)), ((), ())),
+                                 preferred_element_type=jnp.float32)
+        stores[block % 2][g * 4 * TOK + at:g * 4 * TOK + at + step, :] = scores
+        own = jnp.max(scores.reshape(step // 8, 8, width), axis=0)
+        return own if top is None else jnp.maximum(top, own)
+
+    def weigh(block, g, at, top, total, acc):
+        weights = jnp.exp2(stores[block % 2][g * 4 * TOK + at:g * 4 * TOK + at + step, :] - top)
+        part = jnp.sum(weights.reshape(step // 8, 8, width), axis=0)
+        out = jnp.dot(values[g][:, at:at + step], weights.astype(jnp.bfloat16), preferred_element_type=jnp.float32)
+        return (part, out) if total is None else (total + part, acc + out)
+
+    top = None
+    for block in range(5):
+        if block < 4:
+            scaled = queries[block][0].astype(jnp.float32) * LOG2_SCALE
+            high = scaled.astype(jnp.bfloat16)
+            low = (scaled - high.astype(jnp.float32)).astype(jnp.bfloat16)
+            rhs = jnp.concatenate([high, low], axis=1)
+        new_top = total = acc = None
+        for g in range(4):
+            for at in range(0, 4 * TOK, step):
+                if block < 4:
+                    new_top = score(block, g, at, rhs, new_top)
+                if block > 0:
+                    total, acc = weigh(block - 1, g, at, top, total, acc)
+        if block > 0:
+            done = (acc / jnp.sum(total, axis=0, keepdims=True)).T.astype(jnp.bfloat16)
+            for i in range(4):
+                row = pl.multiple_of(source_ref[4 * (block - 1) + i] * LOC, LOC)
+                out_ref[pl.ds(row, LOC), :] = done[i * LOC:(i + 1) * LOC, :]
+        if block < 4:
+            top = jnp.max(new_top, axis=0, keepdims=True)
 
 
 def attend(klass, source, groups):
-    full = pl.BlockSpec(memory_space=pltpu.VMEM)
     rows = SEQ * LOC
     grid_spec = pltpu.PrefetchScalarGridSpec(
         num_scalar_prefetch=2,
-        grid=(2,),
+        grid=(1,),
         in_specs=[pl.BlockSpec((1, 4 * LOC, HEAD_DIM), lambda i, klass, source: (klass[0], 0, 0))] * 4
         + [pl.BlockSpec((4 * TOK, HEAD_DIM), lambda i, klass, source: (0, 0))] * 4
         + [pl.BlockSpec((HEAD_DIM, 4 * TOK), lambda i, klass, source: (0, 0))] * 4,
         out_specs=pl.BlockSpec((rows, HEAD_DIM), lambda i, klass, source: (0, 0)),
+        scratch_shapes=[pltpu.VMEM((SEQ * TOK, 4 * LOC), jnp.float32)] * 2,
     )
     return pl.pallas_call(
         attend_kernel,
@@ -195,7 +203,7 @@
         out_shape=jax.ShapeDtypeStruct((rows, HEAD_DIM), jnp.bfloat16),
         cost_estimate=pl.CostEstimate(flops=4 * rows * SEQ * TOK * HEAD_DIM, transcendentals=rows * SEQ * TOK,
                                       bytes_accessed=2 * 3 * SEQ * TOK * HEAD_DIM),
-        compiler_params=pltpu.CompilerParams(vmem_limit_bytes=32 * 2**20),
+        compiler_params=pltpu.CompilerParams(vmem_limit_bytes=24 * 2**20),
         name="attend",
     )(klass, source, *[g[0] for g in groups], *[g[1] for g in groups], *[g[2] for g in groups])
 
@@ -235,7 +243,8 @@
     messages = pack(send, queries, key_rows, value_rows)
     got = [messages[0]]
     for r in range(1, 16):
-        perm = pairs(lambda s: turn(s, ROTATIONS[r]), lambda core, s, t: HEAD_OF[core, t] >= 0)
+        near = min(ROTATIONS[r][1], 8 - ROTATIONS[r][1]) <= 2
+        perm = pairs(lambda s: turn(s, ROTATIONS[r]), lambda core, s, t: near or HEAD_OF[core, t] >= 0)
         got.append(lax.ppermute(messages[r], axes, perm))
     groups = [gather_group(got[i:i + 4]) for i in range(0, 16, 4)]
 
@@ -244,13 +253,13 @@
         klass = ((seq // 4) ^ flip).reshape(1)
         out = attend(klass, source, groups)
         if flip:
-            perm = pairs(lambda s: ((s // 4) ^ flip) * 4 + s % 4, lambda core, s, t: HEAD_OF[core, s] >= 0)
+            perm = pairs(lambda s: ((s // 4) ^ flip) * 4 + s % 4, lambda core, s, t: True)
             out = lax.ppermute(out, axes, perm)
         blocks.append(out)
     tail = blocks[0]
     for j in range(1, 4):
         tail = jnp.where(last == j, blocks[j], tail)
-    perm = pairs(lambda s: s + 1 if s % 4 < 3 else None, lambda core, s, t: True)
+    perm = pairs(lambda s: turn(s, (0, 1)), lambda core, s, t: True)
     blocks.append(lax.ppermute(tail, axes, perm))
     return merge(shift, blocks)
 

time: 165 us -> 137 us (0.83)
  the two profiles are of different devices: /device:TPU:50 before, /device:TPU:200 now
where the time goes in v2:
time: 137 us; the launch traced here: 136 us
  starting transfers between devices  77.5 us (57%)
  Pallas kernels  28 us (20%)
  waiting for transfers between devices  21.2 us (15%)
  local copies, waits for them, and re-layouts  7.39 us (5%)
  between operations  2.15 us (2%)
    ppermute x15, starting transfers between devices, exchange_and_attend(): got.append(lax.ppermute(messages[r], axes, perm))  53 us
    ppermute x3, starting transfers between devices, exchange_and_attend(): out = lax.ppermute(out, axes, perm)  24.5 us
    pallas_call x4, Pallas kernels, attend(): pl.pallas_call(attend_kernel, grid_spec=grid_spec, out_shape=jax.ShapeDty...  23.9 us
    ppermute x15, waiting for transfers between devices, exchange_and_attend(): got.append(lax.ppermute(messages[r], axes, perm))  10.4 us
    ppermute x1, waiting for transfers between devices, exchange_and_attend(): blocks.append(lax.ppermute(tail, axes, perm))  5.66 us
    ppermute x3, waiting for transfers between devices, exchange_and_attend(): out = lax.ppermute(out, axes, perm)  5.18 us
    unnamed x8, local copies, waits for them, and re-layouts  3.47 us
  transfers between devices with their start and end apart: 19, of which 6 were waited for; matrix products, arithmetic and copies ran while one was open for 1% of the time, Pallas kernels for 5%

profile of v2, /device:TPU:200, one launch (start us, length us, event | category | flops | bytes accessed | tf_op | source)
XLA Modules:
  0.0 136.3 jit_solution(2793277312374490214)
XLA Ops:
  0.7 1.2 copy-done
  1.9 1.2 copy-done.1
  3.0 1.2 copy-done.2
  4.2 2.1 %pack.1 = (bf16[768,128]{1,0:T(8,128)(2,1)S(1)}, bf16[768,128]{1,0:T(8,128)(2,1)S(1)}, bf16[768,128]{1,0:T(8,128)(2,1)S(1)}, bf16[768,128]{1,0:T(8,128)(2,1)S(1)...) custom-call(s32[16]{0:T(128)S(1)} %fusion.2.send_ref, ...), custom_call_target="tpu_custom_call" | custom-call | tf_op jit(solution)/shard_map/pack/pallas_call | solution.py:112
  6.3 3.0 %collective-permute-start = (bf16[768,128]{1,0:T(8,128)(2,1)S(1)}, bf16[768,128]{1,0:T(8,128)(2,1)S(1)}, u32[]{:S(2)}, u32[]{:S(2)}) collective-permute-start(bf16[768,128]{1,0:T(8,128)(2,1)S(1)} %get-tuple-element.34), channel_id=1, source_target_pairs={{0,8},{1,9},{2,10},{3,11},{4,12},{5,13},{6,14},{7,15},{8,0},{9,1},... | collective-permute-start | bytes 589832 | tf_op jit(solution)/shard_map/ppermute | solution.py:248
  9.3 1.0 collective-permute-start.1
  10.3 1.0 collective-permute-start.2
  11.3 1.0 collective-permute-start.3
  12.3 3.5 %collective-permute-start.4 = (bf16[768,128]{1,0:T(8,128)(2,1)S(1)}, bf16[768,128]{1,0:T(8,128)(2,1)S(1)}, u32[]{:S(2)}, u32[]{:S(2)}) collective-permute-start(bf16[768,128]{1,0:T(8,128)(2,1)S(1)} %get-tuple-element.39), channel_id=1, source_target_pairs={{0,15},{1,8},{2,9},{3,10},{4,11},{5,12},{6,13},{7,14},{8,7},{9,0},... | collective-permute-start | bytes 589832 | tf_op jit(solution)/shard_map/ppermute | solution.py:248
  15.8 2.9 %collective-permute-start.5 = (bf16[768,128]{1,0:T(8,128)(2,1)S(1)}, bf16[768,128]{1,0:T(8,128)(2,1)S(1)}, u32[]{:S(2)}, u32[]{:S(2)}) collective-permute-start(bf16[768,128]{1,0:T(8,128)(2,1)S(1)} %get-tuple-element.40), channel_id=1, source_target_pairs={{0,2},{1,3},{2,4},{3,5},{4,6},{5,7},{6,0},{7,1},{8,10},{9,11},{10,... | collective-permute-start | bytes 589832 | tf_op jit(solution)/shard_map/ppermute | solution.py:248
  18.6 1.1 collective-permute-start.6
  19.7 3.0 %collective-permute-start.7 = (bf16[768,128]{1,0:T(8,128)(2,1)S(1)}, bf16[768,128]{1,0:T(8,128)(2,1)S(1)}, u32[]{:S(2)}, u32[]{:S(2)}) collective-permute-start(bf16[768,128]{1,0:T(8,128)(2,1)S(1)} %get-tuple-element.43), channel_id=1, source_target_pairs={{0,10},{1,11},{2,12},{3,13},{4,14},{5,15},{6,8},{7,9},{8,2},{9,3},... | collective-permute-start | bytes 589832 | tf_op jit(solution)/shard_map/ppermute | solution.py:248
  22.7 2.8 %collective-permute-done.3.refs_0_ = bf16[768,128]{1,0:T(8,128)(2,1)S(1)} collective-permute-done((bf16[768,128]{1,0:T(8,128)(2,1)S(1)}, bf16[768,128]{1,0:T(8,128)(2,1)S(1)}, u32[]{:S(2)}, u32[]{:S(2)}) %collective-permute-start.3) | collective-permute-done | bytes 196640 | tf_op jit(solution)/shard_map/ppermute | solution.py:248
  25.6 3.1 %collective-permute-start.8 = (bf16[768,128]{1,0:T(8,128)(2,1)S(1)}, bf16[768,128]{1,0:T(8,128)(2,1)S(1)}, u32[]{:S(2)}, u32[]{:S(2)}) collective-permute-start(bf16[768,128]{1,0:T(8,128)(2,1)S(1)} %get-tuple-element.44), channel_id=1, source_target_pairs={{0,14},{1,15},{2,8},{3,9},{4,10},{5,11},{6,12},{7,13},{8,6},{9,7},... | collective-permute-start | bytes 589832 | tf_op jit(solution)/shard_map/ppermute | solution.py:248
  29.3 6.4 %collective-permute-start.10 = (bf16[768,128]{1,0:T(8,128)(2,1)}, bf16[768,128]{1,0:T(8,128)(2,1)S(1)}, u32[]{:S(2)}, u32[]{:S(2)}) collective-permute-start(bf16[768,128]{1,0:T(8,128)(2,1)} %get-tuple-element.46), channel_id=1, source_target_pairs={{0,5},{2,7},{3,0},{5,2},{6,3},{7,4},{8,13},{9,14},{11,8},{12,9},{1... | collective-permute-start | bytes 589832 | tf_op jit(solution)/shard_map/ppermute | solution.py:248
  35.7 1.1 collective-permute-done.6.refs_3_
  36.8 5.7 %collective-permute-start.11 = (bf16[768,128]{1,0:T(8,128)(2,1)}, bf16[768,128]{1,0:T(8,128)(2,1)S(1)}, u32[]{:S(2)}, u32[]{:S(2)}) collective-permute-start(bf16[768,128]{1,0:T(8,128)(2,1)} %get-tuple-element.48), channel_id=1, source_target_pairs={{0,11},{1,12},{2,13},{3,14},{5,8},{6,9},{7,10},{8,3},{9,4},{10,5},... | collective-permute-start | bytes 589832 | tf_op jit(solution)/shard_map/ppermute | solution.py:248
  42.5 6.5 %collective-permute-start.12 = (bf16[768,128]{1,0:T(8,128)(2,1)}, bf16[768,128]{1,0:T(8,128)(2,1)S(1)}, u32[]{:S(2)}, u32[]{:S(2)}) collective-permute-start(bf16[768,128]{1,0:T(8,128)(2,1)} %get-tuple-element.49), channel_id=1, source_target_pairs={{0,13},{1,14},{3,8},{4,9},{5,10},{6,11},{7,12},{8,5},{10,7},{11,0}... | collective-permute-start | bytes 589832 | tf_op jit(solution)/shard_map/ppermute | solution.py:248
  49.1 2.5 %collective-permute-start.13 = (bf16[768,128]{1,0:T(8,128)(2,1)S(1)}, bf16[768,128]{1,0:T(8,128)(2,1)S(1)}, u32[]{:S(2)}, u32[]{:S(2)}) collective-permute-start(bf16[768,128]{1,0:T(8,128)(2,1)S(1)} %get-tuple-element.50), channel_id=1, source_target_pairs={{0,4},{1,5},{3,7},{4,0},{6,2},{7,3},{8,12},{9,13},{10,14},{12,8},{... | collective-permute-start | bytes 589832 | tf_op jit(solution)/shard_map/ppermute | solution.py:248
  51.6 11.7 %collective-permute-start.14 = (bf16[768,128]{1,0:T(8,128)(2,1)S(1)}, bf16[768,128]{1,0:T(8,128)(2,1)S(1)}, u32[]{:S(2)}, u32[]{:S(2)}) collective-permute-start(bf16[768,128]{1,0:T(8,128)(2,1)S(1)} %get-tuple-element.51), channel_id=1, source_target_pairs={{0,12},{1,13},{2,14},{4,8},{5,9},{6,10},{7,11},{8,4},{9,5},{11,7},... | collective-permute-start | bytes 589832 | tf_op jit(solution)/shard_map/ppermute | solution.py:248
  64.4 3.0 %collective-permute-done.13.refs_2_ = bf16[768,128]{1,0:T(8,128)(2,1)S(1)} collective-permute-done((bf16[768,128]{1,0:T(8,128)(2,1)S(1)}, bf16[768,128]{1,0:T(8,128)(2,1)S(1)}, u32[]{:S(2)}, u32[]{:S(2)}) %collective-permute-start.13) | collective-permute-done | bytes 196640 | tf_op jit(solution)/shard_map/ppermute | solution.py:248
  67.4 3.5 %collective-permute-done.14.refs_3_ = bf16[768,128]{1,0:T(8,128)(2,1)S(1)} collective-permute-done((bf16[768,128]{1,0:T(8,128)(2,1)S(1)}, bf16[768,128]{1,0:T(8,128)(2,1)S(1)}, u32[]{:S(2)}, u32[]{:S(2)}) %collective-permute-start.14) | collective-permute-done | bytes 196640 | tf_op jit(solution)/shard_map/ppermute | solution.py:248
  70.9 5.9 %attend.6 = bf16[1024,128]{1,0:T(8,128)(2,1)S(1)} custom-call(s32[1]{0:T(128)} %bitcast.5.klass_ref, s32[16]{0:T(128)S(1)} %fusion.1.source_ref, bf16[4,256,128]{2,1,0:T(8,128)(2,1)S(1)} %get-tuple-element.37.refs_0_, bf16[4,256,128]{2,1,0:T(8,128)(2,1)S(1)} %get-tuple-element.42.refs_1_, bf16[4,256,128]{2,1,0:T(8,128)(2,1)S(1)} %get-tuple-element.47.refs_2_, ...), custom_call_target="tpu_custom_call" | custom-call | flops 2147483648 | bytes 3145728 | tf_op jit(solution)/shard_map/attend/pallas_call | solution.py:200
  76.9 5.9 %attend.5 = bf16[1024,128]{1,0:T(8,128)(2,1)S(1)} custom-call(s32[1]{0:T(128)} %bitcast.4.klass_ref, s32[16]{0:T(128)S(1)} %fusion.1.source_ref, bf16[4,256,128]{2,1,0:T(8,128)(2,1)S(1)} %get-tuple-element.37.refs_0_, bf16[4,256,128]{2,1,0:T(8,128)(2,1)S(1)} %get-tuple-element.42.refs_1_, bf16[4,256,128]{2,1,0:T(8,128)(2,1)S(1)} %get-tuple-element.47.refs_2_, ...), custom_call_target="tpu_custom_call" | custom-call | flops 2147483648 | bytes 3145728 | tf_op jit(solution)/shard_map/attend/pallas_call | solution.py:200
  82.8 6.1 %attend.4 = bf16[1024,128]{1,0:T(8,128)(2,1)S(1)} custom-call(s32[1]{0:T(128)} %bitcast.1.klass_ref, s32[16]{0:T(128)S(1)} %fusion.1.source_ref, bf16[4,256,128]{2,1,0:T(8,128)(2,1)S(1)} %get-tuple-element.37.refs_0_, bf16[4,256,128]{2,1,0:T(8,128)(2,1)S(1)} %get-tuple-element.42.refs_1_, bf16[4,256,128]{2,1,0:T(8,128)(2,1)S(1)} %get-tuple-element.47.refs_2_, ...), custom_call_target="tpu_custom_call" | custom-call | flops 2147483648 | bytes 3145728 | tf_op jit(solution)/shard_map/attend/pallas_call | solution.py:200
  88.9 8.9 %collective-permute-start.15 = (bf16[1024,128]{1,0:T(8,128)(2,1)S(1)}, bf16[1024,128]{1,0:T(8,128)(2,1)S(1)}, u32[]{:S(2)}, u32[]{:S(2)}) collective-permute-start(bf16[1024,128]{1,0:T(8,128)(2,1)S(1)} %attend.4), channel_id=1, source_target_pairs={{0,12},{1,13},{2,14},{3,15},{4,8},{5,9},{6,10},{7,11},{8,4},{9,5},... | collective-permute-start | bytes 786440 | tf_op jit(solution)/shard_map/ppermute | solution.py:257
  97.8 15.6 %collective-permute-start.16 = (bf16[1024,128]{1,0:T(8,128)(2,1)S(1)}, bf16[1024,128]{1,0:T(8,128)(2,1)S(1)}, u32[]{:S(2)}, u32[]{:S(2)}) collective-permute-start(bf16[1024,128]{1,0:T(8,128)(2,1)S(1)} %attend.5), channel_id=1, source_target_pairs={{0,4},{1,5},{2,6},{3,7},{4,0},{5,1},{6,2},{7,3},{8,12},{9,13},{10,... | collective-permute-start | bytes 786440 | tf_op jit(solution)/shard_map/ppermute | solution.py:257
  115.9 5.9 %attend.7.refs_3_ = bf16[1024,128]{1,0:T(8,128)(2,1)S(1)} custom-call(s32[1]{0:T(128)} %bitcast.6.klass_ref, s32[16]{0:T(128)S(1)} %fusion.1.source_ref, bf16[4,256,128]{2,1,0:T(8,128)(2,1)S(1)} %get-tuple-element.37.refs_0_, bf16[4,256,128]{2,1,0:T(8,128)(2,1)S(1)} %get-tuple-element.42.refs_1_, bf16[4,256,128]{2,1,0:T(8,128)(2,1)S(1)} %get-tuple-element.47.refs_2_, ...), custom_call_target="tpu_custom_call" | custom-call | flops 2147483648 | bytes 3145728 | tf_op jit(solution)/shard_map/attend/pallas_call | solution.py:200
  121.8 5.2 %collective-permute-done.16.refs_1_ = bf16[1024,128]{1,0:T(8,128)(2,1)S(1)} collective-permute-done((bf16[1024,128]{1,0:T(8,128)(2,1)S(1)}, bf16[1024,128]{1,0:T(8,128)(2,1)S(1)}, u32[]{:S(2)}, u32[]{:S(2)}) %collective-permute-start.16) | collective-permute-done | bytes 262176 | tf_op jit(solution)/shard_map/ppermute | solution.py:257
  127.8 5.7 %collective-permute-done.18.refs_4_ = bf16[1024,128]{1,0:T(8,128)(2,1)S(1)} collective-permute-done((bf16[1024,128]{1,0:T(8,128)(2,1)S(1)}, bf16[1024,128]{1,0:T(8,128)(2,1)S(1)}, u32[]{:S(2)}, u32[]{:S(2)}) %collective-permute-start.18) | collective-permute-done | bytes 262176 | tf_op jit(solution)/shard_map/ppermute | solution.py:263
  133.5 1.5 %merge.1 = bf16[1024,416]{1,0:T(8,128)(2,1)S(1)} custom-call(s32[5]{0:T(128)S(1)} %fusion.shift_ref, bf16[1024,128]{1,0:T(8,128)(2,1)S(1)} %collective-permute-done.15.refs_0_, bf16[1024,128]{1,0:T(8,128)(2,1)S(1)} %collective-permute-done.16.refs_1_, bf16[1024,128]{1,0:T(8,128)(2,1)S(1)} %collective-permute-done.17.refs_2_, ...), custom_call_target="tpu_custom_call" | custom-call | tf_op jit(solution)/shard_map/merge/pallas_call | solution.py:224
  135.0 1.2 copy.8
  (30 shorter events, 4.0 us)
Async XLA Ops:
  0.7 1.2 copy-start
  1.8 1.2 copy-start.1
  3.0 1.2 copy-start.2
  6.3 9.5 %collective-permute-start = (bf16[768,128]{1,0:T(8,128)(2,1)S(1)}, bf16[768,128]{1,0:T(8,128)(2,1)S(1)}, u32[]{:S(2)}, u32[]{:S(2)}) collective-permute-start(bf16[768,128]{1,0:T(8,128)(2,1)S(1)} %get-tuple-element.34), channel_id=1, source_target_pairs={{0,8},{1,9},{2,10},{3,11},{4,12},{5,13},{6,14},{7,15},{8,0},{9,1},... | collective-permute-start | bytes 589832 | tf_op jit(solution)/shard_map/ppermute | solution.py:248
  9.3 9.3 %collective-permute-start.1 = (bf16[768,128]{1,0:T(8,128)(2,1)S(1)}, bf16[768,128]{1,0:T(8,128)(2,1)S(1)}, u32[]{:S(2)}, u32[]{:S(2)}) collective-permute-start(bf16[768,128]{1,0:T(8,128)(2,1)S(1)} %get-tuple-element.35), channel_id=1, source_target_pairs={{0,1},{1,2},{2,3},{3,4},{4,5},{5,6},{6,7},{7,0},{8,9},{9,10},{10,1... | collective-permute-start | bytes 589832 | tf_op jit(solution)/shard_map/ppermute | solution.py:248
  10.3 9.4 %collective-permute-start.2 = (bf16[768,128]{1,0:T(8,128)(2,1)S(1)}, bf16[768,128]{1,0:T(8,128)(2,1)S(1)}, u32[]{:S(2)}, u32[]{:S(2)}) collective-permute-start(bf16[768,128]{1,0:T(8,128)(2,1)S(1)} %get-tuple-element.36), channel_id=1, source_target_pairs={{0,7},{1,0},{2,1},{3,2},{4,3},{5,4},{6,5},{7,6},{8,15},{9,8},{10,9... | collective-permute-start | bytes 589832 | tf_op jit(solution)/shard_map/ppermute | solution.py:248
  11.3 14.2 %collective-permute-start.3 = (bf16[768,128]{1,0:T(8,128)(2,1)S(1)}, bf16[768,128]{1,0:T(8,128)(2,1)S(1)}, u32[]{:S(2)}, u32[]{:S(2)}) collective-permute-start(bf16[768,128]{1,0:T(8,128)(2,1)S(1)} %get-tuple-element.38), channel_id=1, source_target_pairs={{0,9},{1,10},{2,11},{3,12},{4,13},{5,14},{6,15},{7,8},{8,1},{9,2},... | collective-permute-start | bytes 589832 | tf_op jit(solution)/shard_map/ppermute | solution.py:248
  12.3 16.4 %collective-permute-start.4 = (bf16[768,128]{1,0:T(8,128)(2,1)S(1)}, bf16[768,128]{1,0:T(8,128)(2,1)S(1)}, u32[]{:S(2)}, u32[]{:S(2)}) collective-permute-start(bf16[768,128]{1,0:T(8,128)(2,1)S(1)} %get-tuple-element.39), channel_id=1, source_target_pairs={{0,15},{1,8},{2,9},{3,10},{4,11},{5,12},{6,13},{7,14},{8,7},{9,0},... | collective-permute-start | bytes 589832 | tf_op jit(solution)/shard_map/ppermute | solution.py:248
  15.8 13.6 %collective-permute-start.5 = (bf16[768,128]{1,0:T(8,128)(2,1)S(1)}, bf16[768,128]{1,0:T(8,128)(2,1)S(1)}, u32[]{:S(2)}, u32[]{:S(2)}) collective-permute-start(bf16[768,128]{1,0:T(8,128)(2,1)S(1)} %get-tuple-element.40), channel_id=1, source_target_pairs={{0,2},{1,3},{2,4},{3,5},{4,6},{5,7},{6,0},{7,1},{8,10},{9,11},{10,... | collective-permute-start | bytes 589832 | tf_op jit(solution)/shard_map/ppermute | solution.py:248
  18.6 18.2 %collective-permute-start.6 = (bf16[768,128]{1,0:T(8,128)(2,1)S(1)}, bf16[768,128]{1,0:T(8,128)(2,1)S(1)}, u32[]{:S(2)}, u32[]{:S(2)}) collective-permute-start(bf16[768,128]{1,0:T(8,128)(2,1)S(1)} %get-tuple-element.41), channel_id=1, source_target_pairs={{0,6},{1,7},{2,0},{3,1},{4,2},{5,3},{6,4},{7,5},{8,14},{9,15},{10,... | collective-permute-start | bytes 589832 | tf_op jit(solution)/shard_map/ppermute | solution.py:248
  19.7 22.8 %collective-permute-start.7 = (bf16[768,128]{1,0:T(8,128)(2,1)S(1)}, bf16[768,128]{1,0:T(8,128)(2,1)S(1)}, u32[]{:S(2)}, u32[]{:S(2)}) collective-permute-start(bf16[768,128]{1,0:T(8,128)(2,1)S(1)} %get-tuple-element.43), channel_id=1, source_target_pairs={{0,10},{1,11},{2,12},{3,13},{4,14},{5,15},{6,8},{7,9},{8,2},{9,3},... | collective-permute-start | bytes 589832 | tf_op jit(solution)/shard_map/ppermute | solution.py:248
  25.6 23.5 %collective-permute-start.8 = (bf16[768,128]{1,0:T(8,128)(2,1)S(1)}, bf16[768,128]{1,0:T(8,128)(2,1)S(1)}, u32[]{:S(2)}, u32[]{:S(2)}) collective-permute-start(bf16[768,128]{1,0:T(8,128)(2,1)S(1)} %get-tuple-element.44), channel_id=1, source_target_pairs={{0,14},{1,15},{2,8},{3,9},{4,10},{5,11},{6,12},{7,13},{8,6},{9,7},... | collective-permute-start | bytes 589832 | tf_op jit(solution)/shard_map/ppermute | solution.py:248
  28.6 22.9 %collective-permute-start.9 = (bf16[768,128]{1,0:T(8,128)(2,1)S(1)}, bf16[768,128]{1,0:T(8,128)(2,1)S(1)}, u32[]{:S(2)}, u32[]{:S(2)}) collective-permute-start(bf16[768,128]{1,0:T(8,128)(2,1)S(1)} %get-tuple-element.45), channel_id=1, source_target_pairs={{0,3},{1,4},{2,5},{4,7},{5,0},{7,2},{8,11},{9,12},{10,13},{11,14},... | collective-permute-start | bytes 589832 | tf_op jit(solution)/shard_map/ppermute | solution.py:248
  29.3 34.9 %collective-permute-start.10 = (bf16[768,128]{1,0:T(8,128)(2,1)}, bf16[768,128]{1,0:T(8,128)(2,1)S(1)}, u32[]{:S(2)}, u32[]{:S(2)}) collective-permute-start(bf16[768,128]{1,0:T(8,128)(2,1)} %get-tuple-element.46), channel_id=1, source_target_pairs={{0,5},{2,7},{3,0},{5,2},{6,3},{7,4},{8,13},{9,14},{11,8},{12,9},{1... | collective-permute-start | bytes 589832 | tf_op jit(solution)/shard_map/ppermute | solution.py:248
  36.8 27.6 %collective-permute-start.11 = (bf16[768,128]{1,0:T(8,128)(2,1)}, bf16[768,128]{1,0:T(8,128)(2,1)S(1)}, u32[]{:S(2)}, u32[]{:S(2)}) collective-permute-start(bf16[768,128]{1,0:T(8,128)(2,1)} %get-tuple-element.48), channel_id=1, source_target_pairs={{0,11},{1,12},{2,13},{3,14},{5,8},{6,9},{7,10},{8,3},{9,4},{10,5},... | collective-permute-start | bytes 589832 | tf_op jit(solution)/shard_map/ppermute | solution.py:248
  42.5 21.9 %collective-permute-start.12 = (bf16[768,128]{1,0:T(8,128)(2,1)}, bf16[768,128]{1,0:T(8,128)(2,1)S(1)}, u32[]{:S(2)}, u32[]{:S(2)}) collective-permute-start(bf16[768,128]{1,0:T(8,128)(2,1)} %get-tuple-element.49), channel_id=1, source_target_pairs={{0,13},{1,14},{3,8},{4,9},{5,10},{6,11},{7,12},{8,5},{10,7},{11,0}... | collective-permute-start | bytes 589832 | tf_op jit(solution)/shard_map/ppermute | solution.py:248
  49.1 18.3 %collective-permute-start.13 = (bf16[768,128]{1,0:T(8,128)(2,1)S(1)}, bf16[768,128]{1,0:T(8,128)(2,1)S(1)}, u32[]{:S(2)}, u32[]{:S(2)}) collective-permute-start(bf16[768,128]{1,0:T(8,128)(2,1)S(1)} %get-tuple-element.50), channel_id=1, source_target_pairs={{0,4},{1,5},{3,7},{4,0},{6,2},{7,3},{8,12},{9,13},{10,14},{12,8},{... | collective-permute-start | bytes 589832 | tf_op jit(solution)/shard_map/ppermute | solution.py:248
  51.6 19.2 %collective-permute-start.14 = (bf16[768,128]{1,0:T(8,128)(2,1)S(1)}, bf16[768,128]{1,0:T(8,128)(2,1)S(1)}, u32[]{:S(2)}, u32[]{:S(2)}) collective-permute-start(bf16[768,128]{1,0:T(8,128)(2,1)S(1)} %get-tuple-element.51), channel_id=1, source_target_pairs={{0,12},{1,13},{2,14},{4,8},{5,9},{6,10},{7,11},{8,4},{9,5},{11,7},... | collective-permute-start | bytes 589832 | tf_op jit(solution)/shard_map/ppermute | solution.py:248
  82.8 30.6 %copy-start.3 = (s32[2,16]{1,0:T(2,128)S(1)}, s32[2,16]{1,0:T(2,128)}, u32[]{:S(2)}) copy-start(s32[2,16]{1,0:T(2,128)} %constant.61.clone) | copy-start | bytes 388
  88.9 32.9 %collective-permute-start.15 = (bf16[1024,128]{1,0:T(8,128)(2,1)S(1)}, bf16[1024,128]{1,0:T(8,128)(2,1)S(1)}, u32[]{:S(2)}, u32[]{:S(2)}) collective-permute-start(bf16[1024,128]{1,0:T(8,128)(2,1)S(1)} %attend.4), channel_id=1, source_target_pairs={{0,12},{1,13},{2,14},{3,15},{4,8},{5,9},{6,10},{7,11},{8,4},{9,5},... | collective-permute-start | bytes 786440 | tf_op jit(solution)/shard_map/ppermute | solution.py:257
  97.8 29.2 %collective-permute-start.16 = (bf16[1024,128]{1,0:T(8,128)(2,1)S(1)}, bf16[1024,128]{1,0:T(8,128)(2,1)S(1)}, u32[]{:S(2)}, u32[]{:S(2)}) collective-permute-start(bf16[1024,128]{1,0:T(8,128)(2,1)S(1)} %attend.5), channel_id=1, source_target_pairs={{0,4},{1,5},{2,6},{3,7},{4,0},{5,1},{6,2},{7,3},{8,12},{9,13},{10,... | collective-permute-start | bytes 786440 | tf_op jit(solution)/shard_map/ppermute | solution.py:257
  113.4 13.6 %collective-permute-start.17 = (bf16[1024,128]{1,0:T(8,128)(2,1)S(1)}, bf16[1024,128]{1,0:T(8,128)(2,1)S(1)}, u32[]{:S(2)}, u32[]{:S(2)}) collective-permute-start(bf16[1024,128]{1,0:T(8,128)(2,1)S(1)} %attend.6), channel_id=1, source_target_pairs={{0,8},{1,9},{2,10},{3,11},{4,12},{5,13},{6,14},{7,15},{8,0},{9,1},... | collective-permute-start | bytes 786440 | tf_op jit(solution)/shard_map/ppermute | solution.py:257
  127.1 6.4 %collective-permute-start.18 = (bf16[1024,128]{1,0:T(8,128)(2,1)S(1)}, bf16[1024,128]{1,0:T(8,128)(2,1)S(1)}, u32[]{:S(2)}, u32[]{:S(2)}) collective-permute-start(bf16[1024,128]{1,0:T(8,128)(2,1)S(1)} %select_select_fusion), channel_id=1, source_target_pairs={{0,1},{1,2},{2,3},{3,4},{4,5},{5,6},{6,7},{7,0},{8,9},{9,10},{10,1... | collective-permute-start | bytes 786440 | tf_op jit(solution)/shard_map/ppermute | solution.py:263

commit v3 on v0

v3 whole, which is shorter than its diff:
```python
import math

import jax
import jax.numpy as jnp
from jax import lax
from jax.experimental import pallas as pl
from jax.experimental.pallas import tpu as pltpu
from jax.sharding import PartitionSpec as P


HEAD_DIM = 128
HEADS = 13
SEQ = 16
TOK = 256
LOC = 64
GROUP = 4
WIDE = GROUP * LOC
DEEP = GROUP * TOK
STEP = 512
OUT_COLS = 416
FAR = 1 << 20
LOG2_SCALE = math.log2(math.e) / math.sqrt(HEAD_DIM)


IDLE = ((9, 0, 1, 3), (9, 3, 2, 0))

ROTATIONS = ((0, 0), (1, 0), (0, 1), (0, 7), (1, 1), (1, 7), (0, 2), (0, 6), (1, 2), (1, 6), (0, 3), (0, 5), (1, 3),
             (1, 5), (0, 4), (1, 4))
XORS = (3, 1, 2, 0)


def idle(core, seq):
    place, chunk = seq // 4, seq % 4
    return chunk > 0 and place == IDLE[core][chunk]


def turn(seq, rotation):
    dx, dz = rotation
    return ((seq // 8) ^ dx) * 8 + (seq % 8 + dz) % 8


def pairs(step, active):
    out = []
    for dp in range(16):
        for seq in range(SEQ):
            if active(dp % 2, step(seq)):
                out.append((dp * SEQ + seq, dp * SEQ + step(seq)))
    return out


def pick(index, values):
    out = jnp.int32(values[-1])
    for at in range(len(values) - 1):
        out = jnp.where(index == at, jnp.int32(values[at]), out)
    return out


def idle_place(core, chunk):
    return jnp.where(core == 0, pick(chunk, IDLE[0]), pick(chunk, IDLE[1]))


def head_at(core, seq):
    place, chunk = seq // 4, seq % 4
    late = jnp.where(place > idle_place(core, chunk), 1, 0)
    return jnp.minimum(jnp.where(chunk == 0, place, 1 + 3 * chunk + place - late), HEADS - 1)


def vmem():
    return pl.BlockSpec(memory_space=pltpu.VMEM)


def pack_kernel(q_ref, k_ref, v_ref, *refs):
    outs, queries, sems = refs[:16], refs[16], refs[17]
    core, seq = lax.axis_index("dp") % 2, lax.axis_index("seq")
    first = pltpu.make_async_copy(q_ref, queries, sems.at[32])
    first.start()
    copies, columns = [], []
    for r, (dx, dz) in enumerate(ROTATIONS):
        target = ((seq // 8) ^ dx) * 8 + (seq % 8 + dz) % 8
        at = pl.ds(pl.multiple_of(head_at(core, target) * HEAD_DIM, HEAD_DIM), HEAD_DIM)
        columns.append(at)
        for i, ref in enumerate((k_ref, v_ref)):
            copy = pltpu.make_async_copy(ref.at[:, at], outs[r].at[(i + 1) * TOK:(i + 2) * TOK, :], sems.at[2 * r + i])
            copy.start()
            copies.append(copy)
    row = lax.broadcasted_iota(jnp.int32, (TOK, TOK), 0)
    col = lax.broadcasted_iota(jnp.int32, (TOK, TOK), 1)
    grid_row, grid_col = col // 64, col % 64
    wanted = ((grid_row % 2) * 2 + grid_col % 2) * LOC + (grid_row // 2) * 32 + grid_col // 2
    order = jnp.where(row == wanted, 1.0, 0.0).astype(jnp.bfloat16)
    first.wait()
    for r in range(16):
        outs[r][0:TOK, :] = jnp.dot(order, queries[:, columns[r]],
                                    preferred_element_type=jnp.float32).astype(jnp.bfloat16)
    for copy in copies:
        copy.wait()


def pack(queries, key_rows, value_rows):
    shape = jax.ShapeDtypeStruct((3 * TOK, HEAD_DIM), jnp.bfloat16)
    return pl.pallas_call(
        pack_kernel,
        in_specs=[pl.BlockSpec(memory_space=pl.ANY)] * 3,
        out_specs=[vmem()] * 16,
        out_shape=[shape] * 16,
        scratch_shapes=[pltpu.VMEM((TOK, HEADS * HEAD_DIM), jnp.bfloat16), pltpu.SemaphoreType.DMA((33,))],
        compiler_params=pltpu.CompilerParams(vmem_limit_bytes=16 * 2**20),
        name="pack",
    )(queries, key_rows, value_rows)


def gather_kernel(*refs):
    got, (q_out, k_out, v_out) = refs[:GROUP], refs[GROUP:]
    for i in range(GROUP):
        for klass in range(4):
            q_out[klass, i * LOC:(i + 1) * LOC, :] = got[i][klass * LOC:(klass + 1) * LOC, :]
        k_out[i * TOK:(i + 1) * TOK, :] = got[i][TOK:2 * TOK, :]
        v_out[:, i * TOK:(i + 1) * TOK] = got[i][2 * TOK:, :].T


def gather_group(messages):
    return pl.pallas_call(
        gather_kernel,
        in_specs=[vmem()] * GROUP,
        out_specs=[vmem()] * 3,
        out_shape=[
            jax.ShapeDtypeStruct((4, WIDE, HEAD_DIM), jnp.bfloat16),
            jax.ShapeDtypeStruct((DEEP, HEAD_DIM), jnp.bfloat16),
            jax.ShapeDtypeStruct((HEAD_DIM, DEEP), jnp.bfloat16),
        ],
        compiler_params=pltpu.CompilerParams(vmem_limit_bytes=16 * 2**20),
        name="gather_group",
    )(*messages)


def attend_kernel(stages, groups, known, flip, *refs):
    queries, keys, values, refs = refs[:groups], refs[groups:2 * groups], refs[2 * groups:3 * groups], refs[3 * groups:]
    state = ()
    if known:
        state, refs = refs[:3], refs[3:]
    outs, stores = refs[:-2], refs[-2:]
    seq = lax.axis_index("seq")
    klass = pl.program_id(0) if flip is None else (seq // 4) ^ flip

    units = [[(g, keys_of, at) for g, key_groups in stage for keys_of in key_groups for at in range(0, DEEP, STEP)]
             for stage in stages]
    ready = {}
    tops = {}
    sums = {}

    def score(slot, index, unit):
        g, keys_of, at = unit
        if g not in ready:
            scaled = queries[g][klass].astype(jnp.float32) * LOG2_SCALE
            high = scaled.astype(jnp.bfloat16)
            low = (scaled - high.astype(jnp.float32)).astype(jnp.bfloat16)
            ready[g] = jnp.concatenate([high, low], axis=1)
        k = keys[keys_of][at:at + STEP, :]
        scores = lax.dot_general(jnp.concatenate([k, k], axis=1), ready[g], (((1,), (1,)), ((), ())),
                                 preferred_element_type=jnp.float32)
        stores[slot][index * STEP:(index + 1) * STEP, :] = scores
        own = jnp.max(scores.reshape(STEP // 8, 8, WIDE), axis=0)
        tops[g] = jnp.maximum(tops[g], own) if g in tops else own

    def weigh(slot, index, unit):
        g, keys_of, at = unit
        weights = jnp.exp2(stores[slot][index * STEP:(index + 1) * STEP, :] - tops[g])
        part = jnp.sum(weights.reshape(STEP // 8, 8, WIDE), axis=0)
        out = jnp.dot(values[keys_of][:, at:at + STEP], weights.astype(jnp.bfloat16),
                      preferred_element_type=jnp.float32)
        total, acc = sums.get(g, (None, None))
        sums[g] = (part, out) if total is None else (total + part, acc + out)

    for stage in range(len(stages) + 1):
        scoring = units[stage] if stage < len(stages) else []
        weighing = units[stage - 1] if stage > 0 else []
        steps = max(len(scoring), len(weighing))
        for i in range(steps):
            for n in range(i * len(scoring) // steps, (i + 1) * len(scoring) // steps):
                score(stage % 2, n, scoring[n])
            for n in range(i * len(weighing) // steps, (i + 1) * len(weighing) // steps):
                weigh((stage - 1) % 2, n, weighing[n])
        for g in sorted({unit[0] for unit in weighing}):
            total, acc = sums[g]
            if flip is None:
                outs[0][0, :, g * WIDE:(g + 1) * WIDE] = acc
                outs[1][0, :, g * WIDE:(g + 1) * WIDE] = total
                outs[2][0, :, g * WIDE:(g + 1) * WIDE] = jnp.broadcast_to(tops[g], (8, WIDE))
            else:
                done = (acc / jnp.sum(total, axis=0, keepdims=True)).T.astype(jnp.bfloat16)
                for i in range(GROUP):
                    dx, dz = ROTATIONS[GROUP * g + i]
                    source = ((seq // 8) ^ dx) * 8 + (seq % 8 + 8 - dz) % 8
                    outs[0][pl.ds(pl.multiple_of(source * LOC, LOC), LOC), :] = done[i * LOC:(i + 1) * LOC, :]
        for g in sorted({unit[0] for unit in scoring}):
            top = jnp.max(tops[g], axis=0, keepdims=True)
            if g < known:
                at = slice(g * WIDE, (g + 1) * WIDE)
                old = state[2][klass, 0:1, at]
                top = jnp.maximum(top, old)
                fade = jnp.exp2(old - top)
                sums[g] = (state[1][klass, :, at] * fade, state[0][klass, :, at] * fade)
            tops[g] = top


def attend(stages, groups, known, state, flip):
    count = len(groups)
    rows = SEQ * LOC
    scratch = max(sum(len(key_groups) for _, key_groups in stage) for stage in stages) * DEEP
    if flip is None:
        shapes = [(4, HEAD_DIM, count * WIDE), (4, 8, count * WIDE), (4, 8, count * WIDE)]
        out_shape = [jax.ShapeDtypeStruct(shape, jnp.float32) for shape in shapes]
        out_specs = [pl.BlockSpec((1,) + shape[1:], lambda i: (i, 0, 0)) for shape in shapes]
    else:
        out_shape = [jax.ShapeDtypeStruct((rows, HEAD_DIM), jnp.bfloat16)]
        out_specs = [vmem()]
    work = sum(len(key_groups) for stage in stages for _, key_groups in stage) * WIDE * DEEP * (4 if flip is None else 1)
    return pl.pallas_call(
        lambda *refs: attend_kernel(stages, count, known, flip, *refs),
        grid=(4 if flip is None else 1,),
        in_specs=[vmem()] * (3 * count + len(state)),
        out_specs=out_specs,
        out_shape=out_shape,
        scratch_shapes=[pltpu.VMEM((scratch, WIDE), jnp.float32)] * 2,
        cost_estimate=pl.CostEstimate(flops=4 * work * HEAD_DIM, transcendentals=work,
                                      bytes_accessed=6 * count * DEEP * HEAD_DIM),
        compiler_params=pltpu.CompilerParams(vmem_limit_bytes=16 * 2**20),
        name="attend",
    )(*[g[0] for g in groups], *[g[1] for g in groups], *[g[2] for g in groups], *state)


def last_head_kernel(*refs):
    blocks, out_ref = refs[:4], refs[4]
    core, seq = lax.axis_index("dp") % 2, lax.axis_index("seq")
    wanted = jnp.where(idle_place(core, seq % 4) == 3, 2, 3)
    for flip, block in zip(XORS, blocks):
        @pl.when((seq // 4) ^ flip == wanted)
        def _():
            out_ref[...] = block[...]


def last_head(blocks):
    return pl.pallas_call(
        last_head_kernel,
        in_specs=[vmem()] * 4,
        out_specs=vmem(),
        out_shape=jax.ShapeDtypeStruct((SEQ * LOC, HEAD_DIM), jnp.bfloat16),
        compiler_params=pltpu.CompilerParams(vmem_limit_bytes=8 * 2**20),
        name="last_head",
    )(*blocks)


def merge_kernel(*refs):
    blocks, out_ref = refs[:5], refs[5]
    core, seq = lax.axis_index("dp") % 2, lax.axis_index("seq")
    place, chunk = seq // 4, seq % 4
    rows = out_ref.shape[1]
    at = pl.ds(pl.multiple_of(pl.program_id(0) * rows, rows), rows)
    row = lax.broadcasted_iota(jnp.int32, (OUT_COLS, HEAD_DIM), 0)
    col = lax.broadcasted_iota(jnp.int32, (OUT_COLS, HEAD_DIM), 1)
    shifts = []
    for flip in XORS:
        other = place ^ flip
        shift = head_at(core, other * 4 + chunk) * HEAD_DIM - chunk * OUT_COLS
        shifts.append(jnp.where(other == idle_place(core, chunk), FAR, shift))
    shifts.append(jnp.where(chunk == 0, FAR, 3 * chunk * HEAD_DIM - chunk * OUT_COLS))
    picks = [jnp.where(row == col + shift, 1.0, 0.0).astype(jnp.bfloat16) for shift in shifts]
    block = jnp.concatenate([ref[at, :] for ref in blocks], axis=1)
    out_ref[...] = lax.dot_general(jnp.concatenate(picks, axis=1), block, (((1,), (1,)), ((), ())),
                                   preferred_element_type=jnp.float32).astype(jnp.bfloat16)


def merge(blocks):
    rows = SEQ * LOC
    return pl.pallas_call(
        merge_kernel,
        grid=(4,),
        in_specs=[vmem()] * 5,
        out_specs=pl.BlockSpec((OUT_COLS, rows // 4), lambda i: (0, i)),
        out_shape=jax.ShapeDtypeStruct((OUT_COLS, rows), jnp.bfloat16),
        compiler_params=pltpu.CompilerParams(vmem_limit_bytes=24 * 2**20),
        name="merge",
    )(*blocks).T


def exchange_and_attend(queries, key_rows, value_rows):
    axes = ("dp", "seq")
    messages = pack(queries, key_rows, value_rows)
    got = [messages[0]]
    for r in range(1, 16):
        near = min(ROTATIONS[r][1], 8 - ROTATIONS[r][1]) <= 2
        perm = pairs(lambda s: turn(s, ROTATIONS[r]), lambda core, t: near or not idle(core, t))
        got.append(lax.ppermute(messages[r], axes, perm))
    groups = [gather_group(got[i:i + GROUP]) for i in range(0, 16, GROUP)]

    state = attend([[(0, (0, 1))], [(1, (0, 1))]], groups[:2], 0, [], None)
    state = attend([[(2, (0, 1, 2))], [(0, (2,)), (1, (2,))]], groups[:3], 2, state, None)
    last = [[(3, (0, 1, 2, 3))], [(0, (3,)), (1, (3,)), (2, (3,))]]
    blocks = []
    for flip in XORS:
        out = attend(last, groups, 3, state, flip)[0]
        if flip:
            perm = pairs(lambda s: ((s // 4) ^ flip) * 4 + s % 4, lambda core, t: True)
            out = lax.ppermute(out, axes, perm)
        blocks.append(out)
    tail = last_head(blocks)
    blocks.append(lax.ppermute(tail, axes, pairs(lambda s: turn(s, (0, 1)), lambda core, t: True)))
    return merge(blocks)


def solution(mesh):
    placed = (P(("dp", "seq"), None), P(("dp", "seq"), None), P(("dp", "seq"), None))
    return jax.shard_map(exchange_and_attend, mesh=mesh, in_specs=placed, out_specs=P("dp", "seq"), check_vma=False)
```

time: 231 us -> 131 us (0.57); the launches traced: 231 us -> 128 us
  blocking collectives: 65.1 us -> 0 us
  waiting for transfers between devices: 79 us -> 28.6 us
  starting transfers between devices: 19.8 us -> 64.3 us
  matrix products: 35 us -> 0 us
  Pallas kernels: 0 us -> 31.6 us
  other arithmetic: 14.7 us -> 0 us
  local copies, waits for them, and re-layouts: 17.1 us -> 3.47 us
    all_to_all x3 -> x0, waiting for transfers between devices: 79 us -> none  [the longest x1 26.8 us: by_heads(): lax.all_to_all(spread(value_rows), 'seq', split_axis=1, concat_axis=0, ti...]
    all_to_all x2 -> x0, blocking collectives: 65.1 us -> none  [the longest x1 32.6 us: on_device(): lax.all_to_all(shuffled, 'seq', split_axis=1, concat_axis=0, tiled=True)]
    ppermute x0 -> x19, starting transfers between devices: none -> 64.3 us  [the longest x15 55.2 us: exchange_and_attend(): got.append(lax.ppermute(messages[r], axes, perm))]
    dot_general x16 -> x0, matrix products: 35 us -> none  [the longest x8 17.9 us: one_block(): jnp.einsum('qhd,khd->hqk', query_block, flat_key, preferred_element_type=...]
    pallas_call x0 -> x13, Pallas kernels: none -> 31.6 us  [the longest x6 26.7 us: attend(): pl.pallas_call(lambda *refs: attend_kernel(stages, count, known, flip, *r...]
    ppermute x0 -> x19, waiting for transfers between devices: none -> 28.6 us  [the longest x3 12.6 us: exchange_and_attend(): out = lax.ppermute(out, axes, perm)]
    all_to_all x3 -> x0, starting transfers between devices: 19.8 us -> none  [the longest x1 11 us: by_heads(): lax.all_to_all(spread(queries), 'seq', split_axis=1, concat_axis=0, tiled...]
    reduce_sum x8 -> x0, other arithmetic: 12.1 us -> none  [one_block(): totals = jnp.sum(weights, axis=-1, keepdims=True)]
  transfers between devices with their start and end apart: 3 -> 19, of which waited for: 3 -> 5; matrix products, arithmetic and copies ran while one was open for 3% -> 0% of each run, Pallas kernels for 0% -> 15%
where the time goes in v3:
time: 131 us; the launch traced here: 128 us
  starting transfers between devices  64.3 us (49%)
  Pallas kernels  31.6 us (24%)
  waiting for transfers between devices  28.6 us (22%)
  local copies, waits for them, and re-layouts  3.47 us (3%)
    ppermute x15, starting transfers between devices, exchange_and_attend(): got.append(lax.ppermute(messages[r], axes, perm))  55.2 us
    pallas_call x6, Pallas kernels, attend(): pl.pallas_call(lambda *refs: attend_kernel(stages, count, known, flip, *r...  26.7 us
    ppermute x3, waiting for transfers between devices, exchange_and_attend(): out = lax.ppermute(out, axes, perm)  12.6 us
    ppermute x1, waiting for transfers between devices, exchange_and_attend(): lax.ppermute(tail, axes, pairs(lambda s: turn(s, (0, 1)), lambda core, t:...  10.7 us
    ppermute x3, starting transfers between devices, exchange_and_attend(): out = lax.ppermute(out, axes, perm)  8.99 us
    ppermute x15, waiting for transfers between devices, exchange_and_attend(): got.append(lax.ppermute(messages[r], axes, perm))  5.32 us
    unnamed x6, local copies, waits for them, and re-layouts  3.47 us
  transfers between devices with their start and end apart: 19, of which 5 were waited for; matrix products, arithmetic and copies ran while one was open for 0% of the time, Pallas kernels for 15%

profile of v3, /device:TPU:16, one launch (start us, length us, event | category | flops | bytes accessed | tf_op | source)
XLA Modules:
  0.0 128.2 jit_solution(15294184355430880139)
XLA Ops:
  0.0 1.2 copy-done
  1.2 1.2 copy-done.1
  2.3 1.2 copy-done.2
  3.5 1.9 %pack.1 = (bf16[768,128]{1,0:T(8,128)(2,1)S(1)}, bf16[768,128]{1,0:T(8,128)(2,1)S(1)}, bf16[768,128]{1,0:T(8,128)(2,1)S(1)}, bf16[768,128]{1,0:T(8,128)(2,1)S(1)...) custom-call(bf16[256,1664]{1,0:T(8,128)(2,1)S(1)} %copy-done, ...), custom_call_target="tpu_custom_call" | custom-call | tf_op jit(solution)/shard_map/pack/pallas_call | solution.py:101
  5.4 3.1 %collective-permute-start = (bf16[768,128]{1,0:T(8,128)(2,1)S(1)}, bf16[768,128]{1,0:T(8,128)(2,1)S(1)}, u32[]{:S(2)}, u32[]{:S(2)}) collective-permute-start(bf16[768,128]{1,0:T(8,128)(2,1)S(1)} %get-tuple-element.40), channel_id=1, source_target_pairs={{0,8},{1,9},{2,10},{3,11},{4,12},{5,13},{6,14},{7,15},{8,0},{9,1},... | collective-permute-start | bytes 589832 | tf_op jit(solution)/shard_map/ppermute | solution.py:293
  8.5 1.9 %collective-permute-start.1 = (bf16[768,128]{1,0:T(8,128)(2,1)S(1)}, bf16[768,128]{1,0:T(8,128)(2,1)S(1)}, u32[]{:S(2)}, u32[]{:S(2)}) collective-permute-start(bf16[768,128]{1,0:T(8,128)(2,1)S(1)} %get-tuple-element.41), channel_id=1, source_target_pairs={{0,1},{1,2},{2,3},{3,4},{4,5},{5,6},{6,7},{7,0},{8,9},{9,10},{10,1... | collective-permute-start | bytes 589832 | tf_op jit(solution)/shard_map/ppermute | solution.py:293
  10.4 3.9 %collective-permute-start.2 = (bf16[768,128]{1,0:T(8,128)(2,1)S(1)}, bf16[768,128]{1,0:T(8,128)(2,1)S(1)}, u32[]{:S(2)}, u32[]{:S(2)}) collective-permute-start(bf16[768,128]{1,0:T(8,128)(2,1)S(1)} %get-tuple-element.42), channel_id=1, source_target_pairs={{0,7},{1,0},{2,1},{3,2},{4,3},{5,4},{6,5},{7,6},{8,15},{9,8},{10,9... | collective-permute-start | bytes 589832 | tf_op jit(solution)/shard_map/ppermute | solution.py:293
  14.4 5.6 %collective-permute-start.4 = (bf16[768,128]{1,0:T(8,128)(2,1)S(1)}, bf16[768,128]{1,0:T(8,128)(2,1)S(1)}, u32[]{:S(2)}, u32[]{:S(2)}) collective-permute-start(bf16[768,128]{1,0:T(8,128)(2,1)S(1)} %get-tuple-element.45), channel_id=1, source_target_pairs={{0,15},{1,8},{2,9},{3,10},{4,11},{5,12},{6,13},{7,14},{8,7},{9,0},... | collective-permute-start | bytes 589832 | tf_op jit(solution)/shard_map/ppermute | solution.py:293
  20.1 4.0 %collective-permute-start.6 = (bf16[768,128]{1,0:T(8,128)(2,1)S(1)}, bf16[768,128]{1,0:T(8,128)(2,1)S(1)}, u32[]{:S(2)}, u32[]{:S(2)}) collective-permute-start(bf16[768,128]{1,0:T(8,128)(2,1)S(1)} %get-tuple-element.47), channel_id=1, source_target_pairs={{0,6},{1,7},{2,0},{3,1},{4,2},{5,3},{6,4},{7,5},{8,14},{9,15},{10,... | collective-permute-start | bytes 589832 | tf_op jit(solution)/shard_map/ppermute | solution.py:293
  24.2 1.0 collective-permute-start.7
  25.3 5.2 %collective-permute-done.3.refs_0_ = bf16[768,128]{1,0:T(8,128)(2,1)S(1)} collective-permute-done((bf16[768,128]{1,0:T(8,128)(2,1)S(1)}, bf16[768,128]{1,0:T(8,128)(2,1)S(1)}, u32[]{:S(2)}, u32[]{:S(2)}) %collective-permute-start.3) | collective-permute-done | bytes 196640 | tf_op jit(solution)/shard_map/ppermute | solution.py:293
  30.5 0.8 collective-permute-start.8
  31.3 3.1 %collective-permute-start.9 = (bf16[768,128]{1,0:T(8,128)(2,1)S(1)}, bf16[768,128]{1,0:T(8,128)(2,1)S(1)}, u32[]{:S(2)}, u32[]{:S(2)}) collective-permute-start(bf16[768,128]{1,0:T(8,128)(2,1)S(1)} %get-tuple-element.51), channel_id=1, source_target_pairs={{0,3},{1,4},{2,5},{4,7},{5,0},{7,2},{8,11},{9,12},{10,13},{11,14},... | collective-permute-start | bytes 589832 | tf_op jit(solution)/shard_map/ppermute | solution.py:293
  34.5 7.9 %collective-permute-start.10 = (bf16[768,128]{1,0:T(8,128)(2,1)S(1)}, bf16[768,128]{1,0:T(8,128)(2,1)S(1)}, u32[]{:S(2)}, u32[]{:S(2)}) collective-permute-start(bf16[768,128]{1,0:T(8,128)(2,1)S(1)} %get-tuple-element.52), channel_id=1, source_target_pairs={{0,5},{2,7},{3,0},{5,2},{6,3},{7,4},{8,13},{9,14},{11,8},{12,9},{1... | collective-permute-start | bytes 589832 | tf_op jit(solution)/shard_map/ppermute | solution.py:293
  42.4 8.3 %collective-permute-start.11 = (bf16[768,128]{1,0:T(8,128)(2,1)S(1)}, bf16[768,128]{1,0:T(8,128)(2,1)S(1)}, u32[]{:S(2)}, u32[]{:S(2)}) collective-permute-start(bf16[768,128]{1,0:T(8,128)(2,1)S(1)} %get-tuple-element.54), channel_id=1, source_target_pairs={{0,11},{1,12},{2,13},{3,14},{5,8},{6,9},{7,10},{8,3},{9,4},{10,5},... | collective-permute-start | bytes 589832 | tf_op jit(solution)/shard_map/ppermute | solution.py:293
  50.6 0.1 gather_group.5
  50.8 7.7 %attend.6 = (f32[4,128,512]{2,1,0:T(8,128)S(1)}, f32[4,8,512]{2,1,0:T(8,128)S(1)}, f32[4,8,512]{2,1,0:T(8,128)S(1)}) custom-call(bf16[4,256,128]{2,1,0:T(8,128)(2,1)S(1)} %get-tuple-element.43.refs_0_, bf16[4,256,128]{2,1,0:T(8,128)(2,1)S(1)} %get-tuple-element.48.refs_1_, bf16[1024,128]{1,0:T(8,128)(2,1)S(1)} %get-tuple-element.59.refs_2_.refs_3_.refs_4_, ...), custom_call_target="tpu_custom_call" | custom-call | flops 2147483648 | bytes 1572864 | tf_op jit(solution)/shard_map/attend/pallas_call | solution.py:218
  58.5 3.0 %collective-permute-start.12 = (bf16[768,128]{1,0:T(8,128)(2,1)S(1)}, bf16[768,128]{1,0:T(8,128)(2,1)S(1)}, u32[]{:S(2)}, u32[]{:S(2)}) collective-permute-start(bf16[768,128]{1,0:T(8,128)(2,1)S(1)} %get-tuple-element.55), channel_id=1, source_target_pairs={{0,13},{1,14},{3,8},{4,9},{5,10},{6,11},{7,12},{8,5},{10,7},{11,0}... | collective-permute-start | bytes 589832 | tf_op jit(solution)/shard_map/ppermute | solution.py:293
  61.5 2.6 %collective-permute-start.13 = (bf16[768,128]{1,0:T(8,128)(2,1)S(1)}, bf16[768,128]{1,0:T(8,128)(2,1)S(1)}, u32[]{:S(2)}, u32[]{:S(2)}) collective-permute-start(bf16[768,128]{1,0:T(8,128)(2,1)S(1)} %get-tuple-element.56), channel_id=1, source_target_pairs={{0,4},{1,5},{3,7},{4,0},{6,2},{7,3},{8,12},{9,13},{10,14},{12,8},{... | collective-permute-start | bytes 589832 | tf_op jit(solution)/shard_map/ppermute | solution.py:293
  64.1 9.9 %collective-permute-start.14 = (bf16[768,128]{1,0:T(8,128)(2,1)S(1)}, bf16[768,128]{1,0:T(8,128)(2,1)S(1)}, u32[]{:S(2)}, u32[]{:S(2)}) collective-permute-start(bf16[768,128]{1,0:T(8,128)(2,1)S(1)} %get-tuple-element.57), channel_id=1, source_target_pairs={{0,12},{1,13},{2,14},{4,8},{5,9},{6,10},{7,11},{8,4},{9,5},{11,7},... | collective-permute-start | bytes 589832 | tf_op jit(solution)/shard_map/ppermute | solution.py:293
  74.1 8.7 %attend.7 = (f32[4,128,768]{2,1,0:T(8,128)S(1)}, f32[4,8,768]{2,1,0:T(8,128)S(1)}, f32[4,8,768]{2,1,0:T(8,128)S(1)}) custom-call(bf16[4,256,128]{2,1,0:T(8,128)(2,1)S(1)} %get-tuple-element.43.refs_0_, bf16[4,256,128]{2,1,0:T(8,128)(2,1)S(1)} %get-tuple-element.48.refs_1_, bf16[4,256,128]{2,1,0:T(8,128)(2,1)S(1)} %get-tuple-element.53.refs_2_, ...), custom_call_target="tpu_custom_call" | custom-call | flops 2684354560 | bytes 2359296 | tf_op jit(solution)/shard_map/attend/pallas_call | solution.py:218
  83.1 2.6 %attend.10 = bf16[1024,128]{1,0:T(8,128)(2,1)S(1)} custom-call(bf16[4,256,128]{2,1,0:T(8,128)(2,1)S(1)} %get-tuple-element.43.refs_0_, bf16[4,256,128]{2,1,0:T(8,128)(2,1)S(1)} %get-tuple-element.48.refs_1_, bf16[4,256,128]{2,1,0:T(8,128)(2,1)S(1)} %get-tuple-element.53.refs_2_, bf16[4,256,128]{2,1,0:T(8,128)(2,1)S(1)} %get-tuple-element.58.refs_3_, ...), custom_call_target="tpu_custom_call" | custom-call | flops 939524096 | bytes 3145728 | tf_op jit(solution)/shard_map/attend/pallas_call | solution.py:218
  85.6 2.6 %attend.9 = bf16[1024,128]{1,0:T(8,128)(2,1)S(1)} custom-call(bf16[4,256,128]{2,1,0:T(8,128)(2,1)S(1)} %get-tuple-element.43.refs_0_, bf16[4,256,128]{2,1,0:T(8,128)(2,1)S(1)} %get-tuple-element.48.refs_1_, bf16[4,256,128]{2,1,0:T(8,128)(2,1)S(1)} %get-tuple-element.53.refs_2_, bf16[4,256,128]{2,1,0:T(8,128)(2,1)S(1)} %get-tuple-element.58.refs_3_, ...), custom_call_target="tpu_custom_call" | custom-call | flops 939524096 | bytes 3145728 | tf_op jit(solution)/shard_map/attend/pallas_call | solution.py:218
  88.2 2.6 %attend.8 = bf16[1024,128]{1,0:T(8,128)(2,1)S(1)} custom-call(bf16[4,256,128]{2,1,0:T(8,128)(2,1)S(1)} %get-tuple-element.43.refs_0_, bf16[4,256,128]{2,1,0:T(8,128)(2,1)S(1)} %get-tuple-element.48.refs_1_, bf16[4,256,128]{2,1,0:T(8,128)(2,1)S(1)} %get-tuple-element.53.refs_2_, bf16[4,256,128]{2,1,0:T(8,128)(2,1)S(1)} %get-tuple-element.58.refs_3_, ...), custom_call_target="tpu_custom_call" | custom-call | flops 939524096 | bytes 3145728 | tf_op jit(solution)/shard_map/attend/pallas_call | solution.py:218
  90.8 3.0 %collective-permute-start.15 = (bf16[1024,128]{1,0:T(8,128)(2,1)S(1)}, bf16[1024,128]{1,0:T(8,128)(2,1)S(1)}, u32[]{:S(2)}, u32[]{:S(2)}) collective-permute-start(bf16[1024,128]{1,0:T(8,128)(2,1)S(1)} %attend.8), channel_id=1, source_target_pairs={{0,12},{1,13},{2,14},{3,15},{4,8},{5,9},{6,10},{7,11},{8,4},{9,5},... | collective-permute-start | bytes 786440 | tf_op jit(solution)/shard_map/ppermute | solution.py:304
  93.8 2.9 %collective-permute-start.16 = (bf16[1024,128]{1,0:T(8,128)(2,1)S(1)}, bf16[1024,128]{1,0:T(8,128)(2,1)S(1)}, u32[]{:S(2)}, u32[]{:S(2)}) collective-permute-start(bf16[1024,128]{1,0:T(8,128)(2,1)S(1)} %attend.9), channel_id=1, source_target_pairs={{0,4},{1,5},{2,6},{3,7},{4,0},{5,1},{6,2},{7,3},{8,12},{9,13},{10,... | collective-permute-start | bytes 786440 | tf_op jit(solution)/shard_map/ppermute | solution.py:304
  96.6 3.1 %collective-permute-start.17 = (bf16[1024,128]{1,0:T(8,128)(2,1)S(1)}, bf16[1024,128]{1,0:T(8,128)(2,1)S(1)}, u32[]{:S(2)}, u32[]{:S(2)}) collective-permute-start(bf16[1024,128]{1,0:T(8,128)(2,1)S(1)} %attend.10), channel_id=1, source_target_pairs={{0,8},{1,9},{2,10},{3,11},{4,12},{5,13},{6,14},{7,15},{8,0},{9,1},... | collective-permute-start | bytes 786440 | tf_op jit(solution)/shard_map/ppermute | solution.py:304
  99.7 2.5 %attend.11.refs_3_ = bf16[1024,128]{1,0:T(8,128)(2,1)S(1)} custom-call(bf16[4,256,128]{2,1,0:T(8,128)(2,1)S(1)} %get-tuple-element.43.refs_0_, bf16[4,256,128]{2,1,0:T(8,128)(2,1)S(1)} %get-tuple-element.48.refs_1_, bf16[4,256,128]{2,1,0:T(8,128)(2,1)S(1)} %get-tuple-element.53.refs_2_, bf16[4,256,128]{2,1,0:T(8,128)(2,1)S(1)} %get-tuple-element.58.refs_3_, ...), custom_call_target="tpu_custom_call" | custom-call | flops 939524096 | bytes 3145728 | tf_op jit(solution)/shard_map/attend/pallas_call | solution.py:218
  102.3 5.2 %collective-permute-done.15.refs_0_ = bf16[1024,128]{1,0:T(8,128)(2,1)S(1)} collective-permute-done((bf16[1024,128]{1,0:T(8,128)(2,1)S(1)}, bf16[1024,128]{1,0:T(8,128)(2,1)S(1)}, u32[]{:S(2)}, u32[]{:S(2)}) %collective-permute-start.15) | collective-permute-done | bytes 262176 | tf_op jit(solution)/shard_map/ppermute | solution.py:304
  107.5 7.4 %collective-permute-done.16.refs_1_ = bf16[1024,128]{1,0:T(8,128)(2,1)S(1)} collective-permute-done((bf16[1024,128]{1,0:T(8,128)(2,1)S(1)}, bf16[1024,128]{1,0:T(8,128)(2,1)S(1)}, u32[]{:S(2)}, u32[]{:S(2)}) %collective-permute-start.16) | collective-permute-done | bytes 262176 | tf_op jit(solution)/shard_map/ppermute | solution.py:304
  115.0 10.7 %collective-permute-done.18.refs_4_ = bf16[1024,128]{1,0:T(8,128)(2,1)S(1)} collective-permute-done((bf16[1024,128]{1,0:T(8,128)(2,1)S(1)}, bf16[1024,128]{1,0:T(8,128)(2,1)S(1)}, u32[]{:S(2)}, u32[]{:S(2)}) %collective-permute-start.18) | collective-permute-done | bytes 262176 | tf_op jit(solution)/shard_map/ppermute | solution.py:307
  125.7 2.5 %merge.1 = bf16[416,1024]{1,0:T(8,128)(2,1)} custom-call(bf16[1024,128]{1,0:T(8,128)(2,1)S(1)} %collective-permute-done.15.refs_0_, bf16[1024,128]{1,0:T(8,128)(2,1)S(1)} %collective-permute-done.16.refs_1_, bf16[1024,128]{1,0:T(8,128)(2,1)S(1)} %collective-permute-done.17.refs_2_, bf16[1024,128]{1,0:T(8,128)(2,1)S(1)} %attend.11.refs_3_, ...), custom_call_target="tpu_custom_call" | custom-call | tf_op jit(solution)/shard_map/merge/pallas_call | solution.py:275
  (25 shorter events, 0.6 us)
Async XLA Ops:
  0.0 1.2 copy-start
  1.2 1.2 copy-start.1
  2.3 1.2 copy-start.2
  5.4 14.6 %collective-permute-start = (bf16[768,128]{1,0:T(8,128)(2,1)S(1)}, bf16[768,128]{1,0:T(8,128)(2,1)S(1)}, u32[]{:S(2)}, u32[]{:S(2)}) collective-permute-start(bf16[768,128]{1,0:T(8,128)(2,1)S(1)} %get-tuple-element.40), channel_id=1, source_target_pairs={{0,8},{1,9},{2,10},{3,11},{4,12},{5,13},{6,14},{7,15},{8,0},{9,1},... | collective-permute-start | bytes 589832 | tf_op jit(solution)/shard_map/ppermute | solution.py:293
  8.5 11.6 %collective-permute-start.1 = (bf16[768,128]{1,0:T(8,128)(2,1)S(1)}, bf16[768,128]{1,0:T(8,128)(2,1)S(1)}, u32[]{:S(2)}, u32[]{:S(2)}) collective-permute-start(bf16[768,128]{1,0:T(8,128)(2,1)S(1)} %get-tuple-element.41), channel_id=1, source_target_pairs={{0,1},{1,2},{2,3},{3,4},{4,5},{5,6},{6,7},{7,0},{8,9},{9,10},{10,1... | collective-permute-start | bytes 589832 | tf_op jit(solution)/shard_map/ppermute | solution.py:293
  10.4 13.7 %collective-permute-start.2 = (bf16[768,128]{1,0:T(8,128)(2,1)S(1)}, bf16[768,128]{1,0:T(8,128)(2,1)S(1)}, u32[]{:S(2)}, u32[]{:S(2)}) collective-permute-start(bf16[768,128]{1,0:T(8,128)(2,1)S(1)} %get-tuple-element.42), channel_id=1, source_target_pairs={{0,7},{1,0},{2,1},{3,2},{4,3},{5,4},{6,5},{7,6},{8,15},{9,8},{10,9... | collective-permute-start | bytes 589832 | tf_op jit(solution)/shard_map/ppermute | solution.py:293
  14.4 16.1 %collective-permute-start.3 = (bf16[768,128]{1,0:T(8,128)(2,1)S(1)}, bf16[768,128]{1,0:T(8,128)(2,1)S(1)}, u32[]{:S(2)}, u32[]{:S(2)}) collective-permute-start(bf16[768,128]{1,0:T(8,128)(2,1)S(1)} %get-tuple-element.44), channel_id=1, source_target_pairs={{0,9},{1,10},{2,11},{3,12},{4,13},{5,14},{6,15},{7,8},{8,1},{9,2},... | collective-permute-start | bytes 589832 | tf_op jit(solution)/shard_map/ppermute | solution.py:293
  14.4 17.0 %collective-permute-start.4 = (bf16[768,128]{1,0:T(8,128)(2,1)S(1)}, bf16[768,128]{1,0:T(8,128)(2,1)S(1)}, u32[]{:S(2)}, u32[]{:S(2)}) collective-permute-start(bf16[768,128]{1,0:T(8,128)(2,1)S(1)} %get-tuple-element.45), channel_id=1, source_target_pairs={{0,15},{1,8},{2,9},{3,10},{4,11},{5,12},{6,13},{7,14},{8,7},{9,0},... | collective-permute-start | bytes 589832 | tf_op jit(solution)/shard_map/ppermute | solution.py:293
  20.0 14.4 %collective-permute-start.5 = (bf16[768,128]{1,0:T(8,128)(2,1)S(1)}, bf16[768,128]{1,0:T(8,128)(2,1)S(1)}, u32[]{:S(2)}, u32[]{:S(2)}) collective-permute-start(bf16[768,128]{1,0:T(8,128)(2,1)S(1)} %get-tuple-element.46), channel_id=1, source_target_pairs={{0,2},{1,3},{2,4},{3,5},{4,6},{5,7},{6,0},{7,1},{8,10},{9,11},{10,... | collective-permute-start | bytes 589832 | tf_op jit(solution)/shard_map/ppermute | solution.py:293
  20.1 22.2 %collective-permute-start.6 = (bf16[768,128]{1,0:T(8,128)(2,1)S(1)}, bf16[768,128]{1,0:T(8,128)(2,1)S(1)}, u32[]{:S(2)}, u32[]{:S(2)}) collective-permute-start(bf16[768,128]{1,0:T(8,128)(2,1)S(1)} %get-tuple-element.47), channel_id=1, source_target_pairs={{0,6},{1,7},{2,0},{3,1},{4,2},{5,3},{6,4},{7,5},{8,14},{9,15},{10,... | collective-permute-start | bytes 589832 | tf_op jit(solution)/shard_map/ppermute | solution.py:293
  24.2 34.3 %collective-permute-start.7 = (bf16[768,128]{1,0:T(8,128)(2,1)S(1)}, bf16[768,128]{1,0:T(8,128)(2,1)S(1)}, u32[]{:S(2)}, u32[]{:S(2)}) collective-permute-start(bf16[768,128]{1,0:T(8,128)(2,1)S(1)} %get-tuple-element.49), channel_id=1, source_target_pairs={{0,10},{1,11},{2,12},{3,13},{4,14},{5,15},{6,8},{7,9},{8,2},{9,3},... | collective-permute-start | bytes 589832 | tf_op jit(solution)/shard_map/ppermute | solution.py:293
  30.5 31.0 %collective-permute-start.8 = (bf16[768,128]{1,0:T(8,128)(2,1)S(1)}, bf16[768,128]{1,0:T(8,128)(2,1)S(1)}, u32[]{:S(2)}, u32[]{:S(2)}) collective-permute-start(bf16[768,128]{1,0:T(8,128)(2,1)S(1)} %get-tuple-element.50), channel_id=1, source_target_pairs={{0,14},{1,15},{2,8},{3,9},{4,10},{5,11},{6,12},{7,13},{8,6},{9,7},... | collective-permute-start | bytes 589832 | tf_op jit(solution)/shard_map/ppermute | solution.py:293
  31.3 32.7 %collective-permute-start.9 = (bf16[768,128]{1,0:T(8,128)(2,1)S(1)}, bf16[768,128]{1,0:T(8,128)(2,1)S(1)}, u32[]{:S(2)}, u32[]{:S(2)}) collective-permute-start(bf16[768,128]{1,0:T(8,128)(2,1)S(1)} %get-tuple-element.51), channel_id=1, source_target_pairs={{0,3},{1,4},{2,5},{4,7},{5,0},{7,2},{8,11},{9,12},{10,13},{11,14},... | collective-permute-start | bytes 589832 | tf_op jit(solution)/shard_map/ppermute | solution.py:293
  34.5 39.5 %collective-permute-start.10 = (bf16[768,128]{1,0:T(8,128)(2,1)S(1)}, bf16[768,128]{1,0:T(8,128)(2,1)S(1)}, u32[]{:S(2)}, u32[]{:S(2)}) collective-permute-start(bf16[768,128]{1,0:T(8,128)(2,1)S(1)} %get-tuple-element.52), channel_id=1, source_target_pairs={{0,5},{2,7},{3,0},{5,2},{6,3},{7,4},{8,13},{9,14},{11,8},{12,9},{1... | collective-permute-start | bytes 589832 | tf_op jit(solution)/shard_map/ppermute | solution.py:293
  42.4 40.5 %collective-permute-start.11 = (bf16[768,128]{1,0:T(8,128)(2,1)S(1)}, bf16[768,128]{1,0:T(8,128)(2,1)S(1)}, u32[]{:S(2)}, u32[]{:S(2)}) collective-permute-start(bf16[768,128]{1,0:T(8,128)(2,1)S(1)} %get-tuple-element.54), channel_id=1, source_target_pairs={{0,11},{1,12},{2,13},{3,14},{5,8},{6,9},{7,10},{8,3},{9,4},{10,5},... | collective-permute-start | bytes 589832 | tf_op jit(solution)/shard_map/ppermute | solution.py:293
  58.5 24.4 %collective-permute-start.12 = (bf16[768,128]{1,0:T(8,128)(2,1)S(1)}, bf16[768,128]{1,0:T(8,128)(2,1)S(1)}, u32[]{:S(2)}, u32[]{:S(2)}) collective-permute-start(bf16[768,128]{1,0:T(8,128)(2,1)S(1)} %get-tuple-element.55), channel_id=1, source_target_pairs={{0,13},{1,14},{3,8},{4,9},{5,10},{6,11},{7,12},{8,5},{10,7},{11,0}... | collective-permute-start | bytes 589832 | tf_op jit(solution)/shard_map/ppermute | solution.py:293
  61.5 21.4 %collective-permute-start.13 = (bf16[768,128]{1,0:T(8,128)(2,1)S(1)}, bf16[768,128]{1,0:T(8,128)(2,1)S(1)}, u32[]{:S(2)}, u32[]{:S(2)}) collective-permute-start(bf16[768,128]{1,0:T(8,128)(2,1)S(1)} %get-tuple-element.56), channel_id=1, source_target_pairs={{0,4},{1,5},{3,7},{4,0},{6,2},{7,3},{8,12},{9,13},{10,14},{12,8},{... | collective-permute-start | bytes 589832 | tf_op jit(solution)/shard_map/ppermute | solution.py:293
  64.1 18.8 %collective-permute-start.14 = (bf16[768,128]{1,0:T(8,128)(2,1)S(1)}, bf16[768,128]{1,0:T(8,128)(2,1)S(1)}, u32[]{:S(2)}, u32[]{:S(2)}) collective-permute-start(bf16[768,128]{1,0:T(8,128)(2,1)S(1)} %get-tuple-element.57), channel_id=1, source_target_pairs={{0,12},{1,13},{2,14},{4,8},{5,9},{6,10},{7,11},{8,4},{9,5},{11,7},... | collective-permute-start | bytes 589832 | tf_op jit(solution)/shard_map/ppermute | solution.py:293
  90.8 16.7 %collective-permute-start.15 = (bf16[1024,128]{1,0:T(8,128)(2,1)S(1)}, bf16[1024,128]{1,0:T(8,128)(2,1)S(1)}, u32[]{:S(2)}, u32[]{:S(2)}) collective-permute-start(bf16[1024,128]{1,0:T(8,128)(2,1)S(1)} %attend.8), channel_id=1, source_target_pairs={{0,12},{1,13},{2,14},{3,15},{4,8},{5,9},{6,10},{7,11},{8,4},{9,5},... | collective-permute-start | bytes 786440 | tf_op jit(solution)/shard_map/ppermute | solution.py:304
  93.8 21.1 %collective-permute-start.16 = (bf16[1024,128]{1,0:T(8,128)(2,1)S(1)}, bf16[1024,128]{1,0:T(8,128)(2,1)S(1)}, u32[]{:S(2)}, u32[]{:S(2)}) collective-permute-start(bf16[1024,128]{1,0:T(8,128)(2,1)S(1)} %attend.9), channel_id=1, source_target_pairs={{0,4},{1,5},{2,6},{3,7},{4,0},{5,1},{6,2},{7,3},{8,12},{9,13},{10,... | collective-permute-start | bytes 786440 | tf_op jit(solution)/shard_map/ppermute | solution.py:304
  96.6 18.2 %collective-permute-start.17 = (bf16[1024,128]{1,0:T(8,128)(2,1)S(1)}, bf16[1024,128]{1,0:T(8,128)(2,1)S(1)}, u32[]{:S(2)}, u32[]{:S(2)}) collective-permute-start(bf16[1024,128]{1,0:T(8,128)(2,1)S(1)} %attend.10), channel_id=1, source_target_pairs={{0,8},{1,9},{2,10},{3,11},{4,12},{5,13},{6,14},{7,15},{8,0},{9,1},... | collective-permute-start | bytes 786440 | tf_op jit(solution)/shard_map/ppermute | solution.py:304
  114.9 10.8 %collective-permute-start.18 = (bf16[1024,128]{1,0:T(8,128)(2,1)S(1)}, bf16[1024,128]{1,0:T(8,128)(2,1)S(1)}, u32[]{:S(2)}, u32[]{:S(2)}) collective-permute-start(bf16[1024,128]{1,0:T(8,128)(2,1)S(1)} %last_head.1), channel_id=1, source_target_pairs={{0,1},{1,2},{2,3},{3,4},{4,5},{5,6},{6,7},{7,0},{8,9},{9,10},{10,1... | collective-permute-start | bytes 786440 | tf_op jit(solution)/shard_map/ppermute | solution.py:307

commit v4 on v3

v4 whole, which is shorter than its diff:
```python
import itertools
import math

import jax
import jax.numpy as jnp
from jax import lax
from jax.experimental import pallas as pl
from jax.experimental.pallas import tpu as pltpu
from jax.sharding import PartitionSpec as P


HEAD_DIM = 128
HEADS = 13
SEQ = 16
TOK = 256
LOC = 64
GROUP = 4
WIDE = GROUP * LOC
DEEP = GROUP * TOK
STEP = 512
OUT_COLS = 416
SPLIT = 96
FAR = 1 << 20
LOG2_SCALE = math.log2(math.e) / math.sqrt(HEAD_DIM)


IDLE = ((9, 0, 1, 3), (9, 3, 2, 0))

ROTATIONS = ((0, 0), (1, 0), (0, 1), (0, 7), (1, 1), (1, 7), (0, 2), (0, 6), (1, 2), (1, 6), (0, 3), (0, 5), (1, 3),
             (1, 5), (0, 4), (1, 4))
XORS = (3, 1, 2, 0)
NEAR = 2
FILL_SPREAD = False
FILL_RETURN = True


def idle(core, seq):
    place, chunk = seq // 4, seq % 4
    return chunk > 0 and place == IDLE[core][chunk]


def turn(seq, rotation):
    dx, dz = rotation
    return ((seq // 8) ^ dx) * 8 + (seq % 8 + dz) % 8


def hops(source, target):
    along_z = abs(source % 8 - target % 8)
    return 10 * min(along_z, 8 - along_z) + (source // 8 != target // 8)


def pairs(step, active, fill=False):
    out = []
    for dp in range(16):
        rest = []
        for seq in range(SEQ):
            if active(dp % 2, seq, step(seq)):
                out.append((dp * SEQ + seq, dp * SEQ + step(seq)))
            else:
                rest.append(seq)
        if fill and rest:
            targets = min(itertools.permutations([step(seq) for seq in rest]),
                          key=lambda order: sum(map(hops, rest, order)))
            out.extend((dp * SEQ + seq, dp * SEQ + target) for seq, target in zip(rest, targets))
    return out


def pick(index, values):
    out = jnp.int32(values[-1])
    for at in range(len(values) - 1):
        out = jnp.where(index == at, jnp.int32(values[at]), out)
    return out


def idle_place(core, chunk):
    return jnp.where(core == 0, pick(chunk, IDLE[0]), pick(chunk, IDLE[1]))


def head_at(core, seq):
    place, chunk = seq // 4, seq % 4
    late = jnp.where(place > idle_place(core, chunk), 1, 0)
    return jnp.minimum(jnp.where(chunk == 0, place, 1 + 3 * chunk + place - late), HEADS - 1)


def vmem():
    return pl.BlockSpec(memory_space=pltpu.VMEM)


def pack_kernel(q_ref, k_ref, v_ref, *refs):
    outs, queries, sems = refs[:16], refs[16], refs[17]
    core, seq = lax.axis_index("dp") % 2, lax.axis_index("seq")
    first = pltpu.make_async_copy(q_ref, queries, sems.at[32])
    first.start()
    copies, columns = [], []
    for r, (dx, dz) in enumerate(ROTATIONS):
        target = ((seq // 8) ^ dx) * 8 + (seq % 8 + dz) % 8
        at = pl.ds(pl.multiple_of(head_at(core, target) * HEAD_DIM, HEAD_DIM), HEAD_DIM)
        columns.append(at)
        for i, ref in enumerate((k_ref, v_ref)):
            copy = pltpu.make_async_copy(ref.at[:, at], outs[r].at[(i + 1) * TOK:(i + 2) * TOK, :], sems.at[2 * r + i])
            copy.start()
            copies.append(copy)
    row = lax.broadcasted_iota(jnp.int32, (TOK, TOK), 0)
    col = lax.broadcasted_iota(jnp.int32, (TOK, TOK), 1)
    grid_row, grid_col = col // 64, col % 64
    wanted = ((grid_row % 2) * 2 + grid_col % 2) * LOC + (grid_row // 2) * 32 + grid_col // 2
    order = jnp.where(row == wanted, 1.0, 0.0).astype(jnp.bfloat16)
    first.wait()
    for r in range(16):
        outs[r][0:TOK, :] = jnp.dot(order, queries[:, columns[r]],
                                    preferred_element_type=jnp.float32).astype(jnp.bfloat16)
    for copy in copies:
        copy.wait()


def pack(queries, key_rows, value_rows):
    shape = jax.ShapeDtypeStruct((3 * TOK, HEAD_DIM), jnp.bfloat16)
    return pl.pallas_call(
        pack_kernel,
        in_specs=[pl.BlockSpec(memory_space=pltpu.HBM)] * 3,
        out_specs=[vmem()] * 16,
        out_shape=[shape] * 16,
        scratch_shapes=[pltpu.VMEM((TOK, HEADS * HEAD_DIM), jnp.bfloat16), pltpu.SemaphoreType.DMA((33,))],
        compiler_params=pltpu.CompilerParams(vmem_limit_bytes=16 * 2**20),
        name="pack",
    )(queries, key_rows, value_rows)


def gather_kernel(*refs):
    got, (q_out, k_out, v_out) = refs[:GROUP], refs[GROUP:]
    for i in range(GROUP):
        for klass in range(4):
            q_out[klass, i * LOC:(i + 1) * LOC, :] = got[i][klass * LOC:(klass + 1) * LOC, :]
        k_out[i * TOK:(i + 1) * TOK, :] = got[i][TOK:2 * TOK, :]
        v_out[:, i * TOK:(i + 1) * TOK] = got[i][2 * TOK:, :].T


def gather_group(messages):
    return pl.pallas_call(
        gather_kernel,
        in_specs=[vmem()] * GROUP,
        out_specs=[vmem()] * 3,
        out_shape=[
            jax.ShapeDtypeStruct((4, WIDE, HEAD_DIM), jnp.bfloat16),
            jax.ShapeDtypeStruct((DEEP, HEAD_DIM), jnp.bfloat16),
            jax.ShapeDtypeStruct((HEAD_DIM, DEEP), jnp.bfloat16),
        ],
        compiler_params=pltpu.CompilerParams(vmem_limit_bytes=16 * 2**20),
        name="gather_group",
    )(*messages)


def attend_kernel(stages, groups, known, flips, slots, final, *refs):
    queries, keys, values, refs = refs[:groups], refs[groups:2 * groups], refs[2 * groups:3 * groups], refs[3 * groups:]
    state = ()
    if known:
        state, refs = refs[:3], refs[3:]
    outs, stores = refs[:-2], refs[-2:]
    seq = lax.axis_index("seq")
    classes = range(4) if flips is None else [(seq // 4) ^ flip for flip in flips]
    kept = slots or classes
    stages = [(n, stage) for n in range(len(classes)) for stage in stages]

    units = [[((n, g), keys_of, at) for g, key_groups in stage for keys_of in key_groups
              for at in range(0, DEEP, STEP)] for n, stage in stages]
    ready = {}
    tops = {}
    sums = {}

    def score(slot, index, unit):
        block, keys_of, at = unit
        if block not in ready:
            scaled = queries[block[1]][classes[block[0]]].astype(jnp.float32) * LOG2_SCALE
            high = scaled.astype(jnp.bfloat16)
            low = (scaled - high.astype(jnp.float32)).astype(jnp.bfloat16)
            ready[block] = jnp.concatenate([high, low], axis=1)
        k = keys[keys_of][at:at + STEP, :]
        scores = lax.dot_general(jnp.concatenate([k, k], axis=1), ready[block], (((1,), (1,)), ((), ())),
                                 preferred_element_type=jnp.float32)
        stores[slot][index * STEP:(index + 1) * STEP, :] = scores
        own = jnp.max(scores.reshape(STEP // 8, 8, WIDE), axis=0)
        tops[block] = jnp.maximum(tops[block], own) if block in tops else own

    def weigh(slot, index, unit):
        block, keys_of, at = unit
        weights = jnp.exp2(stores[slot][index * STEP:(index + 1) * STEP, :] - tops[block])
        part = jnp.sum(weights.reshape(STEP // 8, 8, WIDE), axis=0)
        out = jnp.dot(values[keys_of][:, at:at + STEP], weights.astype(jnp.bfloat16),
                      preferred_element_type=jnp.float32)
        total, acc = sums.get(block, (None, None))
        sums[block] = (part, out) if total is None else (total + part, acc + out)

    for stage in range(len(stages) + 1):
        scoring = units[stage] if stage < len(stages) else []
        weighing = units[stage - 1] if stage > 0 else []
        steps = max(len(scoring), len(weighing))
        for i in range(steps):
            for n in range(i * len(scoring) // steps, (i + 1) * len(scoring) // steps):
                score(stage % 2, n, scoring[n])
            for n in range(i * len(weighing) // steps, (i + 1) * len(weighing) // steps):
                weigh((stage - 1) % 2, n, weighing[n])
        for n, g in sorted({unit[0] for unit in weighing}):
            total, acc = sums[n, g]
            if not final:
                outs[0][n, :, g * WIDE:(g + 1) * WIDE] = acc
                outs[1][n, :, g * WIDE:(g + 1) * WIDE] = total
                outs[2][n, :, g * WIDE:(g + 1) * WIDE] = jnp.broadcast_to(tops[n, g], (8, WIDE))
            else:
                done = (acc / jnp.sum(total, axis=0, keepdims=True)).T.astype(jnp.bfloat16)
                for i in range(GROUP):
                    dx, dz = ROTATIONS[GROUP * g + i]
                    source = ((seq // 8) ^ dx) * 8 + (seq % 8 + 8 - dz) % 8
                    outs[0][pl.ds(pl.multiple_of(source * LOC, LOC), LOC), :] = done[i * LOC:(i + 1) * LOC, :]
        for n, g in sorted({unit[0] for unit in scoring}):
            top = jnp.max(tops[n, g], axis=0, keepdims=True)
            if g < known:
                at = slice(g * WIDE, (g + 1) * WIDE)
                old = state[2][kept[n], 0:1, at]
                top = jnp.maximum(top, old)
                fade = jnp.exp2(old - top)
                sums[n, g] = (state[1][kept[n], :, at] * fade, state[0][kept[n], :, at] * fade)
            tops[n, g] = top


def attend(stages, groups, known=0, state=(), flips=None, slots=None, final=False):
    count = len(groups)
    scratch = max(sum(len(key_groups) for _, key_groups in stage) for stage in stages) * DEEP
    classes = 4 if flips is None else len(flips)
    if final:
        out_shape = [jax.ShapeDtypeStruct((SEQ * LOC, HEAD_DIM), jnp.bfloat16)]
    else:
        out_shape = [jax.ShapeDtypeStruct((classes, rows, count * WIDE), jnp.float32) for rows in (HEAD_DIM, 8, 8)]
    work = classes * sum(len(key_groups) for stage in stages for _, key_groups in stage) * WIDE * DEEP
    return pl.pallas_call(
        lambda *refs: attend_kernel(stages, count, known, flips, slots, final, *refs),
        in_specs=[vmem()] * (3 * count + len(state)),
        out_specs=[vmem()] * len(out_shape),
        out_shape=out_shape,
        scratch_shapes=[pltpu.VMEM((scratch, WIDE), jnp.float32)] * 2,
        cost_estimate=pl.CostEstimate(flops=4 * work * HEAD_DIM, transcendentals=work,
                                      bytes_accessed=6 * count * DEEP * HEAD_DIM),
        compiler_params=pltpu.CompilerParams(vmem_limit_bytes=16 * 2**20),
        name="attend",
    )(*[g[0] for g in groups], *[g[1] for g in groups], *[g[2] for g in groups], *state)


def last_head_kernel(*refs):
    blocks, out_ref = refs[:4], refs[4]
    core, seq = lax.axis_index("dp") % 2, lax.axis_index("seq")
    wanted = jnp.where(idle_place(core, seq % 4) == 3, 2, 3)
    row = lax.broadcasted_iota(jnp.int32, (SPLIT, HEAD_DIM), 0)
    col = lax.broadcasted_iota(jnp.int32, (SPLIT, HEAD_DIM), 1)
    picks = [jnp.where((col == row + HEAD_DIM - SPLIT) & ((seq // 4) ^ flip == wanted), 1.0, 0.0).astype(jnp.bfloat16)
             for flip in XORS]
    block = jnp.concatenate([ref[...] for ref in blocks], axis=1)
    out_ref[...] = lax.dot_general(jnp.concatenate(picks, axis=1), block, (((1,), (1,)), ((), ())),
                                   preferred_element_type=jnp.float32).astype(jnp.bfloat16)


def last_head(blocks):
    return pl.pallas_call(
        last_head_kernel,
        in_specs=[vmem()] * 4,
        out_specs=vmem(),
        out_shape=jax.ShapeDtypeStruct((SPLIT, SEQ * LOC), jnp.bfloat16),
        compiler_params=pltpu.CompilerParams(vmem_limit_bytes=8 * 2**20),
        name="last_head",
    )(*blocks)


def own_rows(blocks, rows):
    core, seq = lax.axis_index("dp") % 2, lax.axis_index("seq")
    place, chunk = seq // 4, seq % 4
    row = lax.broadcasted_iota(jnp.int32, (rows, HEAD_DIM), 0)
    col = lax.broadcasted_iota(jnp.int32, (rows, HEAD_DIM), 1)
    picks = []
    for flip in XORS:
        other = place ^ flip
        shift = head_at(core, other * 4 + chunk) * HEAD_DIM - chunk * OUT_COLS
        shift = jnp.where(other == idle_place(core, chunk), FAR, shift)
        picks.append(jnp.where(row == col + shift, 1.0, 0.0).astype(jnp.bfloat16))
    block = jnp.concatenate(blocks, axis=1)
    return lax.dot_general(jnp.concatenate(picks, axis=1), block, (((1,), (1,)), ((), ())),
                           preferred_element_type=jnp.float32)


def merge_kernel(*refs):
    blocks, out_ref = refs[:4], refs[4]
    rows = out_ref.shape[1]
    at = pl.ds(pl.multiple_of(pl.program_id(0) * rows, rows), rows)
    out_ref[...] = own_rows([ref[at, :] for ref in blocks], OUT_COLS).astype(jnp.bfloat16)


def merge(blocks):
    rows = SEQ * LOC
    return pl.pallas_call(
        merge_kernel,
        grid=(2,),
        in_specs=[vmem()] * 4,
        out_specs=pl.BlockSpec((OUT_COLS, rows // 2), lambda i: (0, i)),
        out_shape=jax.ShapeDtypeStruct((OUT_COLS, rows), jnp.bfloat16),
        compiler_params=pltpu.CompilerParams(vmem_limit_bytes=16 * 2**20),
        name="merge",
    )(*blocks)


def finish_kernel(*refs):
    blocks, split, out_ref = refs[:4], refs[4], refs[6]
    chunk = lax.axis_index("seq") % 4
    row = lax.broadcasted_iota(jnp.int32, (HEAD_DIM, SPLIT), 0)
    col = lax.broadcasted_iota(jnp.int32, (HEAD_DIM, SPLIT), 1)
    taken = jnp.where((row == col + 32 - 32 * chunk) & (chunk > 0), 1.0, 0.0).astype(jnp.bfloat16)
    out = own_rows([ref[...] for ref in blocks], HEAD_DIM) + jnp.dot(taken, split[...],
                                                                     preferred_element_type=jnp.float32)
    out_ref[...] = out.astype(jnp.bfloat16)


def finish(blocks, split, merged):
    rows = SEQ * LOC
    return pl.pallas_call(
        finish_kernel,
        grid=(1,),
        in_specs=[vmem()] * 5 + [pl.BlockSpec(memory_space=pltpu.HBM)],
        out_specs=pl.BlockSpec((HEAD_DIM, rows), lambda i: (0, 0)),
        out_shape=jax.ShapeDtypeStruct((OUT_COLS, rows), jnp.bfloat16),
        input_output_aliases={5: 0},
        compiler_params=pltpu.CompilerParams(vmem_limit_bytes=16 * 2**20),
        name="finish",
    )(*blocks, split, merged).T


def exchange_and_attend(queries, key_rows, value_rows):
    axes = ("dp", "seq")
    messages = pack(queries, key_rows, value_rows)
    got = [messages[0]]
    for r in range(1, 16):
        near = min(ROTATIONS[r][1], 8 - ROTATIONS[r][1]) <= NEAR
        perm = pairs(lambda s: turn(s, ROTATIONS[r]), lambda core, s, t: near or not idle(core, t), FILL_SPREAD)
        got.append(lax.ppermute(messages[r], axes, perm))
    groups = [gather_group(got[i:i + GROUP]) for i in range(0, 16, GROUP)]

    first = attend([[(0, (0, 1))], [(1, (0, 1))]], groups[:2])
    second = attend([[(2, (0, 1, 2))], [(0, (2,)), (1, (2,))]], groups[:3], 2, first, XORS[:2])
    blocks = []
    for n, flip in enumerate(XORS):
        if n < 2:
            stages = [[(3, (0, 1, 2, 3))], [(0, (3,)), (1, (3,)), (2, (3,))]]
            out = attend(stages, groups, 3, second, (flip,), (n,), True)[0]
        else:
            stages = [[(3, (0, 1, 2, 3))], [(2, (0, 1, 2, 3))], [(0, (2, 3)), (1, (2, 3))]]
            out = attend(stages, groups, 2, first, (flip,), None, True)[0]
        if flip:
            perm = pairs(lambda s: ((s // 4) ^ flip) * 4 + s % 4, lambda core, s, t: not idle(core, s), FILL_RETURN)
            out = lax.ppermute(out, axes, perm)
        blocks.append(out)
    split = lax.ppermute(last_head(blocks), axes, pairs(lambda s: turn(s, (0, 1)), lambda core, s, t: True))
    merged = merge(blocks)
    return finish(blocks, split, merged)


def solution(mesh):
    placed = (P(("dp", "seq"), None), P(("dp", "seq"), None), P(("dp", "seq"), None))
    return jax.shard_map(exchange_and_attend, mesh=mesh, in_specs=placed, out_specs=P("dp", "seq"), check_vma=False)
```

time: 131 us -> 128 us (0.977); the launches traced: 128 us -> 127 us
  waiting for transfers between devices: 28.6 us -> 31.6 us
  Pallas kernels: 31.6 us -> 29.4 us
  starting transfers between devices: 64.3 us -> 62.6 us
    ppermute x1, waiting for transfers between devices: 10.7 us -> 5.22 us  [exchange_and_attend(): lax.ppermute(last_head(blocks), axes, pairs(lambda s: turn(s, (0, 1)), la...]
    ppermute x15, waiting for transfers between devices: 5.32 us -> 9.88 us  [exchange_and_attend(): got.append(lax.ppermute(messages[r], axes, perm))]
    ppermute x3, waiting for transfers between devices: 12.6 us -> 16.5 us  [exchange_and_attend(): out = lax.ppermute(out, axes, perm)]
    pallas_call x8 -> x9, Pallas kernels: 31.1 us -> 28.4 us  [the longest x6 23.6 us: attend(): pl.pallas_call(lambda *refs: attend_kernel(stages, count, known, flips, s...]
    ppermute x15, starting transfers between devices: 55.2 us -> 53.2 us  [exchange_and_attend(): got.append(lax.ppermute(messages[r], axes, perm))]
  transfers between devices with their start and end apart: 19 -> 19, of which waited for: 5 -> 6; matrix products, arithmetic and copies ran while one was open for 0% -> 0% of each run, Pallas kernels for 15% -> 13%
where the time goes in v4:
time: 128 us; the launch traced here: 127 us
  starting transfers between devices  62.6 us (49%)
  waiting for transfers between devices  31.6 us (25%)
  Pallas kernels  29.4 us (23%)
  local copies, waits for them, and re-layouts  3.47 us (3%)
    ppermute x15, starting transfers between devices, exchange_and_attend(): got.append(lax.ppermute(messages[r], axes, perm))  53.2 us
    pallas_call x6, Pallas kernels, attend(): pl.pallas_call(lambda *refs: attend_kernel(stages, count, known, flips, s...  23.6 us
    ppermute x3, waiting for transfers between devices, exchange_and_attend(): out = lax.ppermute(out, axes, perm)  16.5 us
    ppermute x15, waiting for transfers between devices, exchange_and_attend(): got.append(lax.ppermute(messages[r], axes, perm))  9.88 us
    ppermute x3, starting transfers between devices, exchange_and_attend(): out = lax.ppermute(out, axes, perm)  9.33 us
    ppermute x1, waiting for transfers between devices, exchange_and_attend(): lax.ppermute(last_head(blocks), axes, pairs(lambda s: turn(s, (0, 1)), la...  5.22 us
    unnamed x6, local copies, waits for them, and re-layouts  3.47 us
  transfers between devices with their start and end apart: 19, of which 6 were waited for; matrix products, arithmetic and copies ran while one was open for 0% of the time, Pallas kernels for 13%

profile of v4, /device:TPU:16, one launch (start us, length us, event | category | flops | bytes accessed | tf_op | source)
XLA Modules:
  0.0 127.2 jit_solution(15685283198431854574)
XLA Ops:
  0.0 1.2 copy-done
  1.2 1.2 copy-done.1
  2.3 1.2 copy-done.2
  3.5 1.9 %pack.1 = (bf16[768,128]{1,0:T(8,128)(2,1)S(1)}, bf16[768,128]{1,0:T(8,128)(2,1)S(1)}, bf16[768,128]{1,0:T(8,128)(2,1)S(1)}, bf16[768,128]{1,0:T(8,128)(2,1)S(1)...) custom-call(bf16[256,1664]{1,0:T(8,128)(2,1)S(1)} %copy-done, ...), custom_call_target="tpu_custom_call" | custom-call | tf_op jit(solution)/shard_map/pack/pallas_call | solution.py:118
  5.4 3.1 %collective-permute-start = (bf16[768,128]{1,0:T(8,128)(2,1)S(1)}, bf16[768,128]{1,0:T(8,128)(2,1)S(1)}, u32[]{:S(2)}, u32[]{:S(2)}) collective-permute-start(bf16[768,128]{1,0:T(8,128)(2,1)S(1)} %get-tuple-element.40), channel_id=1, source_target_pairs={{0,8},{1,9},{2,10},{3,11},{4,12},{5,13},{6,14},{7,15},{8,0},{9,1},... | collective-permute-start | bytes 589832 | tf_op jit(solution)/shard_map/ppermute | solution.py:339
  8.5 1.9 %collective-permute-start.1 = (bf16[768,128]{1,0:T(8,128)(2,1)S(1)}, bf16[768,128]{1,0:T(8,128)(2,1)S(1)}, u32[]{:S(2)}, u32[]{:S(2)}) collective-permute-start(bf16[768,128]{1,0:T(8,128)(2,1)S(1)} %get-tuple-element.41), channel_id=1, source_target_pairs={{0,1},{1,2},{2,3},{3,4},{4,5},{5,6},{6,7},{7,0},{8,9},{9,10},{10,1... | collective-permute-start | bytes 589832 | tf_op jit(solution)/shard_map/ppermute | solution.py:339
  10.4 3.9 %collective-permute-start.2 = (bf16[768,128]{1,0:T(8,128)(2,1)S(1)}, bf16[768,128]{1,0:T(8,128)(2,1)S(1)}, u32[]{:S(2)}, u32[]{:S(2)}) collective-permute-start(bf16[768,128]{1,0:T(8,128)(2,1)S(1)} %get-tuple-element.42), channel_id=1, source_target_pairs={{0,7},{1,0},{2,1},{3,2},{4,3},{5,4},{6,5},{7,6},{8,15},{9,8},{10,9... | collective-permute-start | bytes 589832 | tf_op jit(solution)/shard_map/ppermute | solution.py:339
  14.4 5.6 %collective-permute-start.4 = (bf16[768,128]{1,0:T(8,128)(2,1)S(1)}, bf16[768,128]{1,0:T(8,128)(2,1)S(1)}, u32[]{:S(2)}, u32[]{:S(2)}) collective-permute-start(bf16[768,128]{1,0:T(8,128)(2,1)S(1)} %get-tuple-element.45), channel_id=1, source_target_pairs={{0,15},{1,8},{2,9},{3,10},{4,11},{5,12},{6,13},{7,14},{8,7},{9,0},... | collective-permute-start | bytes 589832 | tf_op jit(solution)/shard_map/ppermute | solution.py:339
  20.1 4.0 %collective-permute-start.6 = (bf16[768,128]{1,0:T(8,128)(2,1)S(1)}, bf16[768,128]{1,0:T(8,128)(2,1)S(1)}, u32[]{:S(2)}, u32[]{:S(2)}) collective-permute-start(bf16[768,128]{1,0:T(8,128)(2,1)S(1)} %get-tuple-element.47), channel_id=1, source_target_pairs={{0,6},{1,7},{2,0},{3,1},{4,2},{5,3},{6,4},{7,5},{8,14},{9,15},{10,... | collective-permute-start | bytes 589832 | tf_op jit(solution)/shard_map/ppermute | solution.py:339
  24.2 1.0 collective-permute-start.7
  25.2 5.3 %collective-permute-done.3.refs_0_ = bf16[768,128]{1,0:T(8,128)(2,1)S(1)} collective-permute-done((bf16[768,128]{1,0:T(8,128)(2,1)S(1)}, bf16[768,128]{1,0:T(8,128)(2,1)S(1)}, u32[]{:S(2)}, u32[]{:S(2)}) %collective-permute-start.3) | collective-permute-done | bytes 196640 | tf_op jit(solution)/shard_map/ppermute | solution.py:339
  30.5 0.8 collective-permute-start.8
  31.3 3.1 %collective-permute-start.9 = (bf16[768,128]{1,0:T(8,128)(2,1)S(1)}, bf16[768,128]{1,0:T(8,128)(2,1)S(1)}, u32[]{:S(2)}, u32[]{:S(2)}) collective-permute-start(bf16[768,128]{1,0:T(8,128)(2,1)S(1)} %get-tuple-element.51), channel_id=1, source_target_pairs={{0,3},{1,4},{2,5},{4,7},{5,0},{7,2},{8,11},{9,12},{10,13},{11,14},... | collective-permute-start | bytes 589832 | tf_op jit(solution)/shard_map/ppermute | solution.py:339
  34.6 7.7 %collective-permute-start.10 = (bf16[768,128]{1,0:T(8,128)(2,1)S(1)}, bf16[768,128]{1,0:T(8,128)(2,1)S(1)}, u32[]{:S(2)}, u32[]{:S(2)}) collective-permute-start(bf16[768,128]{1,0:T(8,128)(2,1)S(1)} %get-tuple-element.52), channel_id=1, source_target_pairs={{0,5},{2,7},{3,0},{5,2},{6,3},{7,4},{8,13},{9,14},{11,8},{12,9},{1... | collective-permute-start | bytes 589832 | tf_op jit(solution)/shard_map/ppermute | solution.py:339
  42.4 8.4 %collective-permute-start.11 = (bf16[768,128]{1,0:T(8,128)(2,1)S(1)}, bf16[768,128]{1,0:T(8,128)(2,1)S(1)}, u32[]{:S(2)}, u32[]{:S(2)}) collective-permute-start(bf16[768,128]{1,0:T(8,128)(2,1)S(1)} %get-tuple-element.54), channel_id=1, source_target_pairs={{0,11},{1,12},{2,13},{3,14},{5,8},{6,9},{7,10},{8,3},{9,4},{10,5},... | collective-permute-start | bytes 589832 | tf_op jit(solution)/shard_map/ppermute | solution.py:339
  50.9 4.0 %collective-permute-start.12 = (bf16[768,128]{1,0:T(8,128)(2,1)S(1)}, bf16[768,128]{1,0:T(8,128)(2,1)S(1)}, u32[]{:S(2)}, u32[]{:S(2)}) collective-permute-start(bf16[768,128]{1,0:T(8,128)(2,1)S(1)} %get-tuple-element.55), channel_id=1, source_target_pairs={{0,13},{1,14},{3,8},{4,9},{5,10},{6,11},{7,12},{8,5},{10,7},{11,0}... | collective-permute-start | bytes 589832 | tf_op jit(solution)/shard_map/ppermute | solution.py:339
  54.9 1.9 %collective-permute-start.13 = (bf16[768,128]{1,0:T(8,128)(2,1)S(1)}, bf16[768,128]{1,0:T(8,128)(2,1)S(1)}, u32[]{:S(2)}, u32[]{:S(2)}) collective-permute-start(bf16[768,128]{1,0:T(8,128)(2,1)S(1)} %get-tuple-element.56), channel_id=1, source_target_pairs={{0,4},{1,5},{3,7},{4,0},{6,2},{7,3},{8,12},{9,13},{10,14},{12,8},{... | collective-permute-start | bytes 589832 | tf_op jit(solution)/shard_map/ppermute | solution.py:339
  56.8 4.4 %collective-permute-done.9.refs_2_ = bf16[768,128]{1,0:T(8,128)(2,1)S(1)} collective-permute-done((bf16[768,128]{1,0:T(8,128)(2,1)S(1)}, bf16[768,128]{1,0:T(8,128)(2,1)S(1)}, u32[]{:S(2)}, u32[]{:S(2)}) %collective-permute-start.9) | collective-permute-done | bytes 196640 | tf_op jit(solution)/shard_map/ppermute | solution.py:339
  61.2 7.6 %collective-permute-start.14 = (bf16[768,128]{1,0:T(8,128)(2,1)S(1)}, bf16[768,128]{1,0:T(8,128)(2,1)S(1)}, u32[]{:S(2)}, u32[]{:S(2)}) collective-permute-start(bf16[768,128]{1,0:T(8,128)(2,1)S(1)} %get-tuple-element.57), channel_id=1, source_target_pairs={{0,12},{1,13},{2,14},{4,8},{5,9},{6,10},{7,11},{8,4},{9,5},{11,7},... | collective-permute-start | bytes 589832 | tf_op jit(solution)/shard_map/ppermute | solution.py:339
  68.8 5.9 %attend.6 = (f32[4,128,512]{2,1,0:T(8,128)S(1)}, f32[4,8,512]{2,1,0:T(8,128)S(1)}, f32[4,8,512]{2,1,0:T(8,128)S(1)}) custom-call(bf16[4,256,128]{2,1,0:T(8,128)(2,1)S(1)} %get-tuple-element.43.refs_0_, bf16[4,256,128]{2,1,0:T(8,128)(2,1)S(1)} %get-tuple-element.48.refs_1_, bf16[1024,128]{1,0:T(8,128)(2,1)S(1)} %get-tuple-element.59.refs_2_.refs_3_.refs_4_, ...), custom_call_target="tpu_custom_call" | custom-call | flops 2147483648 | bytes 1572864 | tf_op jit(solution)/shard_map/attend/pallas_call | solution.py:234
  74.8 3.8 %attend.7 = (f32[2,128,768]{2,1,0:T(8,128)S(1)}, f32[2,8,768]{2,1,0:T(8,128)S(1)}, f32[2,8,768]{2,1,0:T(8,128)S(1)}) custom-call(bf16[4,256,128]{2,1,0:T(8,128)(2,1)S(1)} %get-tuple-element.43.refs_0_, bf16[4,256,128]{2,1,0:T(8,128)(2,1)S(1)} %get-tuple-element.48.refs_1_, bf16[4,256,128]{2,1,0:T(8,128)(2,1)S(1)} %get-tuple-element.53.refs_2_, ...), custom_call_target="tpu_custom_call" | custom-call | flops 1342177280 | bytes 2359296 | tf_op jit(solution)/shard_map/attend/pallas_call | solution.py:234
  78.8 4.5 %attend.10 = bf16[1024,128]{1,0:T(8,128)(2,1)S(1)} custom-call(bf16[4,256,128]{2,1,0:T(8,128)(2,1)S(1)} %get-tuple-element.43.refs_0_, bf16[4,256,128]{2,1,0:T(8,128)(2,1)S(1)} %get-tuple-element.48.refs_1_, bf16[4,256,128]{2,1,0:T(8,128)(2,1)S(1)} %get-tuple-element.53.refs_2_, bf16[4,256,128]{2,1,0:T(8,128)(2,1)S(1)} %get-tuple-element.58.refs_3_, ...), custom_call_target="tpu_custom_call" | custom-call | flops 1610612736 | bytes 3145728 | tf_op jit(solution)/shard_map/attend/pallas_call | solution.py:234
  83.4 2.5 %attend.9 = bf16[1024,128]{1,0:T(8,128)(2,1)S(1)} custom-call(bf16[4,256,128]{2,1,0:T(8,128)(2,1)S(1)} %get-tuple-element.43.refs_0_, bf16[4,256,128]{2,1,0:T(8,128)(2,1)S(1)} %get-tuple-element.48.refs_1_, bf16[4,256,128]{2,1,0:T(8,128)(2,1)S(1)} %get-tuple-element.53.refs_2_, bf16[4,256,128]{2,1,0:T(8,128)(2,1)S(1)} %get-tuple-element.58.refs_3_, ...), custom_call_target="tpu_custom_call" | custom-call | flops 939524096 | bytes 3145728 | tf_op jit(solution)/shard_map/attend/pallas_call | solution.py:234
  85.9 2.6 %attend.8 = bf16[1024,128]{1,0:T(8,128)(2,1)S(1)} custom-call(bf16[4,256,128]{2,1,0:T(8,128)(2,1)S(1)} %get-tuple-element.43.refs_0_, bf16[4,256,128]{2,1,0:T(8,128)(2,1)S(1)} %get-tuple-element.48.refs_1_, bf16[4,256,128]{2,1,0:T(8,128)(2,1)S(1)} %get-tuple-element.53.refs_2_, bf16[4,256,128]{2,1,0:T(8,128)(2,1)S(1)} %get-tuple-element.58.refs_3_, ...), custom_call_target="tpu_custom_call" | custom-call | flops 939524096 | bytes 3145728 | tf_op jit(solution)/shard_map/attend/pallas_call | solution.py:234
  88.5 5.9 %collective-permute-start.15 = (bf16[1024,128]{1,0:T(8,128)(2,1)S(1)}, bf16[1024,128]{1,0:T(8,128)(2,1)S(1)}, u32[]{:S(2)}, u32[]{:S(2)}) collective-permute-start(bf16[1024,128]{1,0:T(8,128)(2,1)S(1)} %attend.8), channel_id=1, source_target_pairs={{0,12},{2,14},{3,15},{4,8},{5,9},{7,11},{8,4},{9,5},{10,6},{11,7},... | collective-permute-start | bytes 786440 | tf_op jit(solution)/shard_map/ppermute | solution.py:354
  94.4 3.4 %collective-permute-start.16 = (bf16[1024,128]{1,0:T(8,128)(2,1)S(1)}, bf16[1024,128]{1,0:T(8,128)(2,1)S(1)}, u32[]{:S(2)}, u32[]{:S(2)}) collective-permute-start(bf16[1024,128]{1,0:T(8,128)(2,1)S(1)} %attend.9), channel_id=1, source_target_pairs={{0,4},{2,6},{3,7},{4,0},{5,1},{7,3},{8,12},{9,13},{10,14},{11,15},... | collective-permute-start | bytes 786440 | tf_op jit(solution)/shard_map/ppermute | solution.py:354
  97.8 4.3 %attend.11.refs_3_ = bf16[1024,128]{1,0:T(8,128)(2,1)S(1)} custom-call(bf16[4,256,128]{2,1,0:T(8,128)(2,1)S(1)} %get-tuple-element.43.refs_0_, bf16[4,256,128]{2,1,0:T(8,128)(2,1)S(1)} %get-tuple-element.48.refs_1_, bf16[4,256,128]{2,1,0:T(8,128)(2,1)S(1)} %get-tuple-element.53.refs_2_, bf16[4,256,128]{2,1,0:T(8,128)(2,1)S(1)} %get-tuple-element.58.refs_3_, ...), custom_call_target="tpu_custom_call" | custom-call | flops 1610612736 | bytes 3145728 | tf_op jit(solution)/shard_map/attend/pallas_call | solution.py:234
  102.1 4.4 %collective-permute-done.15.refs_0_ = bf16[1024,128]{1,0:T(8,128)(2,1)S(1)} collective-permute-done((bf16[1024,128]{1,0:T(8,128)(2,1)S(1)}, bf16[1024,128]{1,0:T(8,128)(2,1)S(1)}, u32[]{:S(2)}, u32[]{:S(2)}) %collective-permute-start.15) | collective-permute-done | bytes 262176 | tf_op jit(solution)/shard_map/ppermute | solution.py:354
  106.5 12.1 %collective-permute-done.16.refs_1_ = bf16[1024,128]{1,0:T(8,128)(2,1)S(1)} collective-permute-done((bf16[1024,128]{1,0:T(8,128)(2,1)S(1)}, bf16[1024,128]{1,0:T(8,128)(2,1)S(1)}, u32[]{:S(2)}, u32[]{:S(2)}) %collective-permute-start.16) | collective-permute-done | bytes 262176 | tf_op jit(solution)/shard_map/ppermute | solution.py:354
  119.1 1.6 %merge.1.refs_5_ = bf16[416,1024]{1,0:T(8,128)(2,1)} custom-call(bf16[1024,128]{1,0:T(8,128)(2,1)S(1)} %collective-permute-done.15.refs_0_, bf16[1024,128]{1,0:T(8,128)(2,1)S(1)} %collective-permute-done.16.refs_1_, bf16[1024,128]{1,0:T(8,128)(2,1)S(1)} %collective-permute-done.17.refs_2_, bf16[1024,128]{1,0:T(8,128)(2,1)S(1)} %attend.11.refs_3_), custom_call_target="tpu_custom_call" | custom-call | tf_op jit(solution)/shard_map/merge/pallas_call | solution.py:296
  120.7 5.2 %collective-permute-done.18.refs_4_ = bf16[96,1024]{1,0:T(8,128)(2,1)S(1)} collective-permute-done((bf16[96,1024]{1,0:T(8,128)(2,1)S(1)}, bf16[96,1024]{1,0:T(8,128)(2,1)S(1)}, u32[]{:S(2)}, u32[]{:S(2)}) %collective-permute-start.18) | collective-permute-done | bytes 196640 | tf_op jit(solution)/shard_map/ppermute | solution.py:356
  125.9 1.2 finish.1
  (26 shorter events, 1.2 us)
Async XLA Ops:
  0.0 1.2 copy-start
  1.2 1.2 copy-start.1
  2.3 1.2 copy-start.2
  5.4 14.6 %collective-permute-start = (bf16[768,128]{1,0:T(8,128)(2,1)S(1)}, bf16[768,128]{1,0:T(8,128)(2,1)S(1)}, u32[]{:S(2)}, u32[]{:S(2)}) collective-permute-start(bf16[768,128]{1,0:T(8,128)(2,1)S(1)} %get-tuple-element.40), channel_id=1, source_target_pairs={{0,8},{1,9},{2,10},{3,11},{4,12},{5,13},{6,14},{7,15},{8,0},{9,1},... | collective-permute-start | bytes 589832 | tf_op jit(solution)/shard_map/ppermute | solution.py:339
  8.5 11.6 %collective-permute-start.1 = (bf16[768,128]{1,0:T(8,128)(2,1)S(1)}, bf16[768,128]{1,0:T(8,128)(2,1)S(1)}, u32[]{:S(2)}, u32[]{:S(2)}) collective-permute-start(bf16[768,128]{1,0:T(8,128)(2,1)S(1)} %get-tuple-element.41), channel_id=1, source_target_pairs={{0,1},{1,2},{2,3},{3,4},{4,5},{5,6},{6,7},{7,0},{8,9},{9,10},{10,1... | collective-permute-start | bytes 589832 | tf_op jit(solution)/shard_map/ppermute | solution.py:339
  10.4 13.7 %collective-permute-start.2 = (bf16[768,128]{1,0:T(8,128)(2,1)S(1)}, bf16[768,128]{1,0:T(8,128)(2,1)S(1)}, u32[]{:S(2)}, u32[]{:S(2)}) collective-permute-start(bf16[768,128]{1,0:T(8,128)(2,1)S(1)} %get-tuple-element.42), channel_id=1, source_target_pairs={{0,7},{1,0},{2,1},{3,2},{4,3},{5,4},{6,5},{7,6},{8,15},{9,8},{10,9... | collective-permute-start | bytes 589832 | tf_op jit(solution)/shard_map/ppermute | solution.py:339
  14.4 16.1 %collective-permute-start.3 = (bf16[768,128]{1,0:T(8,128)(2,1)S(1)}, bf16[768,128]{1,0:T(8,128)(2,1)S(1)}, u32[]{:S(2)}, u32[]{:S(2)}) collective-permute-start(bf16[768,128]{1,0:T(8,128)(2,1)S(1)} %get-tuple-element.44), channel_id=1, source_target_pairs={{0,9},{1,10},{2,11},{3,12},{4,13},{5,14},{6,15},{7,8},{8,1},{9,2},... | collective-permute-start | bytes 589832 | tf_op jit(solution)/shard_map/ppermute | solution.py:339
  14.4 17.0 %collective-permute-start.4 = (bf16[768,128]{1,0:T(8,128)(2,1)S(1)}, bf16[768,128]{1,0:T(8,128)(2,1)S(1)}, u32[]{:S(2)}, u32[]{:S(2)}) collective-permute-start(bf16[768,128]{1,0:T(8,128)(2,1)S(1)} %get-tuple-element.45), channel_id=1, source_target_pairs={{0,15},{1,8},{2,9},{3,10},{4,11},{5,12},{6,13},{7,14},{8,7},{9,0},... | collective-permute-start | bytes 589832 | tf_op jit(solution)/shard_map/ppermute | solution.py:339
  20.0 14.6 %collective-permute-start.5 = (bf16[768,128]{1,0:T(8,128)(2,1)S(1)}, bf16[768,128]{1,0:T(8,128)(2,1)S(1)}, u32[]{:S(2)}, u32[]{:S(2)}) collective-permute-start(bf16[768,128]{1,0:T(8,128)(2,1)S(1)} %get-tuple-element.46), channel_id=1, source_target_pairs={{0,2},{1,3},{2,4},{3,5},{4,6},{5,7},{6,0},{7,1},{8,10},{9,11},{10,... | collective-permute-start | bytes 589832 | tf_op jit(solution)/shard_map/ppermute | solution.py:339
  20.1 22.2 %collective-permute-start.6 = (bf16[768,128]{1,0:T(8,128)(2,1)S(1)}, bf16[768,128]{1,0:T(8,128)(2,1)S(1)}, u32[]{:S(2)}, u32[]{:S(2)}) collective-permute-start(bf16[768,128]{1,0:T(8,128)(2,1)S(1)} %get-tuple-element.47), channel_id=1, source_target_pairs={{0,6},{1,7},{2,0},{3,1},{4,2},{5,3},{6,4},{7,5},{8,14},{9,15},{10,... | collective-permute-start | bytes 589832 | tf_op jit(solution)/shard_map/ppermute | solution.py:339
  24.2 26.7 %collective-permute-start.7 = (bf16[768,128]{1,0:T(8,128)(2,1)S(1)}, bf16[768,128]{1,0:T(8,128)(2,1)S(1)}, u32[]{:S(2)}, u32[]{:S(2)}) collective-permute-start(bf16[768,128]{1,0:T(8,128)(2,1)S(1)} %get-tuple-element.49), channel_id=1, source_target_pairs={{0,10},{1,11},{2,12},{3,13},{4,14},{5,15},{6,8},{7,9},{8,2},{9,3},... | collective-permute-start | bytes 589832 | tf_op jit(solution)/shard_map/ppermute | solution.py:339
  30.5 24.4 %collective-permute-start.8 = (bf16[768,128]{1,0:T(8,128)(2,1)S(1)}, bf16[768,128]{1,0:T(8,128)(2,1)S(1)}, u32[]{:S(2)}, u32[]{:S(2)}) collective-permute-start(bf16[768,128]{1,0:T(8,128)(2,1)S(1)} %get-tuple-element.50), channel_id=1, source_target_pairs={{0,14},{1,15},{2,8},{3,9},{4,10},{5,11},{6,12},{7,13},{8,6},{9,7},... | collective-permute-start | bytes 589832 | tf_op jit(solution)/shard_map/ppermute | solution.py:339
  31.3 29.9 %collective-permute-start.9 = (bf16[768,128]{1,0:T(8,128)(2,1)S(1)}, bf16[768,128]{1,0:T(8,128)(2,1)S(1)}, u32[]{:S(2)}, u32[]{:S(2)}) collective-permute-start(bf16[768,128]{1,0:T(8,128)(2,1)S(1)} %get-tuple-element.51), channel_id=1, source_target_pairs={{0,3},{1,4},{2,5},{4,7},{5,0},{7,2},{8,11},{9,12},{10,13},{11,14},... | collective-permute-start | bytes 589832 | tf_op jit(solution)/shard_map/ppermute | solution.py:339
  34.6 40.1 %collective-permute-start.10 = (bf16[768,128]{1,0:T(8,128)(2,1)S(1)}, bf16[768,128]{1,0:T(8,128)(2,1)S(1)}, u32[]{:S(2)}, u32[]{:S(2)}) collective-permute-start(bf16[768,128]{1,0:T(8,128)(2,1)S(1)} %get-tuple-element.52), channel_id=1, source_target_pairs={{0,5},{2,7},{3,0},{5,2},{6,3},{7,4},{8,13},{9,14},{11,8},{12,9},{1... | collective-permute-start | bytes 589832 | tf_op jit(solution)/shard_map/ppermute | solution.py:339
  42.4 36.3 %collective-permute-start.11 = (bf16[768,128]{1,0:T(8,128)(2,1)S(1)}, bf16[768,128]{1,0:T(8,128)(2,1)S(1)}, u32[]{:S(2)}, u32[]{:S(2)}) collective-permute-start(bf16[768,128]{1,0:T(8,128)(2,1)S(1)} %get-tuple-element.54), channel_id=1, source_target_pairs={{0,11},{1,12},{2,13},{3,14},{5,8},{6,9},{7,10},{8,3},{9,4},{10,5},... | collective-permute-start | bytes 589832 | tf_op jit(solution)/shard_map/ppermute | solution.py:339
  50.9 27.8 %collective-permute-start.12 = (bf16[768,128]{1,0:T(8,128)(2,1)S(1)}, bf16[768,128]{1,0:T(8,128)(2,1)S(1)}, u32[]{:S(2)}, u32[]{:S(2)}) collective-permute-start(bf16[768,128]{1,0:T(8,128)(2,1)S(1)} %get-tuple-element.55), channel_id=1, source_target_pairs={{0,13},{1,14},{3,8},{4,9},{5,10},{6,11},{7,12},{8,5},{10,7},{11,0}... | collective-permute-start | bytes 589832 | tf_op jit(solution)/shard_map/ppermute | solution.py:339
  54.9 23.8 %collective-permute-start.13 = (bf16[768,128]{1,0:T(8,128)(2,1)S(1)}, bf16[768,128]{1,0:T(8,128)(2,1)S(1)}, u32[]{:S(2)}, u32[]{:S(2)}) collective-permute-start(bf16[768,128]{1,0:T(8,128)(2,1)S(1)} %get-tuple-element.56), channel_id=1, source_target_pairs={{0,4},{1,5},{3,7},{4,0},{6,2},{7,3},{8,12},{9,13},{10,14},{12,8},{... | collective-permute-start | bytes 589832 | tf_op jit(solution)/shard_map/ppermute | solution.py:339
  61.2 17.5 %collective-permute-start.14 = (bf16[768,128]{1,0:T(8,128)(2,1)S(1)}, bf16[768,128]{1,0:T(8,128)(2,1)S(1)}, u32[]{:S(2)}, u32[]{:S(2)}) collective-permute-start(bf16[768,128]{1,0:T(8,128)(2,1)S(1)} %get-tuple-element.57), channel_id=1, source_target_pairs={{0,12},{1,13},{2,14},{4,8},{5,9},{6,10},{7,11},{8,4},{9,5},{11,7},... | collective-permute-start | bytes 589832 | tf_op jit(solution)/shard_map/ppermute | solution.py:339
  88.5 18.0 %collective-permute-start.15 = (bf16[1024,128]{1,0:T(8,128)(2,1)S(1)}, bf16[1024,128]{1,0:T(8,128)(2,1)S(1)}, u32[]{:S(2)}, u32[]{:S(2)}) collective-permute-start(bf16[1024,128]{1,0:T(8,128)(2,1)S(1)} %attend.8), channel_id=1, source_target_pairs={{0,12},{2,14},{3,15},{4,8},{5,9},{7,11},{8,4},{9,5},{10,6},{11,7},... | collective-permute-start | bytes 786440 | tf_op jit(solution)/shard_map/ppermute | solution.py:354
  94.4 24.1 %collective-permute-start.16 = (bf16[1024,128]{1,0:T(8,128)(2,1)S(1)}, bf16[1024,128]{1,0:T(8,128)(2,1)S(1)}, u32[]{:S(2)}, u32[]{:S(2)}) collective-permute-start(bf16[1024,128]{1,0:T(8,128)(2,1)S(1)} %attend.9), channel_id=1, source_target_pairs={{0,4},{2,6},{3,7},{4,0},{5,1},{7,3},{8,12},{9,13},{10,14},{11,15},... | collective-permute-start | bytes 786440 | tf_op jit(solution)/shard_map/ppermute | solution.py:354
  97.8 20.7 %collective-permute-start.17 = (bf16[1024,128]{1,0:T(8,128)(2,1)S(1)}, bf16[1024,128]{1,0:T(8,128)(2,1)S(1)}, u32[]{:S(2)}, u32[]{:S(2)}) collective-permute-start(bf16[1024,128]{1,0:T(8,128)(2,1)S(1)} %attend.10), channel_id=1, source_target_pairs={{0,8},{2,10},{3,11},{4,12},{5,13},{7,15},{8,0},{9,1},{10,2},{11,3}... | collective-permute-start | bytes 786440 | tf_op jit(solution)/shard_map/ppermute | solution.py:354
  119.0 7.0 %collective-permute-start.18 = (bf16[96,1024]{1,0:T(8,128)(2,1)S(1)}, bf16[96,1024]{1,0:T(8,128)(2,1)S(1)}, u32[]{:S(2)}, u32[]{:S(2)}) collective-permute-start(bf16[96,1024]{1,0:T(8,128)(2,1)S(1)} %last_head.1), channel_id=1, source_target_pairs={{0,1},{1,2},{2,3},{3,4},{4,5},{5,6},{6,7},{7,0},{8,9},{9,10},{10,1... | collective-permute-start | bytes 589832 | tf_op jit(solution)/shard_map/ppermute | solution.py:356

commit v5 on v4

--- a/solution.py
+++ b/solution.py
@@ -26,11 +26,13 @@
 
 IDLE = ((9, 0, 1, 3), (9, 3, 2, 0))
 
-ROTATIONS = ((0, 0), (1, 0), (0, 1), (0, 7), (1, 1), (1, 7), (0, 2), (0, 6), (1, 2), (1, 6), (0, 3), (0, 5), (1, 3),
+ROTATIONS = ((0, 0), (0, 1), (0, 7), (0, 2), (0, 6), (1, 0), (1, 1), (1, 7), (1, 2), (1, 6), (0, 3), (0, 5), (1, 3),
              (1, 5), (0, 4), (1, 4))
+NEAR_Z = range(1, 5)
+PASSED = range(5, 10)
+FAR_AWAY = range(10, 16)
+ROWS = 3 * TOK
 XORS = (3, 1, 2, 0)
-NEAR = 2
-FILL_SPREAD = False
 FILL_RETURN = True
 
 
@@ -87,17 +89,22 @@
 
 
 def pack_kernel(q_ref, k_ref, v_ref, *refs):
-    outs, queries, sems = refs[:16], refs[16], refs[17]
+    outs, queries, sems = refs[:12], refs[12], refs[13]
     core, seq = lax.axis_index("dp") % 2, lax.axis_index("seq")
     first = pltpu.make_async_copy(q_ref, queries, sems.at[32])
     first.start()
-    copies, columns = [], []
+    copies, places = [], []
     for r, (dx, dz) in enumerate(ROTATIONS):
         target = ((seq // 8) ^ dx) * 8 + (seq % 8 + dz) % 8
         at = pl.ds(pl.multiple_of(head_at(core, target) * HEAD_DIM, HEAD_DIM), HEAD_DIM)
-        columns.append(at)
+        if r in PASSED[1:]:
+            out, top = outs[r - PASSED[0]], ROWS
+        else:
+            out, top = outs[r if r <= PASSED[0] else r - 4], 0
+        places.append((out, top, at))
         for i, ref in enumerate((k_ref, v_ref)):
-            copy = pltpu.make_async_copy(ref.at[:, at], outs[r].at[(i + 1) * TOK:(i + 2) * TOK, :], sems.at[2 * r + i])
+            copy = pltpu.make_async_copy(ref.at[:, at], out.at[top + (i + 1) * TOK:top + (i + 2) * TOK, :],
+                                         sems.at[2 * r + i])
             copy.start()
             copies.append(copy)
     row = lax.broadcasted_iota(jnp.int32, (TOK, TOK), 0)
@@ -106,38 +113,56 @@
     wanted = ((grid_row % 2) * 2 + grid_col % 2) * LOC + (grid_row // 2) * 32 + grid_col // 2
     order = jnp.where(row == wanted, 1.0, 0.0).astype(jnp.bfloat16)
     first.wait()
-    for r in range(16):
-        outs[r][0:TOK, :] = jnp.dot(order, queries[:, columns[r]],
-                                    preferred_element_type=jnp.float32).astype(jnp.bfloat16)
+    for out, top, at in places:
+        out[top:top + TOK, :] = jnp.dot(order, queries[:, at], preferred_element_type=jnp.float32).astype(jnp.bfloat16)
     for copy in copies:
         copy.wait()
 
 
-def pack(queries, key_rows, value_rows):
-    shape = jax.ShapeDtypeStruct((3 * TOK, HEAD_DIM), jnp.bfloat16)
+def pack(*arrays):
+    arrays = [pltpu.with_memory_space_constraint(array, pltpu.HBM) for array in arrays]
+    rows = [ROWS] + [2 * ROWS] * 4 + [ROWS] * 7
     return pl.pallas_call(
         pack_kernel,
         in_specs=[pl.BlockSpec(memory_space=pltpu.HBM)] * 3,
-        out_specs=[vmem()] * 16,
-        out_shape=[shape] * 16,
+        out_specs=[vmem()] * 12,
+        out_shape=[jax.ShapeDtypeStruct((n, HEAD_DIM), jnp.bfloat16) for n in rows],
         scratch_shapes=[pltpu.VMEM((TOK, HEADS * HEAD_DIM), jnp.bfloat16), pltpu.SemaphoreType.DMA((33,))],
         compiler_params=pltpu.CompilerParams(vmem_limit_bytes=16 * 2**20),
         name="pack",
-    )(queries, key_rows, value_rows)
-
-
-def gather_kernel(*refs):
+    )(*arrays)
+
+
+def pass_kernel(*refs):
+    for i, ref in enumerate(refs[:-1]):
+        refs[-1][i * ROWS:(i + 1) * ROWS, :] = ref[-ROWS:, :]
+
+
+def pass_on(*arrays):
+    return pl.pallas_call(
+        pass_kernel,
+        in_specs=[vmem()] * len(arrays),
+        out_specs=vmem(),
+        out_shape=jax.ShapeDtypeStruct((len(arrays) * ROWS, HEAD_DIM), jnp.bfloat16),
+        compiler_params=pltpu.CompilerParams(vmem_limit_bytes=8 * 2**20),
+        name="pass_on",
+    )(*arrays)
+
+
+def gather_kernel(tops, *refs):
     got, (q_out, k_out, v_out) = refs[:GROUP], refs[GROUP:]
-    for i in range(GROUP):
+    for i, top in enumerate(tops):
         for klass in range(4):
-            q_out[klass, i * LOC:(i + 1) * LOC, :] = got[i][klass * LOC:(klass + 1) * LOC, :]
-        k_out[i * TOK:(i + 1) * TOK, :] = got[i][TOK:2 * TOK, :]
-        v_out[:, i * TOK:(i + 1) * TOK] = got[i][2 * TOK:, :].T
-
-
-def gather_group(messages):
-    return pl.pallas_call(
-        gather_kernel,
+            at = top + klass * LOC
+            q_out[klass, i * LOC:(i + 1) * LOC, :] = got[i][at:at + LOC, :]
+        k_out[i * TOK:(i + 1) * TOK, :] = got[i][top + TOK:top + 2 * TOK, :]
+        v_out[:, i * TOK:(i + 1) * TOK] = got[i][top + 2 * TOK:top + ROWS, :].T
+
+
+def gather_group(parts):
+    tops = [top for _, top in parts]
+    return pl.pallas_call(
+        lambda *refs: gather_kernel(tops, *refs),
         in_specs=[vmem()] * GROUP,
         out_specs=[vmem()] * 3,
         out_shape=[
@@ -147,7 +172,7 @@
         ],
         compiler_params=pltpu.CompilerParams(vmem_limit_bytes=16 * 2**20),
         name="gather_group",
-    )(*messages)
+    )(*[part for part, _ in parts])
 
 
 def attend_kernel(stages, groups, known, flips, slots, final, *refs):
@@ -332,12 +357,20 @@
 def exchange_and_attend(queries, key_rows, value_rows):
     axes = ("dp", "seq")
     messages = pack(queries, key_rows, value_rows)
-    got = [messages[0]]
-    for r in range(1, 16):
-        near = min(ROTATIONS[r][1], 8 - ROTATIONS[r][1]) <= NEAR
-        perm = pairs(lambda s: turn(s, ROTATIONS[r]), lambda core, s, t: near or not idle(core, t), FILL_SPREAD)
-        got.append(lax.ppermute(messages[r], axes, perm))
-    groups = [gather_group(got[i:i + GROUP]) for i in range(0, 16, GROUP)]
+    everyone = lambda core, s, t: True
+    parts = {0: (messages[0], 0)}
+    near = []
+    for r in NEAR_Z:
+        near.append(lax.ppermute(messages[r], axes, pairs(lambda s: turn(s, ROTATIONS[r]), everyone)))
+        parts[r] = (near[-1], 0)
+    for ranks, arrays in ((PASSED[:3], [messages[5]] + near[:2]), (PASSED[3:], near[2:])):
+        passed = lax.ppermute(pass_on(*arrays), axes, pairs(lambda s: turn(s, (1, 0)), everyone))
+        for i, r in enumerate(ranks):
+            parts[r] = (passed, i * ROWS)
+    for r in FAR_AWAY:
+        perm = pairs(lambda s: turn(s, ROTATIONS[r]), lambda core, s, t: not idle(core, t))
+        parts[r] = (lax.ppermute(messages[r - 4], axes, perm), 0)
+    groups = [gather_group([parts[i] for i in range(g, g + GROUP)]) for g in range(0, 16, GROUP)]
 
     first = attend([[(0, (0, 1))], [(1, (0, 1))]], groups[:2])
     second = attend([[(2, (0, 1, 2))], [(0, (2,)), (1, (2,))]], groups[:3], 2, first, XORS[:2])

time: 128 us -> 137 us (1.070)
  waiting for transfers between devices: 31.6 us -> 38.6 us
  starting transfers between devices: 62.6 us -> 68.5 us
  local copies, waits for them, and re-layouts: 3.47 us -> 0 us
    ppermute x15 -> x12, waiting for transfers between devices: 9.88 us -> 19.8 us  [the longest x4 12.9 us: exchange_and_attend(): lax.ppermute(messages[r], axes, pairs(lambda s: turn(s, ROTATIONS[r]), ev...]
    unnamed x6 -> x0, local copies, waits for them, and re-layouts: 3.47 us -> none
    ppermute x15 -> x12, starting transfers between devices: 53.2 us -> 56.3 us  [the longest x6 42.2 us: exchange_and_attend(): parts[r] = (lax.ppermute(messages[r - 4], axes, perm), 0)]
    ppermute x1, starting transfers between devices: 0.08 us -> 3.16 us  [exchange_and_attend(): lax.ppermute(last_head(blocks), axes, pairs(lambda s: turn(s, (0, 1)), la...]
    ppermute x1, waiting for transfers between devices: 5.22 us -> 2.67 us  [exchange_and_attend(): lax.ppermute(last_head(blocks), axes, pairs(lambda s: turn(s, (0, 1)), la...]
  transfers between devices with their start and end apart: 19 -> 16, of which waited for: 6 -> 9; matrix products, arithmetic and copies ran while one was open for 0% -> 0% of each run, Pallas kernels for 13% -> 5%
where the time goes in v5:
time: 137 us
  starting transfers between devices  68.5 us (50%)
  waiting for transfers between devices  38.6 us (28%)
  Pallas kernels  29.7 us (22%)
    ppermute x6, starting transfers between devices, exchange_and_attend(): parts[r] = (lax.ppermute(messages[r - 4], axes, perm), 0)  42.2 us
    pallas_call x6, Pallas kernels, attend(): pl.pallas_call(lambda *refs: attend_kernel(stages, count, known, flips, s...  23.6 us
    ppermute x3, waiting for transfers between devices, exchange_and_attend(): out = lax.ppermute(out, axes, perm)  16.1 us
    ppermute x4, waiting for transfers between devices, exchange_and_attend(): lax.ppermute(messages[r], axes, pairs(lambda s: turn(s, ROTATIONS[r]), ev...  12.9 us
    ppermute x4, starting transfers between devices, exchange_and_attend(): lax.ppermute(messages[r], axes, pairs(lambda s: turn(s, ROTATIONS[r]), ev...  10.2 us
    ppermute x3, starting transfers between devices, exchange_and_attend(): out = lax.ppermute(out, axes, perm)  8.99 us
    ppermute x6, waiting for transfers between devices, exchange_and_attend(): parts[r] = (lax.ppermute(messages[r - 4], axes, perm), 0)  6.9 us
    ppermute x2, starting transfers between devices, exchange_and_attend(): lax.ppermute(pass_on(*arrays), axes, pairs(lambda s: turn(s, (1, 0)), eve...  3.96 us
  transfers between devices with their start and end apart: 16, of which 9 were waited for; matrix products, arithmetic and copies ran while one was open for 0% of the time, Pallas kernels for 5%

profile of v5, /device:TPU:16, one launch (start us, length us, event | category | flops | bytes accessed | tf_op | source)
XLA Modules:
  0.0 137.0 jit_solution(4802701864609995408)
XLA Ops:
  0.0 2.2 %pack.1 = (bf16[768,128]{1,0:T(8,128)(2,1)S(1)}, bf16[1536,128]{1,0:T(8,128)(2,1)S(1)}, bf16[1536,128]{1,0:T(8,128)(2,1)S(1)}, bf16[1536,128]{1,0:T(8,128)(2,1)S...) custom-call(bf16[256,1664]{1,0:T(8,128)(2,1)} %q_ref.1, ...), custom_call_target="tpu_custom_call" | custom-call | tf_op jit(solution)/shard_map/pack/pallas_call | solution.py:125
  2.2 2.0 %collective-permute-start = (bf16[1536,128]{1,0:T(8,128)(2,1)S(1)}, bf16[1536,128]{1,0:T(8,128)(2,1)S(1)}, u32[]{:S(2)}, u32[]{:S(2)}) collective-permute-start(bf16[1536,128]{1,0:T(8,128)(2,1)S(1)} %get-tuple-element.36), channel_id=1, source_target_pairs={{0,1},{1,2},{2,3},{3,4},{4,5},{5,6},{6,7},{7,0},{8,9},{9,10},{10,1... | collective-permute-start | bytes 1179656 | tf_op jit(solution)/shard_map/ppermute | solution.py:364
  4.2 4.0 %collective-permute-start.1 = (bf16[1536,128]{1,0:T(8,128)(2,1)S(1)}, bf16[1536,128]{1,0:T(8,128)(2,1)S(1)}, u32[]{:S(2)}, u32[]{:S(2)}) collective-permute-start(bf16[1536,128]{1,0:T(8,128)(2,1)S(1)} %get-tuple-element.37), channel_id=1, source_target_pairs={{0,7},{1,0},{2,1},{3,2},{4,3},{5,4},{6,5},{7,6},{8,15},{9,8},{10,9... | collective-permute-start | bytes 1179656 | tf_op jit(solution)/shard_map/ppermute | solution.py:364
  8.2 4.1 %collective-permute-start.3 = (bf16[1536,128]{1,0:T(8,128)(2,1)S(1)}, bf16[1536,128]{1,0:T(8,128)(2,1)S(1)}, u32[]{:S(2)}, u32[]{:S(2)}) collective-permute-start(bf16[1536,128]{1,0:T(8,128)(2,1)S(1)} %get-tuple-element.40), channel_id=1, source_target_pairs={{0,6},{1,7},{2,0},{3,1},{4,2},{5,3},{6,4},{7,5},{8,14},{9,15},{10,... | collective-permute-start | bytes 1179656 | tf_op jit(solution)/shard_map/ppermute | solution.py:364
  12.4 6.2 %collective-permute-done.refs_1_ = bf16[1536,128]{1,0:T(8,128)(2,1)S(1)} collective-permute-done((bf16[1536,128]{1,0:T(8,128)(2,1)S(1)}, bf16[1536,128]{1,0:T(8,128)(2,1)S(1)}, u32[]{:S(2)}, u32[]{:S(2)}) %collective-permute-start) | collective-permute-done | bytes 393248 | tf_op jit(solution)/shard_map/ppermute | solution.py:364
  18.6 4.7 %collective-permute-done.1.refs_2_ = bf16[1536,128]{1,0:T(8,128)(2,1)S(1)} collective-permute-done((bf16[1536,128]{1,0:T(8,128)(2,1)S(1)}, bf16[1536,128]{1,0:T(8,128)(2,1)S(1)}, u32[]{:S(2)}, u32[]{:S(2)}) %collective-permute-start.1) | collective-permute-done | bytes 393248 | tf_op jit(solution)/shard_map/ppermute | solution.py:364
  23.4 2.1 %collective-permute-start.4 = (bf16[2304,128]{1,0:T(8,128)(2,1)S(1)}, bf16[2304,128]{1,0:T(8,128)(2,1)S(1)}, u32[]{:S(2)}, u32[]{:S(2)}) collective-permute-start(bf16[2304,128]{1,0:T(8,128)(2,1)S(1)} %pass_on.2), channel_id=1, source_target_pairs={{0,8},{1,9},{2,10},{3,11},{4,12},{5,13},{6,14},{7,15},{8,0},{9,1},... | collective-permute-start | bytes 1769480 | tf_op jit(solution)/shard_map/ppermute | solution.py:367
  25.4 11.3 %collective-permute-start.8 = (bf16[768,128]{1,0:T(8,128)(2,1)S(1)}, bf16[768,128]{1,0:T(8,128)(2,1)S(1)}, u32[]{:S(2)}, u32[]{:S(2)}) collective-permute-start(bf16[768,128]{1,0:T(8,128)(2,1)S(1)} %get-tuple-element.46), channel_id=1, source_target_pairs={{0,11},{1,12},{2,13},{3,14},{5,8},{6,9},{7,10},{8,3},{9,4},{10,5},... | collective-permute-start | bytes 589832 | tf_op jit(solution)/shard_map/ppermute | solution.py:372
  36.7 1.9 %collective-permute-start.9 = (bf16[768,128]{1,0:T(8,128)(2,1)S(1)}, bf16[768,128]{1,0:T(8,128)(2,1)S(1)}, u32[]{:S(2)}, u32[]{:S(2)}) collective-permute-start(bf16[768,128]{1,0:T(8,128)(2,1)S(1)} %get-tuple-element.47), channel_id=1, source_target_pairs={{0,13},{1,14},{3,8},{4,9},{5,10},{6,11},{7,12},{8,5},{10,7},{11,0}... | collective-permute-start | bytes 589832 | tf_op jit(solution)/shard_map/ppermute | solution.py:372
  38.7 2.0 %collective-permute-done.2.refs_3_.refs_0_ = bf16[1536,128]{1,0:T(8,128)(2,1)S(1)} collective-permute-done((bf16[1536,128]{1,0:T(8,128)(2,1)S(1)}, bf16[1536,128]{1,0:T(8,128)(2,1)S(1)}, u32[]{:S(2)}, u32[]{:S(2)}) %collective-permute-start.2) | collective-permute-done | bytes 393248 | tf_op jit(solution)/shard_map/ppermute | solution.py:364
  40.6 6.8 %collective-permute-start.10 = (bf16[768,128]{1,0:T(8,128)(2,1)S(1)}, bf16[768,128]{1,0:T(8,128)(2,1)S(1)}, u32[]{:S(2)}, u32[]{:S(2)}) collective-permute-start(bf16[768,128]{1,0:T(8,128)(2,1)S(1)} %get-tuple-element.48), channel_id=1, source_target_pairs={{0,4},{1,5},{3,7},{4,0},{6,2},{7,3},{8,12},{9,13},{10,14},{12,8},{... | collective-permute-start | bytes 589832 | tf_op jit(solution)/shard_map/ppermute | solution.py:372
  47.5 1.9 %collective-permute-start.5 = (bf16[1536,128]{1,0:T(8,128)(2,1)S(1)}, bf16[1536,128]{1,0:T(8,128)(2,1)S(1)}, u32[]{:S(2)}, u32[]{:S(2)}) collective-permute-start(bf16[1536,128]{1,0:T(8,128)(2,1)S(1)} %pass_on.3), channel_id=1, source_target_pairs={{0,8},{1,9},{2,10},{3,11},{4,12},{5,13},{6,14},{7,15},{8,0},{9,1},... | collective-permute-start | bytes 1179656 | tf_op jit(solution)/shard_map/ppermute | solution.py:367
  49.5 7.2 %collective-permute-start.11 = (bf16[768,128]{1,0:T(8,128)(2,1)S(1)}, bf16[768,128]{1,0:T(8,128)(2,1)S(1)}, u32[]{:S(2)}, u32[]{:S(2)}) collective-permute-start(bf16[768,128]{1,0:T(8,128)(2,1)S(1)} %get-tuple-element.49), channel_id=1, source_target_pairs={{0,12},{1,13},{2,14},{4,8},{5,9},{6,10},{7,11},{8,4},{9,5},{11,7},... | collective-permute-start | bytes 589832 | tf_op jit(solution)/shard_map/ppermute | solution.py:372
  56.6 3.1 %collective-permute-start.6 = (bf16[768,128]{1,0:T(8,128)(2,1)S(1)}, bf16[768,128]{1,0:T(8,128)(2,1)S(1)}, u32[]{:S(2)}, u32[]{:S(2)}) collective-permute-start(bf16[768,128]{1,0:T(8,128)(2,1)S(1)} %get-tuple-element.43), channel_id=1, source_target_pairs={{0,3},{1,4},{2,5},{4,7},{5,0},{7,2},{8,11},{9,12},{10,13},{11,14},... | collective-permute-start | bytes 589832 | tf_op jit(solution)/shard_map/ppermute | solution.py:372
  59.7 12.0 %collective-permute-start.7 = (bf16[768,128]{1,0:T(8,128)(2,1)S(1)}, bf16[768,128]{1,0:T(8,128)(2,1)S(1)}, u32[]{:S(2)}, u32[]{:S(2)}) collective-permute-start(bf16[768,128]{1,0:T(8,128)(2,1)S(1)} %get-tuple-element.44), channel_id=1, source_target_pairs={{0,5},{2,7},{3,0},{5,2},{6,3},{7,4},{8,13},{9,14},{11,8},{12,9},{1... | collective-permute-start | bytes 589832 | tf_op jit(solution)/shard_map/ppermute | solution.py:372
  72.0 4.3 %collective-permute-done.6.refs_2_ = bf16[768,128]{1,0:T(8,128)(2,1)S(1)} collective-permute-done((bf16[768,128]{1,0:T(8,128)(2,1)S(1)}, bf16[768,128]{1,0:T(8,128)(2,1)S(1)}, u32[]{:S(2)}, u32[]{:S(2)}) %collective-permute-start.6) | collective-permute-done | bytes 196640 | tf_op jit(solution)/shard_map/ppermute | solution.py:372
  76.3 2.5 %collective-permute-done.7.refs_3_ = bf16[768,128]{1,0:T(8,128)(2,1)S(1)} collective-permute-done((bf16[768,128]{1,0:T(8,128)(2,1)S(1)}, bf16[768,128]{1,0:T(8,128)(2,1)S(1)}, u32[]{:S(2)}, u32[]{:S(2)}) %collective-permute-start.7) | collective-permute-done | bytes 196640 | tf_op jit(solution)/shard_map/ppermute | solution.py:372
  79.0 5.9 %attend.6 = (f32[4,128,512]{2,1,0:T(8,128)S(1)}, f32[4,8,512]{2,1,0:T(8,128)S(1)}, f32[4,8,512]{2,1,0:T(8,128)S(1)}) custom-call(bf16[4,256,128]{2,1,0:T(8,128)(2,1)S(1)} %get-tuple-element.39.refs_0_, bf16[4,256,128]{2,1,0:T(8,128)(2,1)S(1)} %get-tuple-element.42.refs_1_, bf16[1024,128]{1,0:T(8,128)(2,1)S(1)} %get-tuple-element.51.refs_2_.refs_3_.refs_4_, ...), custom_call_target="tpu_custom_call" | custom-call | flops 2147483648 | bytes 1572864 | tf_op jit(solution)/shard_map/attend/pallas_call | solution.py:259
  84.9 3.8 %attend.7 = (f32[2,128,768]{2,1,0:T(8,128)S(1)}, f32[2,8,768]{2,1,0:T(8,128)S(1)}, f32[2,8,768]{2,1,0:T(8,128)S(1)}) custom-call(bf16[4,256,128]{2,1,0:T(8,128)(2,1)S(1)} %get-tuple-element.39.refs_0_, bf16[4,256,128]{2,1,0:T(8,128)(2,1)S(1)} %get-tuple-element.42.refs_1_, bf16[4,256,128]{2,1,0:T(8,128)(2,1)S(1)} %get-tuple-element.45.refs_2_, ...), custom_call_target="tpu_custom_call" | custom-call | flops 1342177280 | bytes 2359296 | tf_op jit(solution)/shard_map/attend/pallas_call | solution.py:259
  88.8 4.5 %attend.10 = bf16[1024,128]{1,0:T(8,128)(2,1)S(1)} custom-call(bf16[4,256,128]{2,1,0:T(8,128)(2,1)S(1)} %get-tuple-element.39.refs_0_, bf16[4,256,128]{2,1,0:T(8,128)(2,1)S(1)} %get-tuple-element.42.refs_1_, bf16[4,256,128]{2,1,0:T(8,128)(2,1)S(1)} %get-tuple-element.45.refs_2_, bf16[4,256,128]{2,1,0:T(8,128)(2,1)S(1)} %get-tuple-element.50.refs_3_, ...), custom_call_target="tpu_custom_call" | custom-call | flops 1610612736 | bytes 3145728 | tf_op jit(solution)/shard_map/attend/pallas_call | solution.py:259
  93.3 2.6 %attend.9 = bf16[1024,128]{1,0:T(8,128)(2,1)S(1)} custom-call(bf16[4,256,128]{2,1,0:T(8,128)(2,1)S(1)} %get-tuple-element.39.refs_0_, bf16[4,256,128]{2,1,0:T(8,128)(2,1)S(1)} %get-tuple-element.42.refs_1_, bf16[4,256,128]{2,1,0:T(8,128)(2,1)S(1)} %get-tuple-element.45.refs_2_, bf16[4,256,128]{2,1,0:T(8,128)(2,1)S(1)} %get-tuple-element.50.refs_3_, ...), custom_call_target="tpu_custom_call" | custom-call | flops 939524096 | bytes 3145728 | tf_op jit(solution)/shard_map/attend/pallas_call | solution.py:259
  95.9 2.6 %attend.8 = bf16[1024,128]{1,0:T(8,128)(2,1)S(1)} custom-call(bf16[4,256,128]{2,1,0:T(8,128)(2,1)S(1)} %get-tuple-element.39.refs_0_, bf16[4,256,128]{2,1,0:T(8,128)(2,1)S(1)} %get-tuple-element.42.refs_1_, bf16[4,256,128]{2,1,0:T(8,128)(2,1)S(1)} %get-tuple-element.45.refs_2_, bf16[4,256,128]{2,1,0:T(8,128)(2,1)S(1)} %get-tuple-element.50.refs_3_, ...), custom_call_target="tpu_custom_call" | custom-call | flops 939524096 | bytes 3145728 | tf_op jit(solution)/shard_map/attend/pallas_call | solution.py:259
  98.4 4.3 %collective-permute-start.12 = (bf16[1024,128]{1,0:T(8,128)(2,1)S(1)}, bf16[1024,128]{1,0:T(8,128)(2,1)S(1)}, u32[]{:S(2)}, u32[]{:S(2)}) collective-permute-start(bf16[1024,128]{1,0:T(8,128)(2,1)S(1)} %attend.8), channel_id=1, source_target_pairs={{0,12},{2,14},{3,15},{4,8},{5,9},{7,11},{8,4},{9,5},{10,6},{11,7},... | collective-permute-start | bytes 786440 | tf_op jit(solution)/shard_map/ppermute | solution.py:387
  102.8 2.6 %collective-permute-start.13 = (bf16[1024,128]{1,0:T(8,128)(2,1)S(1)}, bf16[1024,128]{1,0:T(8,128)(2,1)S(1)}, u32[]{:S(2)}, u32[]{:S(2)}) collective-permute-start(bf16[1024,128]{1,0:T(8,128)(2,1)S(1)} %attend.9), channel_id=1, source_target_pairs={{0,4},{2,6},{3,7},{4,0},{5,1},{7,3},{8,12},{9,13},{10,14},{11,15},... | collective-permute-start | bytes 786440 | tf_op jit(solution)/shard_map/ppermute | solution.py:387
  105.4 2.0 %collective-permute-start.14 = (bf16[1024,128]{1,0:T(8,128)(2,1)S(1)}, bf16[1024,128]{1,0:T(8,128)(2,1)S(1)}, u32[]{:S(2)}, u32[]{:S(2)}) collective-permute-start(bf16[1024,128]{1,0:T(8,128)(2,1)S(1)} %attend.10), channel_id=1, source_target_pairs={{0,8},{2,10},{3,11},{4,12},{5,13},{7,15},{8,0},{9,1},{10,2},{11,3}... | collective-permute-start | bytes 786440 | tf_op jit(solution)/shard_map/ppermute | solution.py:387
  107.4 4.3 %attend.11.refs_3_ = bf16[1024,128]{1,0:T(8,128)(2,1)S(1)} custom-call(bf16[4,256,128]{2,1,0:T(8,128)(2,1)S(1)} %get-tuple-element.39.refs_0_, bf16[4,256,128]{2,1,0:T(8,128)(2,1)S(1)} %get-tuple-element.42.refs_1_, bf16[4,256,128]{2,1,0:T(8,128)(2,1)S(1)} %get-tuple-element.45.refs_2_, bf16[4,256,128]{2,1,0:T(8,128)(2,1)S(1)} %get-tuple-element.50.refs_3_, ...), custom_call_target="tpu_custom_call" | custom-call | flops 1610612736 | bytes 3145728 | tf_op jit(solution)/shard_map/attend/pallas_call | solution.py:259
  111.7 4.3 %collective-permute-done.12.refs_0_ = bf16[1024,128]{1,0:T(8,128)(2,1)S(1)} collective-permute-done((bf16[1024,128]{1,0:T(8,128)(2,1)S(1)}, bf16[1024,128]{1,0:T(8,128)(2,1)S(1)}, u32[]{:S(2)}, u32[]{:S(2)}) %collective-permute-start.12) | collective-permute-done | bytes 262176 | tf_op jit(solution)/shard_map/ppermute | solution.py:387
  116.0 11.8 %collective-permute-done.13.refs_1_ = bf16[1024,128]{1,0:T(8,128)(2,1)S(1)} collective-permute-done((bf16[1024,128]{1,0:T(8,128)(2,1)S(1)}, bf16[1024,128]{1,0:T(8,128)(2,1)S(1)}, u32[]{:S(2)}, u32[]{:S(2)}) %collective-permute-start.13) | collective-permute-done | bytes 262176 | tf_op jit(solution)/shard_map/ppermute | solution.py:387
  128.3 3.2 %collective-permute-start.15 = (bf16[96,1024]{1,0:T(8,128)(2,1)S(1)}, bf16[96,1024]{1,0:T(8,128)(2,1)S(1)}, u32[]{:S(2)}, u32[]{:S(2)}) collective-permute-start(bf16[96,1024]{1,0:T(8,128)(2,1)S(1)} %last_head.1), channel_id=1, source_target_pairs={{0,1},{1,2},{2,3},{3,4},{4,5},{5,6},{6,7},{7,0},{8,9},{9,10},{10,1... | collective-permute-start | bytes 589832 | tf_op jit(solution)/shard_map/ppermute | solution.py:389
  131.4 1.6 %merge.1.refs_5_ = bf16[416,1024]{1,0:T(8,128)(2,1)} custom-call(bf16[1024,128]{1,0:T(8,128)(2,1)S(1)} %collective-permute-done.12.refs_0_, bf16[1024,128]{1,0:T(8,128)(2,1)S(1)} %collective-permute-done.13.refs_1_, bf16[1024,128]{1,0:T(8,128)(2,1)S(1)} %collective-permute-done.14.refs_2_, bf16[1024,128]{1,0:T(8,128)(2,1)S(1)} %attend.11.refs_3_), custom_call_target="tpu_custom_call" | custom-call | tf_op jit(solution)/shard_map/merge/pallas_call | solution.py:321
  133.0 2.7 %collective-permute-done.15.refs_4_ = bf16[96,1024]{1,0:T(8,128)(2,1)S(1)} collective-permute-done((bf16[96,1024]{1,0:T(8,128)(2,1)S(1)}, bf16[96,1024]{1,0:T(8,128)(2,1)S(1)}, u32[]{:S(2)}, u32[]{:S(2)}) %collective-permute-start.15) | collective-permute-done | bytes 196640 | tf_op jit(solution)/shard_map/ppermute | solution.py:389
  135.7 1.2 finish.1
  (16 shorter events, 1.1 us)
Async XLA Ops:
  2.2 16.4 %collective-permute-start = (bf16[1536,128]{1,0:T(8,128)(2,1)S(1)}, bf16[1536,128]{1,0:T(8,128)(2,1)S(1)}, u32[]{:S(2)}, u32[]{:S(2)}) collective-permute-start(bf16[1536,128]{1,0:T(8,128)(2,1)S(1)} %get-tuple-element.36), channel_id=1, source_target_pairs={{0,1},{1,2},{2,3},{3,4},{4,5},{5,6},{6,7},{7,0},{8,9},{9,10},{10,1... | collective-permute-start | bytes 1179656 | tf_op jit(solution)/shard_map/ppermute | solution.py:364
  4.2 19.1 %collective-permute-start.1 = (bf16[1536,128]{1,0:T(8,128)(2,1)S(1)}, bf16[1536,128]{1,0:T(8,128)(2,1)S(1)}, u32[]{:S(2)}, u32[]{:S(2)}) collective-permute-start(bf16[1536,128]{1,0:T(8,128)(2,1)S(1)} %get-tuple-element.37), channel_id=1, source_target_pairs={{0,7},{1,0},{2,1},{3,2},{4,3},{5,4},{6,5},{7,6},{8,15},{9,8},{10,9... | collective-permute-start | bytes 1179656 | tf_op jit(solution)/shard_map/ppermute | solution.py:364
  8.2 32.4 %collective-permute-start.2 = (bf16[1536,128]{1,0:T(8,128)(2,1)S(1)}, bf16[1536,128]{1,0:T(8,128)(2,1)S(1)}, u32[]{:S(2)}, u32[]{:S(2)}) collective-permute-start(bf16[1536,128]{1,0:T(8,128)(2,1)S(1)} %get-tuple-element.38), channel_id=1, source_target_pairs={{0,2},{1,3},{2,4},{3,5},{4,6},{5,7},{6,0},{7,1},{8,10},{9,11},{10,... | collective-permute-start | bytes 1179656 | tf_op jit(solution)/shard_map/ppermute | solution.py:364
  8.2 39.2 %collective-permute-start.3 = (bf16[1536,128]{1,0:T(8,128)(2,1)S(1)}, bf16[1536,128]{1,0:T(8,128)(2,1)S(1)}, u32[]{:S(2)}, u32[]{:S(2)}) collective-permute-start(bf16[1536,128]{1,0:T(8,128)(2,1)S(1)} %get-tuple-element.40), channel_id=1, source_target_pairs={{0,6},{1,7},{2,0},{3,1},{4,2},{5,3},{6,4},{7,5},{8,14},{9,15},{10,... | collective-permute-start | bytes 1179656 | tf_op jit(solution)/shard_map/ppermute | solution.py:364
  23.4 55.5 %collective-permute-start.4 = (bf16[2304,128]{1,0:T(8,128)(2,1)S(1)}, bf16[2304,128]{1,0:T(8,128)(2,1)S(1)}, u32[]{:S(2)}, u32[]{:S(2)}) collective-permute-start(bf16[2304,128]{1,0:T(8,128)(2,1)S(1)} %pass_on.2), channel_id=1, source_target_pairs={{0,8},{1,9},{2,10},{3,11},{4,12},{5,13},{6,14},{7,15},{8,0},{9,1},... | collective-permute-start | bytes 1769480 | tf_op jit(solution)/shard_map/ppermute | solution.py:367
  25.4 24.0 %collective-permute-start.8 = (bf16[768,128]{1,0:T(8,128)(2,1)S(1)}, bf16[768,128]{1,0:T(8,128)(2,1)S(1)}, u32[]{:S(2)}, u32[]{:S(2)}) collective-permute-start(bf16[768,128]{1,0:T(8,128)(2,1)S(1)} %get-tuple-element.46), channel_id=1, source_target_pairs={{0,11},{1,12},{2,13},{3,14},{5,8},{6,9},{7,10},{8,3},{9,4},{10,5},... | collective-permute-start | bytes 589832 | tf_op jit(solution)/shard_map/ppermute | solution.py:372
  36.7 19.9 %collective-permute-start.9 = (bf16[768,128]{1,0:T(8,128)(2,1)S(1)}, bf16[768,128]{1,0:T(8,128)(2,1)S(1)}, u32[]{:S(2)}, u32[]{:S(2)}) collective-permute-start(bf16[768,128]{1,0:T(8,128)(2,1)S(1)} %get-tuple-element.47), channel_id=1, source_target_pairs={{0,13},{1,14},{3,8},{4,9},{5,10},{6,11},{7,12},{8,5},{10,7},{11,0}... | collective-permute-start | bytes 589832 | tf_op jit(solution)/shard_map/ppermute | solution.py:372
  40.6 19.1 %collective-permute-start.10 = (bf16[768,128]{1,0:T(8,128)(2,1)S(1)}, bf16[768,128]{1,0:T(8,128)(2,1)S(1)}, u32[]{:S(2)}, u32[]{:S(2)}) collective-permute-start(bf16[768,128]{1,0:T(8,128)(2,1)S(1)} %get-tuple-element.48), channel_id=1, source_target_pairs={{0,4},{1,5},{3,7},{4,0},{6,2},{7,3},{8,12},{9,13},{10,14},{12,8},{... | collective-permute-start | bytes 589832 | tf_op jit(solution)/shard_map/ppermute | solution.py:372
  47.5 31.3 %collective-permute-start.5 = (bf16[1536,128]{1,0:T(8,128)(2,1)S(1)}, bf16[1536,128]{1,0:T(8,128)(2,1)S(1)}, u32[]{:S(2)}, u32[]{:S(2)}) collective-permute-start(bf16[1536,128]{1,0:T(8,128)(2,1)S(1)} %pass_on.3), channel_id=1, source_target_pairs={{0,8},{1,9},{2,10},{3,11},{4,12},{5,13},{6,14},{7,15},{8,0},{9,1},... | collective-permute-start | bytes 1179656 | tf_op jit(solution)/shard_map/ppermute | solution.py:367
  49.5 22.3 %collective-permute-start.11 = (bf16[768,128]{1,0:T(8,128)(2,1)S(1)}, bf16[768,128]{1,0:T(8,128)(2,1)S(1)}, u32[]{:S(2)}, u32[]{:S(2)}) collective-permute-start(bf16[768,128]{1,0:T(8,128)(2,1)S(1)} %get-tuple-element.49), channel_id=1, source_target_pairs={{0,12},{1,13},{2,14},{4,8},{5,9},{6,10},{7,11},{8,4},{9,5},{11,7},... | collective-permute-start | bytes 589832 | tf_op jit(solution)/shard_map/ppermute | solution.py:372
  56.6 19.7 %collective-permute-start.6 = (bf16[768,128]{1,0:T(8,128)(2,1)S(1)}, bf16[768,128]{1,0:T(8,128)(2,1)S(1)}, u32[]{:S(2)}, u32[]{:S(2)}) collective-permute-start(bf16[768,128]{1,0:T(8,128)(2,1)S(1)} %get-tuple-element.43), channel_id=1, source_target_pairs={{0,3},{1,4},{2,5},{4,7},{5,0},{7,2},{8,11},{9,12},{10,13},{11,14},... | collective-permute-start | bytes 589832 | tf_op jit(solution)/shard_map/ppermute | solution.py:372
  59.7 19.1 %collective-permute-start.7 = (bf16[768,128]{1,0:T(8,128)(2,1)S(1)}, bf16[768,128]{1,0:T(8,128)(2,1)S(1)}, u32[]{:S(2)}, u32[]{:S(2)}) collective-permute-start(bf16[768,128]{1,0:T(8,128)(2,1)S(1)} %get-tuple-element.44), channel_id=1, source_target_pairs={{0,5},{2,7},{3,0},{5,2},{6,3},{7,4},{8,13},{9,14},{11,8},{12,9},{1... | collective-permute-start | bytes 589832 | tf_op jit(solution)/shard_map/ppermute | solution.py:372
  98.4 17.6 %collective-permute-start.12 = (bf16[1024,128]{1,0:T(8,128)(2,1)S(1)}, bf16[1024,128]{1,0:T(8,128)(2,1)S(1)}, u32[]{:S(2)}, u32[]{:S(2)}) collective-permute-start(bf16[1024,128]{1,0:T(8,128)(2,1)S(1)} %attend.8), channel_id=1, source_target_pairs={{0,12},{2,14},{3,15},{4,8},{5,9},{7,11},{8,4},{9,5},{10,6},{11,7},... | collective-permute-start | bytes 786440 | tf_op jit(solution)/shard_map/ppermute | solution.py:387
  102.8 25.0 %collective-permute-start.13 = (bf16[1024,128]{1,0:T(8,128)(2,1)S(1)}, bf16[1024,128]{1,0:T(8,128)(2,1)S(1)}, u32[]{:S(2)}, u32[]{:S(2)}) collective-permute-start(bf16[1024,128]{1,0:T(8,128)(2,1)S(1)} %attend.9), channel_id=1, source_target_pairs={{0,4},{2,6},{3,7},{4,0},{5,1},{7,3},{8,12},{9,13},{10,14},{11,15},... | collective-permute-start | bytes 786440 | tf_op jit(solution)/shard_map/ppermute | solution.py:387
  105.4 22.4 %collective-permute-start.14 = (bf16[1024,128]{1,0:T(8,128)(2,1)S(1)}, bf16[1024,128]{1,0:T(8,128)(2,1)S(1)}, u32[]{:S(2)}, u32[]{:S(2)}) collective-permute-start(bf16[1024,128]{1,0:T(8,128)(2,1)S(1)} %attend.10), channel_id=1, source_target_pairs={{0,8},{2,10},{3,11},{4,12},{5,13},{7,15},{8,0},{9,1},{10,2},{11,3}... | collective-permute-start | bytes 786440 | tf_op jit(solution)/shard_map/ppermute | solution.py:387
  128.3 7.5 %collective-permute-start.15 = (bf16[96,1024]{1,0:T(8,128)(2,1)S(1)}, bf16[96,1024]{1,0:T(8,128)(2,1)S(1)}, u32[]{:S(2)}, u32[]{:S(2)}) collective-permute-start(bf16[96,1024]{1,0:T(8,128)(2,1)S(1)} %last_head.1), channel_id=1, source_target_pairs={{0,1},{1,2},{2,3},{3,4},{4,5},{5,6},{6,7},{7,0},{8,9},{9,10},{10,1... | collective-permute-start | bytes 589832 | tf_op jit(solution)/shard_map/ppermute | solution.py:389

commit v6 on v5

--- a/solution.py
+++ b/solution.py
@@ -17,7 +17,7 @@
 GROUP = 4
 WIDE = GROUP * LOC
 DEEP = GROUP * TOK
-STEP = 512
+STEP = 1024
 OUT_COLS = 416
 SPLIT = 96
 FAR = 1 << 20
@@ -33,7 +33,7 @@
 FAR_AWAY = range(10, 16)
 ROWS = 3 * TOK
 XORS = (3, 1, 2, 0)
-FILL_RETURN = True
+FILL_RETURN = False
 
 
 def idle(core, seq):
@@ -373,10 +373,10 @@
     groups = [gather_group([parts[i] for i in range(g, g + GROUP)]) for g in range(0, 16, GROUP)]
 
     first = attend([[(0, (0, 1))], [(1, (0, 1))]], groups[:2])
-    second = attend([[(2, (0, 1, 2))], [(0, (2,)), (1, (2,))]], groups[:3], 2, first, XORS[:2])
+    second = attend([[(2, (0, 1, 2))], [(0, (2,)), (1, (2,))]], groups[:3], 2, first, XORS[:1])
     blocks = []
     for n, flip in enumerate(XORS):
-        if n < 2:
+        if n < 1:
             stages = [[(3, (0, 1, 2, 3))], [(0, (3,)), (1, (3,)), (2, (3,))]]
             out = attend(stages, groups, 3, second, (flip,), (n,), True)[0]
         else:

time: 137 us -> 136 us (level); the launches traced: 137 us -> 134 us
  waiting for transfers between devices: 38.6 us -> 27.9 us
  starting transfers between devices: 68.5 us -> 78.2 us
  Pallas kernels: 29.7 us -> 27.3 us
    ppermute x3, waiting for transfers between devices: 16.1 us -> 6.06 us  [exchange_and_attend(): out = lax.ppermute(out, axes, perm)]
    ppermute x3, starting transfers between devices: 8.99 us -> 14.6 us  [exchange_and_attend(): out = lax.ppermute(out, axes, perm)]
    ppermute x1, starting transfers between devices: 3.16 us -> 7.2 us  [exchange_and_attend(): lax.ppermute(last_head(blocks), axes, pairs(lambda s: turn(s, (0, 1)), la...]
    pallas_call x6, Pallas kernels: 23.6 us -> 21.3 us  [attend(): pl.pallas_call(lambda *refs: attend_kernel(stages, count, known, flips, s...]
  transfers between devices with their start and end apart: 16 -> 16, of which waited for: 9 -> 8; matrix products, arithmetic and copies ran while one was open for 0% -> 0% of each run, Pallas kernels for 5% -> 4%
where the time goes in v6:
time: 136 us; the launch traced here: 134 us
  starting transfers between devices  78.2 us (58%)
  waiting for transfers between devices  27.9 us (21%)
  Pallas kernels  27.3 us (20%)
    ppermute x6, starting transfers between devices, exchange_and_attend(): parts[r] = (lax.ppermute(messages[r - 4], axes, perm), 0)  42.2 us
    pallas_call x6, Pallas kernels, attend(): pl.pallas_call(lambda *refs: attend_kernel(stages, count, known, flips, s...  21.3 us
    ppermute x3, starting transfers between devices, exchange_and_attend(): out = lax.ppermute(out, axes, perm)  14.6 us
    ppermute x4, waiting for transfers between devices, exchange_and_attend(): lax.ppermute(messages[r], axes, pairs(lambda s: turn(s, ROTATIONS[r]), ev...  12.9 us
    ppermute x4, starting transfers between devices, exchange_and_attend(): lax.ppermute(messages[r], axes, pairs(lambda s: turn(s, ROTATIONS[r]), ev...  10.2 us
    ppermute x1, starting transfers between devices, exchange_and_attend(): lax.ppermute(last_head(blocks), axes, pairs(lambda s: turn(s, (0, 1)), la...  7.2 us
    ppermute x6, waiting for transfers between devices, exchange_and_attend(): parts[r] = (lax.ppermute(messages[r - 4], axes, perm), 0)  6.9 us
    ppermute x3, waiting for transfers between devices, exchange_and_attend(): out = lax.ppermute(out, axes, perm)  6.06 us
  transfers between devices with their start and end apart: 16, of which 8 were waited for; matrix products, arithmetic and copies ran while one was open for 0% of the time, Pallas kernels for 4%

profile of v6, /device:TPU:16, one launch (start us, length us, event | category | flops | bytes accessed | tf_op | source)
XLA Modules:
  0.0 133.6 jit_solution(383393582235517488)
XLA Ops:
  0.0 2.2 %pack.1 = (bf16[768,128]{1,0:T(8,128)(2,1)S(1)}, bf16[1536,128]{1,0:T(8,128)(2,1)S(1)}, bf16[1536,128]{1,0:T(8,128)(2,1)S(1)}, bf16[1536,128]{1,0:T(8,128)(2,1)S...) custom-call(bf16[256,1664]{1,0:T(8,128)(2,1)} %q_ref.1, ...), custom_call_target="tpu_custom_call" | custom-call | tf_op jit(solution)/shard_map/pack/pallas_call | solution.py:125
  2.2 2.0 %collective-permute-start = (bf16[1536,128]{1,0:T(8,128)(2,1)S(1)}, bf16[1536,128]{1,0:T(8,128)(2,1)S(1)}, u32[]{:S(2)}, u32[]{:S(2)}) collective-permute-start(bf16[1536,128]{1,0:T(8,128)(2,1)S(1)} %get-tuple-element.36), channel_id=1, source_target_pairs={{0,1},{1,2},{2,3},{3,4},{4,5},{5,6},{6,7},{7,0},{8,9},{9,10},{10,1... | collective-permute-start | bytes 1179656 | tf_op jit(solution)/shard_map/ppermute | solution.py:364
  4.2 4.0 %collective-permute-start.1 = (bf16[1536,128]{1,0:T(8,128)(2,1)S(1)}, bf16[1536,128]{1,0:T(8,128)(2,1)S(1)}, u32[]{:S(2)}, u32[]{:S(2)}) collective-permute-start(bf16[1536,128]{1,0:T(8,128)(2,1)S(1)} %get-tuple-element.37), channel_id=1, source_target_pairs={{0,7},{1,0},{2,1},{3,2},{4,3},{5,4},{6,5},{7,6},{8,15},{9,8},{10,9... | collective-permute-start | bytes 1179656 | tf_op jit(solution)/shard_map/ppermute | solution.py:364
  8.2 4.1 %collective-permute-start.3 = (bf16[1536,128]{1,0:T(8,128)(2,1)S(1)}, bf16[1536,128]{1,0:T(8,128)(2,1)S(1)}, u32[]{:S(2)}, u32[]{:S(2)}) collective-permute-start(bf16[1536,128]{1,0:T(8,128)(2,1)S(1)} %get-tuple-element.40), channel_id=1, source_target_pairs={{0,6},{1,7},{2,0},{3,1},{4,2},{5,3},{6,4},{7,5},{8,14},{9,15},{10,... | collective-permute-start | bytes 1179656 | tf_op jit(solution)/shard_map/ppermute | solution.py:364
  12.4 6.2 %collective-permute-done.refs_1_ = bf16[1536,128]{1,0:T(8,128)(2,1)S(1)} collective-permute-done((bf16[1536,128]{1,0:T(8,128)(2,1)S(1)}, bf16[1536,128]{1,0:T(8,128)(2,1)S(1)}, u32[]{:S(2)}, u32[]{:S(2)}) %collective-permute-start) | collective-permute-done | bytes 393248 | tf_op jit(solution)/shard_map/ppermute | solution.py:364
  18.6 4.7 %collective-permute-done.1.refs_2_ = bf16[1536,128]{1,0:T(8,128)(2,1)S(1)} collective-permute-done((bf16[1536,128]{1,0:T(8,128)(2,1)S(1)}, bf16[1536,128]{1,0:T(8,128)(2,1)S(1)}, u32[]{:S(2)}, u32[]{:S(2)}) %collective-permute-start.1) | collective-permute-done | bytes 393248 | tf_op jit(solution)/shard_map/ppermute | solution.py:364
  23.4 2.1 %collective-permute-start.4 = (bf16[2304,128]{1,0:T(8,128)(2,1)S(1)}, bf16[2304,128]{1,0:T(8,128)(2,1)S(1)}, u32[]{:S(2)}, u32[]{:S(2)}) collective-permute-start(bf16[2304,128]{1,0:T(8,128)(2,1)S(1)} %pass_on.2), channel_id=1, source_target_pairs={{0,8},{1,9},{2,10},{3,11},{4,12},{5,13},{6,14},{7,15},{8,0},{9,1},... | collective-permute-start | bytes 1769480 | tf_op jit(solution)/shard_map/ppermute | solution.py:367
  25.4 11.3 %collective-permute-start.8 = (bf16[768,128]{1,0:T(8,128)(2,1)S(1)}, bf16[768,128]{1,0:T(8,128)(2,1)S(1)}, u32[]{:S(2)}, u32[]{:S(2)}) collective-permute-start(bf16[768,128]{1,0:T(8,128)(2,1)S(1)} %get-tuple-element.46), channel_id=1, source_target_pairs={{0,11},{1,12},{2,13},{3,14},{5,8},{6,9},{7,10},{8,3},{9,4},{10,5},... | collective-permute-start | bytes 589832 | tf_op jit(solution)/shard_map/ppermute | solution.py:372
  36.7 1.9 %collective-permute-start.9 = (bf16[768,128]{1,0:T(8,128)(2,1)S(1)}, bf16[768,128]{1,0:T(8,128)(2,1)S(1)}, u32[]{:S(2)}, u32[]{:S(2)}) collective-permute-start(bf16[768,128]{1,0:T(8,128)(2,1)S(1)} %get-tuple-element.47), channel_id=1, source_target_pairs={{0,13},{1,14},{3,8},{4,9},{5,10},{6,11},{7,12},{8,5},{10,7},{11,0}... | collective-permute-start | bytes 589832 | tf_op jit(solution)/shard_map/ppermute | solution.py:372
  38.7 2.0 %collective-permute-done.2.refs_3_.refs_0_ = bf16[1536,128]{1,0:T(8,128)(2,1)S(1)} collective-permute-done((bf16[1536,128]{1,0:T(8,128)(2,1)S(1)}, bf16[1536,128]{1,0:T(8,128)(2,1)S(1)}, u32[]{:S(2)}, u32[]{:S(2)}) %collective-permute-start.2) | collective-permute-done | bytes 393248 | tf_op jit(solution)/shard_map/ppermute | solution.py:364
  40.6 6.8 %collective-permute-start.10 = (bf16[768,128]{1,0:T(8,128)(2,1)S(1)}, bf16[768,128]{1,0:T(8,128)(2,1)S(1)}, u32[]{:S(2)}, u32[]{:S(2)}) collective-permute-start(bf16[768,128]{1,0:T(8,128)(2,1)S(1)} %get-tuple-element.48), channel_id=1, source_target_pairs={{0,4},{1,5},{3,7},{4,0},{6,2},{7,3},{8,12},{9,13},{10,14},{12,8},{... | collective-permute-start | bytes 589832 | tf_op jit(solution)/shard_map/ppermute | solution.py:372
  47.5 1.9 %collective-permute-start.5 = (bf16[1536,128]{1,0:T(8,128)(2,1)S(1)}, bf16[1536,128]{1,0:T(8,128)(2,1)S(1)}, u32[]{:S(2)}, u32[]{:S(2)}) collective-permute-start(bf16[1536,128]{1,0:T(8,128)(2,1)S(1)} %pass_on.3), channel_id=1, source_target_pairs={{0,8},{1,9},{2,10},{3,11},{4,12},{5,13},{6,14},{7,15},{8,0},{9,1},... | collective-permute-start | bytes 1179656 | tf_op jit(solution)/shard_map/ppermute | solution.py:367
  49.5 7.2 %collective-permute-start.11 = (bf16[768,128]{1,0:T(8,128)(2,1)S(1)}, bf16[768,128]{1,0:T(8,128)(2,1)S(1)}, u32[]{:S(2)}, u32[]{:S(2)}) collective-permute-start(bf16[768,128]{1,0:T(8,128)(2,1)S(1)} %get-tuple-element.49), channel_id=1, source_target_pairs={{0,12},{1,13},{2,14},{4,8},{5,9},{6,10},{7,11},{8,4},{9,5},{11,7},... | collective-permute-start | bytes 589832 | tf_op jit(solution)/shard_map/ppermute | solution.py:372
  56.6 3.1 %collective-permute-start.6 = (bf16[768,128]{1,0:T(8,128)(2,1)S(1)}, bf16[768,128]{1,0:T(8,128)(2,1)S(1)}, u32[]{:S(2)}, u32[]{:S(2)}) collective-permute-start(bf16[768,128]{1,0:T(8,128)(2,1)S(1)} %get-tuple-element.43), channel_id=1, source_target_pairs={{0,3},{1,4},{2,5},{4,7},{5,0},{7,2},{8,11},{9,12},{10,13},{11,14},... | collective-permute-start | bytes 589832 | tf_op jit(solution)/shard_map/ppermute | solution.py:372
  59.7 12.0 %collective-permute-start.7 = (bf16[768,128]{1,0:T(8,128)(2,1)S(1)}, bf16[768,128]{1,0:T(8,128)(2,1)S(1)}, u32[]{:S(2)}, u32[]{:S(2)}) collective-permute-start(bf16[768,128]{1,0:T(8,128)(2,1)S(1)} %get-tuple-element.44), channel_id=1, source_target_pairs={{0,5},{2,7},{3,0},{5,2},{6,3},{7,4},{8,13},{9,14},{11,8},{12,9},{1... | collective-permute-start | bytes 589832 | tf_op jit(solution)/shard_map/ppermute | solution.py:372
  72.0 4.3 %collective-permute-done.6.refs_2_ = bf16[768,128]{1,0:T(8,128)(2,1)S(1)} collective-permute-done((bf16[768,128]{1,0:T(8,128)(2,1)S(1)}, bf16[768,128]{1,0:T(8,128)(2,1)S(1)}, u32[]{:S(2)}, u32[]{:S(2)}) %collective-permute-start.6) | collective-permute-done | bytes 196640 | tf_op jit(solution)/shard_map/ppermute | solution.py:372
  76.3 2.5 %collective-permute-done.7.refs_3_ = bf16[768,128]{1,0:T(8,128)(2,1)S(1)} collective-permute-done((bf16[768,128]{1,0:T(8,128)(2,1)S(1)}, bf16[768,128]{1,0:T(8,128)(2,1)S(1)}, u32[]{:S(2)}, u32[]{:S(2)}) %collective-permute-start.7) | collective-permute-done | bytes 196640 | tf_op jit(solution)/shard_map/ppermute | solution.py:372
  79.0 5.5 %attend.6 = (f32[4,128,512]{2,1,0:T(8,128)S(1)}, f32[4,8,512]{2,1,0:T(8,128)S(1)}, f32[4,8,512]{2,1,0:T(8,128)S(1)}) custom-call(bf16[4,256,128]{2,1,0:T(8,128)(2,1)S(1)} %get-tuple-element.39.refs_0_, bf16[4,256,128]{2,1,0:T(8,128)(2,1)S(1)} %get-tuple-element.42.refs_1_, bf16[1024,128]{1,0:T(8,128)(2,1)S(1)} %get-tuple-element.51.refs_2_.refs_3_.refs_4_, ...), custom_call_target="tpu_custom_call" | custom-call | flops 2147483648 | bytes 1572864 | tf_op jit(solution)/shard_map/attend/pallas_call | solution.py:259
  84.6 2.0 %attend.7 = (f32[1,128,768]{2,1,0:T(8,128)S(1)}, f32[1,8,768]{2,1,0:T(8,128)S(1)}, f32[1,8,768]{2,1,0:T(8,128)S(1)}) custom-call(bf16[4,256,128]{2,1,0:T(8,128)(2,1)S(1)} %get-tuple-element.39.refs_0_, bf16[4,256,128]{2,1,0:T(8,128)(2,1)S(1)} %get-tuple-element.42.refs_1_, bf16[4,256,128]{2,1,0:T(8,128)(2,1)S(1)} %get-tuple-element.45.refs_2_, ...), custom_call_target="tpu_custom_call" | custom-call | flops 671088640 | bytes 2359296 | tf_op jit(solution)/shard_map/attend/pallas_call | solution.py:259
  86.6 3.6 %attend.9 = bf16[1024,128]{1,0:T(8,128)(2,1)S(1)} custom-call(bf16[4,256,128]{2,1,0:T(8,128)(2,1)S(1)} %get-tuple-element.39.refs_0_, bf16[4,256,128]{2,1,0:T(8,128)(2,1)S(1)} %get-tuple-element.42.refs_1_, bf16[4,256,128]{2,1,0:T(8,128)(2,1)S(1)} %get-tuple-element.45.refs_2_, bf16[4,256,128]{2,1,0:T(8,128)(2,1)S(1)} %get-tuple-element.50.refs_3_, ...), custom_call_target="tpu_custom_call" | custom-call | flops 1610612736 | bytes 3145728 | tf_op jit(solution)/shard_map/attend/pallas_call | solution.py:259
  90.2 3.9 %attend.10 = bf16[1024,128]{1,0:T(8,128)(2,1)S(1)} custom-call(bf16[4,256,128]{2,1,0:T(8,128)(2,1)S(1)} %get-tuple-element.39.refs_0_, bf16[4,256,128]{2,1,0:T(8,128)(2,1)S(1)} %get-tuple-element.42.refs_1_, bf16[4,256,128]{2,1,0:T(8,128)(2,1)S(1)} %get-tuple-element.45.refs_2_, bf16[4,256,128]{2,1,0:T(8,128)(2,1)S(1)} %get-tuple-element.50.refs_3_, ...), custom_call_target="tpu_custom_call" | custom-call | flops 1610612736 | bytes 3145728 | tf_op jit(solution)/shard_map/attend/pallas_call | solution.py:259
  94.1 2.6 %attend.8 = bf16[1024,128]{1,0:T(8,128)(2,1)S(1)} custom-call(bf16[4,256,128]{2,1,0:T(8,128)(2,1)S(1)} %get-tuple-element.39.refs_0_, bf16[4,256,128]{2,1,0:T(8,128)(2,1)S(1)} %get-tuple-element.42.refs_1_, bf16[4,256,128]{2,1,0:T(8,128)(2,1)S(1)} %get-tuple-element.45.refs_2_, bf16[4,256,128]{2,1,0:T(8,128)(2,1)S(1)} %get-tuple-element.50.refs_3_, ...), custom_call_target="tpu_custom_call" | custom-call | flops 939524096 | bytes 3145728 | tf_op jit(solution)/shard_map/attend/pallas_call | solution.py:259
  96.7 6.2 %collective-permute-start.12 = (bf16[1024,128]{1,0:T(8,128)(2,1)S(1)}, bf16[1024,128]{1,0:T(8,128)(2,1)S(1)}, u32[]{:S(2)}, u32[]{:S(2)}) collective-permute-start(bf16[1024,128]{1,0:T(8,128)(2,1)S(1)} %attend.8), channel_id=1, source_target_pairs={{0,12},{2,14},{3,15},{4,8},{5,9},{7,11},{8,4},{9,5},{10,6},{11,7},... | collective-permute-start | bytes 786440 | tf_op jit(solution)/shard_map/ppermute | solution.py:387
  102.9 4.5 %collective-permute-start.13 = (bf16[1024,128]{1,0:T(8,128)(2,1)S(1)}, bf16[1024,128]{1,0:T(8,128)(2,1)S(1)}, u32[]{:S(2)}, u32[]{:S(2)}) collective-permute-start(bf16[1024,128]{1,0:T(8,128)(2,1)S(1)} %attend.9), channel_id=1, source_target_pairs={{0,4},{2,6},{3,7},{4,0},{5,1},{7,3},{8,12},{9,13},{10,14},{11,15},... | collective-permute-start | bytes 786440 | tf_op jit(solution)/shard_map/ppermute | solution.py:387
  107.4 3.9 %collective-permute-start.14 = (bf16[1024,128]{1,0:T(8,128)(2,1)S(1)}, bf16[1024,128]{1,0:T(8,128)(2,1)S(1)}, u32[]{:S(2)}, u32[]{:S(2)}) collective-permute-start(bf16[1024,128]{1,0:T(8,128)(2,1)S(1)} %attend.10), channel_id=1, source_target_pairs={{0,8},{2,10},{3,11},{4,12},{5,13},{7,15},{8,0},{9,1},{10,2},{11,3}... | collective-permute-start | bytes 786440 | tf_op jit(solution)/shard_map/ppermute | solution.py:387
  111.3 3.6 %attend.11.refs_3_ = bf16[1024,128]{1,0:T(8,128)(2,1)S(1)} custom-call(bf16[4,256,128]{2,1,0:T(8,128)(2,1)S(1)} %get-tuple-element.39.refs_0_, bf16[4,256,128]{2,1,0:T(8,128)(2,1)S(1)} %get-tuple-element.42.refs_1_, bf16[4,256,128]{2,1,0:T(8,128)(2,1)S(1)} %get-tuple-element.45.refs_2_, bf16[4,256,128]{2,1,0:T(8,128)(2,1)S(1)} %get-tuple-element.50.refs_3_, ...), custom_call_target="tpu_custom_call" | custom-call | flops 1610612736 | bytes 3145728 | tf_op jit(solution)/shard_map/attend/pallas_call | solution.py:259
  115.0 6.1 %collective-permute-done.13.refs_1_ = bf16[1024,128]{1,0:T(8,128)(2,1)S(1)} collective-permute-done((bf16[1024,128]{1,0:T(8,128)(2,1)S(1)}, bf16[1024,128]{1,0:T(8,128)(2,1)S(1)}, u32[]{:S(2)}, u32[]{:S(2)}) %collective-permute-start.13) | collective-permute-done | bytes 262176 | tf_op jit(solution)/shard_map/ppermute | solution.py:387
  121.0 0.4 last_head.1
  121.5 7.2 %collective-permute-start.15 = (bf16[96,1024]{1,0:T(8,128)(2,1)S(1)}, bf16[96,1024]{1,0:T(8,128)(2,1)S(1)}, u32[]{:S(2)}, u32[]{:S(2)}) collective-permute-start(bf16[96,1024]{1,0:T(8,128)(2,1)S(1)} %last_head.1), channel_id=1, source_target_pairs={{0,1},{1,2},{2,3},{3,4},{4,5},{5,6},{6,7},{7,0},{8,9},{9,10},{10,1... | collective-permute-start | bytes 589832 | tf_op jit(solution)/shard_map/ppermute | solution.py:389
  128.7 1.6 %merge.1.refs_5_ = bf16[416,1024]{1,0:T(8,128)(2,1)} custom-call(bf16[1024,128]{1,0:T(8,128)(2,1)S(1)} %collective-permute-done.12.refs_0_, bf16[1024,128]{1,0:T(8,128)(2,1)S(1)} %collective-permute-done.13.refs_1_, bf16[1024,128]{1,0:T(8,128)(2,1)S(1)} %collective-permute-done.14.refs_2_, bf16[1024,128]{1,0:T(8,128)(2,1)S(1)} %attend.11.refs_3_), custom_call_target="tpu_custom_call" | custom-call | tf_op jit(solution)/shard_map/merge/pallas_call | solution.py:321
  130.3 2.0 %collective-permute-done.15.refs_4_ = bf16[96,1024]{1,0:T(8,128)(2,1)S(1)} collective-permute-done((bf16[96,1024]{1,0:T(8,128)(2,1)S(1)}, bf16[96,1024]{1,0:T(8,128)(2,1)S(1)}, u32[]{:S(2)}, u32[]{:S(2)}) %collective-permute-start.15) | collective-permute-done | bytes 196640 | tf_op jit(solution)/shard_map/ppermute | solution.py:389
  132.3 1.2 finish.1
  (16 shorter events, 0.7 us)
Async XLA Ops:
  2.2 16.4 %collective-permute-start = (bf16[1536,128]{1,0:T(8,128)(2,1)S(1)}, bf16[1536,128]{1,0:T(8,128)(2,1)S(1)}, u32[]{:S(2)}, u32[]{:S(2)}) collective-permute-start(bf16[1536,128]{1,0:T(8,128)(2,1)S(1)} %get-tuple-element.36), channel_id=1, source_target_pairs={{0,1},{1,2},{2,3},{3,4},{4,5},{5,6},{6,7},{7,0},{8,9},{9,10},{10,1... | collective-permute-start | bytes 1179656 | tf_op jit(solution)/shard_map/ppermute | solution.py:364
  4.2 19.1 %collective-permute-start.1 = (bf16[1536,128]{1,0:T(8,128)(2,1)S(1)}, bf16[1536,128]{1,0:T(8,128)(2,1)S(1)}, u32[]{:S(2)}, u32[]{:S(2)}) collective-permute-start(bf16[1536,128]{1,0:T(8,128)(2,1)S(1)} %get-tuple-element.37), channel_id=1, source_target_pairs={{0,7},{1,0},{2,1},{3,2},{4,3},{5,4},{6,5},{7,6},{8,15},{9,8},{10,9... | collective-permute-start | bytes 1179656 | tf_op jit(solution)/shard_map/ppermute | solution.py:364
  8.2 32.4 %collective-permute-start.2 = (bf16[1536,128]{1,0:T(8,128)(2,1)S(1)}, bf16[1536,128]{1,0:T(8,128)(2,1)S(1)}, u32[]{:S(2)}, u32[]{:S(2)}) collective-permute-start(bf16[1536,128]{1,0:T(8,128)(2,1)S(1)} %get-tuple-element.38), channel_id=1, source_target_pairs={{0,2},{1,3},{2,4},{3,5},{4,6},{5,7},{6,0},{7,1},{8,10},{9,11},{10,... | collective-permute-start | bytes 1179656 | tf_op jit(solution)/shard_map/ppermute | solution.py:364
  8.2 39.2 %collective-permute-start.3 = (bf16[1536,128]{1,0:T(8,128)(2,1)S(1)}, bf16[1536,128]{1,0:T(8,128)(2,1)S(1)}, u32[]{:S(2)}, u32[]{:S(2)}) collective-permute-start(bf16[1536,128]{1,0:T(8,128)(2,1)S(1)} %get-tuple-element.40), channel_id=1, source_target_pairs={{0,6},{1,7},{2,0},{3,1},{4,2},{5,3},{6,4},{7,5},{8,14},{9,15},{10,... | collective-permute-start | bytes 1179656 | tf_op jit(solution)/shard_map/ppermute | solution.py:364
  23.4 55.5 %collective-permute-start.4 = (bf16[2304,128]{1,0:T(8,128)(2,1)S(1)}, bf16[2304,128]{1,0:T(8,128)(2,1)S(1)}, u32[]{:S(2)}, u32[]{:S(2)}) collective-permute-start(bf16[2304,128]{1,0:T(8,128)(2,1)S(1)} %pass_on.2), channel_id=1, source_target_pairs={{0,8},{1,9},{2,10},{3,11},{4,12},{5,13},{6,14},{7,15},{8,0},{9,1},... | collective-permute-start | bytes 1769480 | tf_op jit(solution)/shard_map/ppermute | solution.py:367
  25.4 24.0 %collective-permute-start.8 = (bf16[768,128]{1,0:T(8,128)(2,1)S(1)}, bf16[768,128]{1,0:T(8,128)(2,1)S(1)}, u32[]{:S(2)}, u32[]{:S(2)}) collective-permute-start(bf16[768,128]{1,0:T(8,128)(2,1)S(1)} %get-tuple-element.46), channel_id=1, source_target_pairs={{0,11},{1,12},{2,13},{3,14},{5,8},{6,9},{7,10},{8,3},{9,4},{10,5},... | collective-permute-start | bytes 589832 | tf_op jit(solution)/shard_map/ppermute | solution.py:372
  36.7 19.9 %collective-permute-start.9 = (bf16[768,128]{1,0:T(8,128)(2,1)S(1)}, bf16[768,128]{1,0:T(8,128)(2,1)S(1)}, u32[]{:S(2)}, u32[]{:S(2)}) collective-permute-start(bf16[768,128]{1,0:T(8,128)(2,1)S(1)} %get-tuple-element.47), channel_id=1, source_target_pairs={{0,13},{1,14},{3,8},{4,9},{5,10},{6,11},{7,12},{8,5},{10,7},{11,0}... | collective-permute-start | bytes 589832 | tf_op jit(solution)/shard_map/ppermute | solution.py:372
  40.6 19.1 %collective-permute-start.10 = (bf16[768,128]{1,0:T(8,128)(2,1)S(1)}, bf16[768,128]{1,0:T(8,128)(2,1)S(1)}, u32[]{:S(2)}, u32[]{:S(2)}) collective-permute-start(bf16[768,128]{1,0:T(8,128)(2,1)S(1)} %get-tuple-element.48), channel_id=1, source_target_pairs={{0,4},{1,5},{3,7},{4,0},{6,2},{7,3},{8,12},{9,13},{10,14},{12,8},{... | collective-permute-start | bytes 589832 | tf_op jit(solution)/shard_map/ppermute | solution.py:372
  47.5 31.3 %collective-permute-start.5 = (bf16[1536,128]{1,0:T(8,128)(2,1)S(1)}, bf16[1536,128]{1,0:T(8,128)(2,1)S(1)}, u32[]{:S(2)}, u32[]{:S(2)}) collective-permute-start(bf16[1536,128]{1,0:T(8,128)(2,1)S(1)} %pass_on.3), channel_id=1, source_target_pairs={{0,8},{1,9},{2,10},{3,11},{4,12},{5,13},{6,14},{7,15},{8,0},{9,1},... | collective-permute-start | bytes 1179656 | tf_op jit(solution)/shard_map/ppermute | solution.py:367
  49.5 22.3 %collective-permute-start.11 = (bf16[768,128]{1,0:T(8,128)(2,1)S(1)}, bf16[768,128]{1,0:T(8,128)(2,1)S(1)}, u32[]{:S(2)}, u32[]{:S(2)}) collective-permute-start(bf16[768,128]{1,0:T(8,128)(2,1)S(1)} %get-tuple-element.49), channel_id=1, source_target_pairs={{0,12},{1,13},{2,14},{4,8},{5,9},{6,10},{7,11},{8,4},{9,5},{11,7},... | collective-permute-start | bytes 589832 | tf_op jit(solution)/shard_map/ppermute | solution.py:372
  56.6 19.7 %collective-permute-start.6 = (bf16[768,128]{1,0:T(8,128)(2,1)S(1)}, bf16[768,128]{1,0:T(8,128)(2,1)S(1)}, u32[]{:S(2)}, u32[]{:S(2)}) collective-permute-start(bf16[768,128]{1,0:T(8,128)(2,1)S(1)} %get-tuple-element.43), channel_id=1, source_target_pairs={{0,3},{1,4},{2,5},{4,7},{5,0},{7,2},{8,11},{9,12},{10,13},{11,14},... | collective-permute-start | bytes 589832 | tf_op jit(solution)/shard_map/ppermute | solution.py:372
  59.7 19.1 %collective-permute-start.7 = (bf16[768,128]{1,0:T(8,128)(2,1)S(1)}, bf16[768,128]{1,0:T(8,128)(2,1)S(1)}, u32[]{:S(2)}, u32[]{:S(2)}) collective-permute-start(bf16[768,128]{1,0:T(8,128)(2,1)S(1)} %get-tuple-element.44), channel_id=1, source_target_pairs={{0,5},{2,7},{3,0},{5,2},{6,3},{7,4},{8,13},{9,14},{11,8},{12,9},{1... | collective-permute-start | bytes 589832 | tf_op jit(solution)/shard_map/ppermute | solution.py:372
  96.7 18.3 %collective-permute-start.12 = (bf16[1024,128]{1,0:T(8,128)(2,1)S(1)}, bf16[1024,128]{1,0:T(8,128)(2,1)S(1)}, u32[]{:S(2)}, u32[]{:S(2)}) collective-permute-start(bf16[1024,128]{1,0:T(8,128)(2,1)S(1)} %attend.8), channel_id=1, source_target_pairs={{0,12},{2,14},{3,15},{4,8},{5,9},{7,11},{8,4},{9,5},{10,6},{11,7},... | collective-permute-start | bytes 786440 | tf_op jit(solution)/shard_map/ppermute | solution.py:387
  102.9 18.2 %collective-permute-start.13 = (bf16[1024,128]{1,0:T(8,128)(2,1)S(1)}, bf16[1024,128]{1,0:T(8,128)(2,1)S(1)}, u32[]{:S(2)}, u32[]{:S(2)}) collective-permute-start(bf16[1024,128]{1,0:T(8,128)(2,1)S(1)} %attend.9), channel_id=1, source_target_pairs={{0,4},{2,6},{3,7},{4,0},{5,1},{7,3},{8,12},{9,13},{10,14},{11,15},... | collective-permute-start | bytes 786440 | tf_op jit(solution)/shard_map/ppermute | solution.py:387
  107.4 13.7 %collective-permute-start.14 = (bf16[1024,128]{1,0:T(8,128)(2,1)S(1)}, bf16[1024,128]{1,0:T(8,128)(2,1)S(1)}, u32[]{:S(2)}, u32[]{:S(2)}) collective-permute-start(bf16[1024,128]{1,0:T(8,128)(2,1)S(1)} %attend.10), channel_id=1, source_target_pairs={{0,8},{2,10},{3,11},{4,12},{5,13},{7,15},{8,0},{9,1},{10,2},{11,3}... | collective-permute-start | bytes 786440 | tf_op jit(solution)/shard_map/ppermute | solution.py:387
  121.5 10.8 %collective-permute-start.15 = (bf16[96,1024]{1,0:T(8,128)(2,1)S(1)}, bf16[96,1024]{1,0:T(8,128)(2,1)S(1)}, u32[]{:S(2)}, u32[]{:S(2)}) collective-permute-start(bf16[96,1024]{1,0:T(8,128)(2,1)S(1)} %last_head.1), channel_id=1, source_target_pairs={{0,1},{1,2},{2,3},{3,4},{4,5},{5,6},{6,7},{7,0},{8,9},{9,10},{10,1... | collective-permute-start | bytes 589832 | tf_op jit(solution)/shard_map/ppermute | solution.py:389

commit v7 on v6

--- a/solution.py
+++ b/solution.py
@@ -310,10 +310,12 @@
 
 
 def merge_kernel(*refs):
-    blocks, out_ref = refs[:4], refs[4]
+    blocks, out_ref, top_ref = refs[:4], refs[4], refs[5]
     rows = out_ref.shape[1]
     at = pl.ds(pl.multiple_of(pl.program_id(0) * rows, rows), rows)
-    out_ref[...] = own_rows([ref[at, :] for ref in blocks], OUT_COLS).astype(jnp.bfloat16)
+    out = own_rows([ref[at, :] for ref in blocks], OUT_COLS).astype(jnp.bfloat16)
+    out_ref[...] = out
+    top_ref[...] = out[:SPLIT]
 
 
 def merge(blocks):
@@ -322,36 +324,35 @@
         merge_kernel,
         grid=(2,),
         in_specs=[vmem()] * 4,
-        out_specs=pl.BlockSpec((OUT_COLS, rows // 2), lambda i: (0, i)),
-        out_shape=jax.ShapeDtypeStruct((OUT_COLS, rows), jnp.bfloat16),
+        out_specs=[pl.BlockSpec((n, rows // 2), lambda i: (0, i)) for n in (OUT_COLS, SPLIT)],
+        out_shape=[jax.ShapeDtypeStruct((n, rows), jnp.bfloat16) for n in (OUT_COLS, SPLIT)],
         compiler_params=pltpu.CompilerParams(vmem_limit_bytes=16 * 2**20),
         name="merge",
     )(*blocks)
 
 
 def finish_kernel(*refs):
-    blocks, split, out_ref = refs[:4], refs[4], refs[6]
+    top, split, _, out_ref = refs
     chunk = lax.axis_index("seq") % 4
-    row = lax.broadcasted_iota(jnp.int32, (HEAD_DIM, SPLIT), 0)
-    col = lax.broadcasted_iota(jnp.int32, (HEAD_DIM, SPLIT), 1)
+    row = lax.broadcasted_iota(jnp.int32, (SPLIT, SPLIT), 0)
+    col = lax.broadcasted_iota(jnp.int32, (SPLIT, SPLIT), 1)
     taken = jnp.where((row == col + 32 - 32 * chunk) & (chunk > 0), 1.0, 0.0).astype(jnp.bfloat16)
-    out = own_rows([ref[...] for ref in blocks], HEAD_DIM) + jnp.dot(taken, split[...],
-                                                                     preferred_element_type=jnp.float32)
+    out = top[...].astype(jnp.float32) + jnp.dot(taken, split[...], preferred_element_type=jnp.float32)
     out_ref[...] = out.astype(jnp.bfloat16)
 
 
-def finish(blocks, split, merged):
+def finish(top, split, merged):
     rows = SEQ * LOC
     return pl.pallas_call(
         finish_kernel,
         grid=(1,),
-        in_specs=[vmem()] * 5 + [pl.BlockSpec(memory_space=pltpu.HBM)],
-        out_specs=pl.BlockSpec((HEAD_DIM, rows), lambda i: (0, 0)),
+        in_specs=[vmem()] * 2 + [pl.BlockSpec(memory_space=pltpu.HBM)],
+        out_specs=pl.BlockSpec((SPLIT, rows), lambda i: (0, 0)),
         out_shape=jax.ShapeDtypeStruct((OUT_COLS, rows), jnp.bfloat16),
-        input_output_aliases={5: 0},
+        input_output_aliases={2: 0},
         compiler_params=pltpu.CompilerParams(vmem_limit_bytes=16 * 2**20),
         name="finish",
-    )(*blocks, split, merged).T
+    )(top, split, merged).T
 
 
 def exchange_and_attend(queries, key_rows, value_rows):
@@ -387,8 +388,8 @@
             out = lax.ppermute(out, axes, perm)
         blocks.append(out)
     split = lax.ppermute(last_head(blocks), axes, pairs(lambda s: turn(s, (0, 1)), lambda core, s, t: True))
-    merged = merge(blocks)
-    return finish(blocks, split, merged)
+    merged, top = merge(blocks)
+    return finish(top, split, merged)
 
 
 def solution(mesh):

time: 136 us -> 135 us (level)
  no operation moved by 1% of the time
where the time goes in v7:
time: 135 us; the launch traced here: 133 us
  starting transfers between devices  78.2 us (58%)
  waiting for transfers between devices  27.9 us (21%)
  Pallas kernels  27 us (20%)
    ppermute x6, starting transfers between devices, exchange_and_attend(): parts[r] = (lax.ppermute(messages[r - 4], axes, perm), 0)  42.2 us
    pallas_call x6, Pallas kernels, attend(): pl.pallas_call(lambda *refs: attend_kernel(stages, count, known, flips, s...  21.3 us
    ppermute x3, starting transfers between devices, exchange_and_attend(): out = lax.ppermute(out, axes, perm)  14.6 us
    ppermute x4, waiting for transfers between devices, exchange_and_attend(): lax.ppermute(messages[r], axes, pairs(lambda s: turn(s, ROTATIONS[r]), ev...  12.9 us
    ppermute x4, starting transfers between devices, exchange_and_attend(): lax.ppermute(messages[r], axes, pairs(lambda s: turn(s, ROTATIONS[r]), ev...  10.2 us
    ppermute x1, starting transfers between devices, exchange_and_attend(): lax.ppermute(last_head(blocks), axes, pairs(lambda s: turn(s, (0, 1)), la...  7.2 us
    ppermute x6, waiting for transfers between devices, exchange_and_attend(): parts[r] = (lax.ppermute(messages[r - 4], axes, perm), 0)  6.9 us
    ppermute x3, waiting for transfers between devices, exchange_and_attend(): out = lax.ppermute(out, axes, perm)  6.06 us
  transfers between devices with their start and end apart: 16, of which 8 were waited for; matrix products, arithmetic and copies ran while one was open for 0% of the time, Pallas kernels for 4%

profile of v7, /device:TPU:16, one launch (start us, length us, event | category | flops | bytes accessed | tf_op | source)
XLA Modules:
  0.0 133.2 jit_solution(14697946063381828847)
XLA Ops:
  0.0 2.2 %pack.1 = (bf16[768,128]{1,0:T(8,128)(2,1)S(1)}, bf16[1536,128]{1,0:T(8,128)(2,1)S(1)}, bf16[1536,128]{1,0:T(8,128)(2,1)S(1)}, bf16[1536,128]{1,0:T(8,128)(2,1)S...) custom-call(bf16[256,1664]{1,0:T(8,128)(2,1)} %q_ref.1, ...), custom_call_target="tpu_custom_call" | custom-call | tf_op jit(solution)/shard_map/pack/pallas_call | solution.py:125
  2.2 2.0 %collective-permute-start = (bf16[1536,128]{1,0:T(8,128)(2,1)S(1)}, bf16[1536,128]{1,0:T(8,128)(2,1)S(1)}, u32[]{:S(2)}, u32[]{:S(2)}) collective-permute-start(bf16[1536,128]{1,0:T(8,128)(2,1)S(1)} %get-tuple-element.38), channel_id=1, source_target_pairs={{0,1},{1,2},{2,3},{3,4},{4,5},{5,6},{6,7},{7,0},{8,9},{9,10},{10,1... | collective-permute-start | bytes 1179656 | tf_op jit(solution)/shard_map/ppermute | solution.py:365
  4.2 4.0 %collective-permute-start.1 = (bf16[1536,128]{1,0:T(8,128)(2,1)S(1)}, bf16[1536,128]{1,0:T(8,128)(2,1)S(1)}, u32[]{:S(2)}, u32[]{:S(2)}) collective-permute-start(bf16[1536,128]{1,0:T(8,128)(2,1)S(1)} %get-tuple-element.39), channel_id=1, source_target_pairs={{0,7},{1,0},{2,1},{3,2},{4,3},{5,4},{6,5},{7,6},{8,15},{9,8},{10,9... | collective-permute-start | bytes 1179656 | tf_op jit(solution)/shard_map/ppermute | solution.py:365
  8.2 4.1 %collective-permute-start.3 = (bf16[1536,128]{1,0:T(8,128)(2,1)S(1)}, bf16[1536,128]{1,0:T(8,128)(2,1)S(1)}, u32[]{:S(2)}, u32[]{:S(2)}) collective-permute-start(bf16[1536,128]{1,0:T(8,128)(2,1)S(1)} %get-tuple-element.42), channel_id=1, source_target_pairs={{0,6},{1,7},{2,0},{3,1},{4,2},{5,3},{6,4},{7,5},{8,14},{9,15},{10,... | collective-permute-start | bytes 1179656 | tf_op jit(solution)/shard_map/ppermute | solution.py:365
  12.4 6.2 %collective-permute-done.refs_1_ = bf16[1536,128]{1,0:T(8,128)(2,1)S(1)} collective-permute-done((bf16[1536,128]{1,0:T(8,128)(2,1)S(1)}, bf16[1536,128]{1,0:T(8,128)(2,1)S(1)}, u32[]{:S(2)}, u32[]{:S(2)}) %collective-permute-start) | collective-permute-done | bytes 393248 | tf_op jit(solution)/shard_map/ppermute | solution.py:365
  18.6 4.7 %collective-permute-done.1.refs_2_ = bf16[1536,128]{1,0:T(8,128)(2,1)S(1)} collective-permute-done((bf16[1536,128]{1,0:T(8,128)(2,1)S(1)}, bf16[1536,128]{1,0:T(8,128)(2,1)S(1)}, u32[]{:S(2)}, u32[]{:S(2)}) %collective-permute-start.1) | collective-permute-done | bytes 393248 | tf_op jit(solution)/shard_map/ppermute | solution.py:365
  23.4 2.1 %collective-permute-start.4 = (bf16[2304,128]{1,0:T(8,128)(2,1)S(1)}, bf16[2304,128]{1,0:T(8,128)(2,1)S(1)}, u32[]{:S(2)}, u32[]{:S(2)}) collective-permute-start(bf16[2304,128]{1,0:T(8,128)(2,1)S(1)} %pass_on.2), channel_id=1, source_target_pairs={{0,8},{1,9},{2,10},{3,11},{4,12},{5,13},{6,14},{7,15},{8,0},{9,1},... | collective-permute-start | bytes 1769480 | tf_op jit(solution)/shard_map/ppermute | solution.py:368
  25.4 11.3 %collective-permute-start.8 = (bf16[768,128]{1,0:T(8,128)(2,1)S(1)}, bf16[768,128]{1,0:T(8,128)(2,1)S(1)}, u32[]{:S(2)}, u32[]{:S(2)}) collective-permute-start(bf16[768,128]{1,0:T(8,128)(2,1)S(1)} %get-tuple-element.48), channel_id=1, source_target_pairs={{0,11},{1,12},{2,13},{3,14},{5,8},{6,9},{7,10},{8,3},{9,4},{10,5},... | collective-permute-start | bytes 589832 | tf_op jit(solution)/shard_map/ppermute | solution.py:373
  36.7 1.9 %collective-permute-start.9 = (bf16[768,128]{1,0:T(8,128)(2,1)S(1)}, bf16[768,128]{1,0:T(8,128)(2,1)S(1)}, u32[]{:S(2)}, u32[]{:S(2)}) collective-permute-start(bf16[768,128]{1,0:T(8,128)(2,1)S(1)} %get-tuple-element.49), channel_id=1, source_target_pairs={{0,13},{1,14},{3,8},{4,9},{5,10},{6,11},{7,12},{8,5},{10,7},{11,0}... | collective-permute-start | bytes 589832 | tf_op jit(solution)/shard_map/ppermute | solution.py:373
  38.7 2.0 %collective-permute-done.2.refs_3_.refs_0_ = bf16[1536,128]{1,0:T(8,128)(2,1)S(1)} collective-permute-done((bf16[1536,128]{1,0:T(8,128)(2,1)S(1)}, bf16[1536,128]{1,0:T(8,128)(2,1)S(1)}, u32[]{:S(2)}, u32[]{:S(2)}) %collective-permute-start.2) | collective-permute-done | bytes 393248 | tf_op jit(solution)/shard_map/ppermute | solution.py:365
  40.6 6.8 %collective-permute-start.10 = (bf16[768,128]{1,0:T(8,128)(2,1)S(1)}, bf16[768,128]{1,0:T(8,128)(2,1)S(1)}, u32[]{:S(2)}, u32[]{:S(2)}) collective-permute-start(bf16[768,128]{1,0:T(8,128)(2,1)S(1)} %get-tuple-element.50), channel_id=1, source_target_pairs={{0,4},{1,5},{3,7},{4,0},{6,2},{7,3},{8,12},{9,13},{10,14},{12,8},{... | collective-permute-start | bytes 589832 | tf_op jit(solution)/shard_map/ppermute | solution.py:373
  47.5 1.9 %collective-permute-start.5 = (bf16[1536,128]{1,0:T(8,128)(2,1)S(1)}, bf16[1536,128]{1,0:T(8,128)(2,1)S(1)}, u32[]{:S(2)}, u32[]{:S(2)}) collective-permute-start(bf16[1536,128]{1,0:T(8,128)(2,1)S(1)} %pass_on.3), channel_id=1, source_target_pairs={{0,8},{1,9},{2,10},{3,11},{4,12},{5,13},{6,14},{7,15},{8,0},{9,1},... | collective-permute-start | bytes 1179656 | tf_op jit(solution)/shard_map/ppermute | solution.py:368
  49.5 7.2 %collective-permute-start.11 = (bf16[768,128]{1,0:T(8,128)(2,1)S(1)}, bf16[768,128]{1,0:T(8,128)(2,1)S(1)}, u32[]{:S(2)}, u32[]{:S(2)}) collective-permute-start(bf16[768,128]{1,0:T(8,128)(2,1)S(1)} %get-tuple-element.51), channel_id=1, source_target_pairs={{0,12},{1,13},{2,14},{4,8},{5,9},{6,10},{7,11},{8,4},{9,5},{11,7},... | collective-permute-start | bytes 589832 | tf_op jit(solution)/shard_map/ppermute | solution.py:373
  56.6 3.1 %collective-permute-start.6 = (bf16[768,128]{1,0:T(8,128)(2,1)S(1)}, bf16[768,128]{1,0:T(8,128)(2,1)S(1)}, u32[]{:S(2)}, u32[]{:S(2)}) collective-permute-start(bf16[768,128]{1,0:T(8,128)(2,1)S(1)} %get-tuple-element.45), channel_id=1, source_target_pairs={{0,3},{1,4},{2,5},{4,7},{5,0},{7,2},{8,11},{9,12},{10,13},{11,14},... | collective-permute-start | bytes 589832 | tf_op jit(solution)/shard_map/ppermute | solution.py:373
  59.7 12.0 %collective-permute-start.7 = (bf16[768,128]{1,0:T(8,128)(2,1)S(1)}, bf16[768,128]{1,0:T(8,128)(2,1)S(1)}, u32[]{:S(2)}, u32[]{:S(2)}) collective-permute-start(bf16[768,128]{1,0:T(8,128)(2,1)S(1)} %get-tuple-element.46), channel_id=1, source_target_pairs={{0,5},{2,7},{3,0},{5,2},{6,3},{7,4},{8,13},{9,14},{11,8},{12,9},{1... | collective-permute-start | bytes 589832 | tf_op jit(solution)/shard_map/ppermute | solution.py:373
  72.0 4.3 %collective-permute-done.6.refs_2_ = bf16[768,128]{1,0:T(8,128)(2,1)S(1)} collective-permute-done((bf16[768,128]{1,0:T(8,128)(2,1)S(1)}, bf16[768,128]{1,0:T(8,128)(2,1)S(1)}, u32[]{:S(2)}, u32[]{:S(2)}) %collective-permute-start.6) | collective-permute-done | bytes 196640 | tf_op jit(solution)/shard_map/ppermute | solution.py:373
  76.3 2.5 %collective-permute-done.7.refs_3_ = bf16[768,128]{1,0:T(8,128)(2,1)S(1)} collective-permute-done((bf16[768,128]{1,0:T(8,128)(2,1)S(1)}, bf16[768,128]{1,0:T(8,128)(2,1)S(1)}, u32[]{:S(2)}, u32[]{:S(2)}) %collective-permute-start.7) | collective-permute-done | bytes 196640 | tf_op jit(solution)/shard_map/ppermute | solution.py:373
  79.0 5.5 %attend.6 = (f32[4,128,512]{2,1,0:T(8,128)S(1)}, f32[4,8,512]{2,1,0:T(8,128)S(1)}, f32[4,8,512]{2,1,0:T(8,128)S(1)}) custom-call(bf16[4,256,128]{2,1,0:T(8,128)(2,1)S(1)} %get-tuple-element.41.refs_0_, bf16[4,256,128]{2,1,0:T(8,128)(2,1)S(1)} %get-tuple-element.44.refs_1_, bf16[1024,128]{1,0:T(8,128)(2,1)S(1)} %get-tuple-element.53.refs_2_.refs_3_.refs_4_, ...), custom_call_target="tpu_custom_call" | custom-call | flops 2147483648 | bytes 1572864 | tf_op jit(solution)/shard_map/attend/pallas_call | solution.py:259
  84.6 2.0 %attend.7 = (f32[1,128,768]{2,1,0:T(8,128)S(1)}, f32[1,8,768]{2,1,0:T(8,128)S(1)}, f32[1,8,768]{2,1,0:T(8,128)S(1)}) custom-call(bf16[4,256,128]{2,1,0:T(8,128)(2,1)S(1)} %get-tuple-element.41.refs_0_, bf16[4,256,128]{2,1,0:T(8,128)(2,1)S(1)} %get-tuple-element.44.refs_1_, bf16[4,256,128]{2,1,0:T(8,128)(2,1)S(1)} %get-tuple-element.47.refs_2_, ...), custom_call_target="tpu_custom_call" | custom-call | flops 671088640 | bytes 2359296 | tf_op jit(solution)/shard_map/attend/pallas_call | solution.py:259
  86.6 3.6 %attend.9 = bf16[1024,128]{1,0:T(8,128)(2,1)S(1)} custom-call(bf16[4,256,128]{2,1,0:T(8,128)(2,1)S(1)} %get-tuple-element.41.refs_0_, bf16[4,256,128]{2,1,0:T(8,128)(2,1)S(1)} %get-tuple-element.44.refs_1_, bf16[4,256,128]{2,1,0:T(8,128)(2,1)S(1)} %get-tuple-element.47.refs_2_, bf16[4,256,128]{2,1,0:T(8,128)(2,1)S(1)} %get-tuple-element.52.refs_3_, ...), custom_call_target="tpu_custom_call" | custom-call | flops 1610612736 | bytes 3145728 | tf_op jit(solution)/shard_map/attend/pallas_call | solution.py:259
  90.2 3.9 %attend.10 = bf16[1024,128]{1,0:T(8,128)(2,1)S(1)} custom-call(bf16[4,256,128]{2,1,0:T(8,128)(2,1)S(1)} %get-tuple-element.41.refs_0_, bf16[4,256,128]{2,1,0:T(8,128)(2,1)S(1)} %get-tuple-element.44.refs_1_, bf16[4,256,128]{2,1,0:T(8,128)(2,1)S(1)} %get-tuple-element.47.refs_2_, bf16[4,256,128]{2,1,0:T(8,128)(2,1)S(1)} %get-tuple-element.52.refs_3_, ...), custom_call_target="tpu_custom_call" | custom-call | flops 1610612736 | bytes 3145728 | tf_op jit(solution)/shard_map/attend/pallas_call | solution.py:259
  94.1 2.6 %attend.8 = bf16[1024,128]{1,0:T(8,128)(2,1)S(1)} custom-call(bf16[4,256,128]{2,1,0:T(8,128)(2,1)S(1)} %get-tuple-element.41.refs_0_, bf16[4,256,128]{2,1,0:T(8,128)(2,1)S(1)} %get-tuple-element.44.refs_1_, bf16[4,256,128]{2,1,0:T(8,128)(2,1)S(1)} %get-tuple-element.47.refs_2_, bf16[4,256,128]{2,1,0:T(8,128)(2,1)S(1)} %get-tuple-element.52.refs_3_, ...), custom_call_target="tpu_custom_call" | custom-call | flops 939524096 | bytes 3145728 | tf_op jit(solution)/shard_map/attend/pallas_call | solution.py:259
  96.7 6.2 %collective-permute-start.12 = (bf16[1024,128]{1,0:T(8,128)(2,1)S(1)}, bf16[1024,128]{1,0:T(8,128)(2,1)S(1)}, u32[]{:S(2)}, u32[]{:S(2)}) collective-permute-start(bf16[1024,128]{1,0:T(8,128)(2,1)S(1)} %attend.8), channel_id=1, source_target_pairs={{0,12},{2,14},{3,15},{4,8},{5,9},{7,11},{8,4},{9,5},{10,6},{11,7},... | collective-permute-start | bytes 786440 | tf_op jit(solution)/shard_map/ppermute | solution.py:388
  102.8 4.5 %collective-permute-start.13 = (bf16[1024,128]{1,0:T(8,128)(2,1)S(1)}, bf16[1024,128]{1,0:T(8,128)(2,1)S(1)}, u32[]{:S(2)}, u32[]{:S(2)}) collective-permute-start(bf16[1024,128]{1,0:T(8,128)(2,1)S(1)} %attend.9), channel_id=1, source_target_pairs={{0,4},{2,6},{3,7},{4,0},{5,1},{7,3},{8,12},{9,13},{10,14},{11,15},... | collective-permute-start | bytes 786440 | tf_op jit(solution)/shard_map/ppermute | solution.py:388
  107.4 3.9 %collective-permute-start.14 = (bf16[1024,128]{1,0:T(8,128)(2,1)S(1)}, bf16[1024,128]{1,0:T(8,128)(2,1)S(1)}, u32[]{:S(2)}, u32[]{:S(2)}) collective-permute-start(bf16[1024,128]{1,0:T(8,128)(2,1)S(1)} %attend.10), channel_id=1, source_target_pairs={{0,8},{2,10},{3,11},{4,12},{5,13},{7,15},{8,0},{9,1},{10,2},{11,3}... | collective-permute-start | bytes 786440 | tf_op jit(solution)/shard_map/ppermute | solution.py:388
  111.3 3.6 %attend.11.refs_3_ = bf16[1024,128]{1,0:T(8,128)(2,1)S(1)} custom-call(bf16[4,256,128]{2,1,0:T(8,128)(2,1)S(1)} %get-tuple-element.41.refs_0_, bf16[4,256,128]{2,1,0:T(8,128)(2,1)S(1)} %get-tuple-element.44.refs_1_, bf16[4,256,128]{2,1,0:T(8,128)(2,1)S(1)} %get-tuple-element.47.refs_2_, bf16[4,256,128]{2,1,0:T(8,128)(2,1)S(1)} %get-tuple-element.52.refs_3_, ...), custom_call_target="tpu_custom_call" | custom-call | flops 1610612736 | bytes 3145728 | tf_op jit(solution)/shard_map/attend/pallas_call | solution.py:259
  115.0 6.1 %collective-permute-done.13.refs_1_ = bf16[1024,128]{1,0:T(8,128)(2,1)S(1)} collective-permute-done((bf16[1024,128]{1,0:T(8,128)(2,1)S(1)}, bf16[1024,128]{1,0:T(8,128)(2,1)S(1)}, u32[]{:S(2)}, u32[]{:S(2)}) %collective-permute-start.13) | collective-permute-done | bytes 262176 | tf_op jit(solution)/shard_map/ppermute | solution.py:388
  121.0 0.4 last_head.1
  121.5 7.2 %collective-permute-start.15 = (bf16[96,1024]{1,0:T(8,128)(2,1)S(1)}, bf16[96,1024]{1,0:T(8,128)(2,1)S(1)}, u32[]{:S(2)}, u32[]{:S(2)}) collective-permute-start(bf16[96,1024]{1,0:T(8,128)(2,1)S(1)} %last_head.1), channel_id=1, source_target_pairs={{0,1},{1,2},{2,3},{3,4},{4,5},{5,6},{6,7},{7,0},{8,9},{9,10},{10,1... | collective-permute-start | bytes 589832 | tf_op jit(solution)/shard_map/ppermute | solution.py:390
  128.7 1.6 %merge.1 = (bf16[416,1024]{1,0:T(8,128)(2,1)}, bf16[96,1024]{1,0:T(8,128)(2,1)S(1)}) custom-call(bf16[1024,128]{1,0:T(8,128)(2,1)S(1)} %collective-permute-done.12.refs_0_, bf16[1024,128]{1,0:T(8,128)(2,1)S(1)} %collective-permute-done.13.refs_1_, bf16[1024,128]{1,0:T(8,128)(2,1)S(1)} %collective-permute-done.14.refs_2_, bf16[1024,128]{1,0:T(8,128)(2,1)S(1)} %attend.11.refs_3_), custom_call_target="tpu_custom_call" | custom-call | tf_op jit(solution)/shard_map/merge/pallas_call | solution.py:323
  130.3 2.0 %collective-permute-done.15.refs_1_ = bf16[96,1024]{1,0:T(8,128)(2,1)S(1)} collective-permute-done((bf16[96,1024]{1,0:T(8,128)(2,1)S(1)}, bf16[96,1024]{1,0:T(8,128)(2,1)S(1)}, u32[]{:S(2)}, u32[]{:S(2)}) %collective-permute-start.15) | collective-permute-done | bytes 196640 | tf_op jit(solution)/shard_map/ppermute | solution.py:390
  132.3 0.9 finish.1
  (16 shorter events, 0.7 us)
Async XLA Ops:
  2.2 16.4 %collective-permute-start = (bf16[1536,128]{1,0:T(8,128)(2,1)S(1)}, bf16[1536,128]{1,0:T(8,128)(2,1)S(1)}, u32[]{:S(2)}, u32[]{:S(2)}) collective-permute-start(bf16[1536,128]{1,0:T(8,128)(2,1)S(1)} %get-tuple-element.38), channel_id=1, source_target_pairs={{0,1},{1,2},{2,3},{3,4},{4,5},{5,6},{6,7},{7,0},{8,9},{9,10},{10,1... | collective-permute-start | bytes 1179656 | tf_op jit(solution)/shard_map/ppermute | solution.py:365
  4.2 19.1 %collective-permute-start.1 = (bf16[1536,128]{1,0:T(8,128)(2,1)S(1)}, bf16[1536,128]{1,0:T(8,128)(2,1)S(1)}, u32[]{:S(2)}, u32[]{:S(2)}) collective-permute-start(bf16[1536,128]{1,0:T(8,128)(2,1)S(1)} %get-tuple-element.39), channel_id=1, source_target_pairs={{0,7},{1,0},{2,1},{3,2},{4,3},{5,4},{6,5},{7,6},{8,15},{9,8},{10,9... | collective-permute-start | bytes 1179656 | tf_op jit(solution)/shard_map/ppermute | solution.py:365
  8.2 32.4 %collective-permute-start.2 = (bf16[1536,128]{1,0:T(8,128)(2,1)S(1)}, bf16[1536,128]{1,0:T(8,128)(2,1)S(1)}, u32[]{:S(2)}, u32[]{:S(2)}) collective-permute-start(bf16[1536,128]{1,0:T(8,128)(2,1)S(1)} %get-tuple-element.40), channel_id=1, source_target_pairs={{0,2},{1,3},{2,4},{3,5},{4,6},{5,7},{6,0},{7,1},{8,10},{9,11},{10,... | collective-permute-start | bytes 1179656 | tf_op jit(solution)/shard_map/ppermute | solution.py:365
  8.2 39.2 %collective-permute-start.3 = (bf16[1536,128]{1,0:T(8,128)(2,1)S(1)}, bf16[1536,128]{1,0:T(8,128)(2,1)S(1)}, u32[]{:S(2)}, u32[]{:S(2)}) collective-permute-start(bf16[1536,128]{1,0:T(8,128)(2,1)S(1)} %get-tuple-element.42), channel_id=1, source_target_pairs={{0,6},{1,7},{2,0},{3,1},{4,2},{5,3},{6,4},{7,5},{8,14},{9,15},{10,... | collective-permute-start | bytes 1179656 | tf_op jit(solution)/shard_map/ppermute | solution.py:365
  23.4 55.5 %collective-permute-start.4 = (bf16[2304,128]{1,0:T(8,128)(2,1)S(1)}, bf16[2304,128]{1,0:T(8,128)(2,1)S(1)}, u32[]{:S(2)}, u32[]{:S(2)}) collective-permute-start(bf16[2304,128]{1,0:T(8,128)(2,1)S(1)} %pass_on.2), channel_id=1, source_target_pairs={{0,8},{1,9},{2,10},{3,11},{4,12},{5,13},{6,14},{7,15},{8,0},{9,1},... | collective-permute-start | bytes 1769480 | tf_op jit(solution)/shard_map/ppermute | solution.py:368
  25.4 24.0 %collective-permute-start.8 = (bf16[768,128]{1,0:T(8,128)(2,1)S(1)}, bf16[768,128]{1,0:T(8,128)(2,1)S(1)}, u32[]{:S(2)}, u32[]{:S(2)}) collective-permute-start(bf16[768,128]{1,0:T(8,128)(2,1)S(1)} %get-tuple-element.48), channel_id=1, source_target_pairs={{0,11},{1,12},{2,13},{3,14},{5,8},{6,9},{7,10},{8,3},{9,4},{10,5},... | collective-permute-start | bytes 589832 | tf_op jit(solution)/shard_map/ppermute | solution.py:373
  36.7 19.9 %collective-permute-start.9 = (bf16[768,128]{1,0:T(8,128)(2,1)S(1)}, bf16[768,128]{1,0:T(8,128)(2,1)S(1)}, u32[]{:S(2)}, u32[]{:S(2)}) collective-permute-start(bf16[768,128]{1,0:T(8,128)(2,1)S(1)} %get-tuple-element.49), channel_id=1, source_target_pairs={{0,13},{1,14},{3,8},{4,9},{5,10},{6,11},{7,12},{8,5},{10,7},{11,0}... | collective-permute-start | bytes 589832 | tf_op jit(solution)/shard_map/ppermute | solution.py:373
  40.6 19.1 %collective-permute-start.10 = (bf16[768,128]{1,0:T(8,128)(2,1)S(1)}, bf16[768,128]{1,0:T(8,128)(2,1)S(1)}, u32[]{:S(2)}, u32[]{:S(2)}) collective-permute-start(bf16[768,128]{1,0:T(8,128)(2,1)S(1)} %get-tuple-element.50), channel_id=1, source_target_pairs={{0,4},{1,5},{3,7},{4,0},{6,2},{7,3},{8,12},{9,13},{10,14},{12,8},{... | collective-permute-start | bytes 589832 | tf_op jit(solution)/shard_map/ppermute | solution.py:373
  47.5 31.3 %collective-permute-start.5 = (bf16[1536,128]{1,0:T(8,128)(2,1)S(1)}, bf16[1536,128]{1,0:T(8,128)(2,1)S(1)}, u32[]{:S(2)}, u32[]{:S(2)}) collective-permute-start(bf16[1536,128]{1,0:T(8,128)(2,1)S(1)} %pass_on.3), channel_id=1, source_target_pairs={{0,8},{1,9},{2,10},{3,11},{4,12},{5,13},{6,14},{7,15},{8,0},{9,1},... | collective-permute-start | bytes 1179656 | tf_op jit(solution)/shard_map/ppermute | solution.py:368
  49.5 22.3 %collective-permute-start.11 = (bf16[768,128]{1,0:T(8,128)(2,1)S(1)}, bf16[768,128]{1,0:T(8,128)(2,1)S(1)}, u32[]{:S(2)}, u32[]{:S(2)}) collective-permute-start(bf16[768,128]{1,0:T(8,128)(2,1)S(1)} %get-tuple-element.51), channel_id=1, source_target_pairs={{0,12},{1,13},{2,14},{4,8},{5,9},{6,10},{7,11},{8,4},{9,5},{11,7},... | collective-permute-start | bytes 589832 | tf_op jit(solution)/shard_map/ppermute | solution.py:373
  56.6 19.7 %collective-permute-start.6 = (bf16[768,128]{1,0:T(8,128)(2,1)S(1)}, bf16[768,128]{1,0:T(8,128)(2,1)S(1)}, u32[]{:S(2)}, u32[]{:S(2)}) collective-permute-start(bf16[768,128]{1,0:T(8,128)(2,1)S(1)} %get-tuple-element.45), channel_id=1, source_target_pairs={{0,3},{1,4},{2,5},{4,7},{5,0},{7,2},{8,11},{9,12},{10,13},{11,14},... | collective-permute-start | bytes 589832 | tf_op jit(solution)/shard_map/ppermute | solution.py:373
  59.7 19.1 %collective-permute-start.7 = (bf16[768,128]{1,0:T(8,128)(2,1)S(1)}, bf16[768,128]{1,0:T(8,128)(2,1)S(1)}, u32[]{:S(2)}, u32[]{:S(2)}) collective-permute-start(bf16[768,128]{1,0:T(8,128)(2,1)S(1)} %get-tuple-element.46), channel_id=1, source_target_pairs={{0,5},{2,7},{3,0},{5,2},{6,3},{7,4},{8,13},{9,14},{11,8},{12,9},{1... | collective-permute-start | bytes 589832 | tf_op jit(solution)/shard_map/ppermute | solution.py:373
  96.7 18.3 %collective-permute-start.12 = (bf16[1024,128]{1,0:T(8,128)(2,1)S(1)}, bf16[1024,128]{1,0:T(8,128)(2,1)S(1)}, u32[]{:S(2)}, u32[]{:S(2)}) collective-permute-start(bf16[1024,128]{1,0:T(8,128)(2,1)S(1)} %attend.8), channel_id=1, source_target_pairs={{0,12},{2,14},{3,15},{4,8},{5,9},{7,11},{8,4},{9,5},{10,6},{11,7},... | collective-permute-start | bytes 786440 | tf_op jit(solution)/shard_map/ppermute | solution.py:388
  102.8 18.2 %collective-permute-start.13 = (bf16[1024,128]{1,0:T(8,128)(2,1)S(1)}, bf16[1024,128]{1,0:T(8,128)(2,1)S(1)}, u32[]{:S(2)}, u32[]{:S(2)}) collective-permute-start(bf16[1024,128]{1,0:T(8,128)(2,1)S(1)} %attend.9), channel_id=1, source_target_pairs={{0,4},{2,6},{3,7},{4,0},{5,1},{7,3},{8,12},{9,13},{10,14},{11,15},... | collective-permute-start | bytes 786440 | tf_op jit(solution)/shard_map/ppermute | solution.py:388
  107.4 13.7 %collective-permute-start.14 = (bf16[1024,128]{1,0:T(8,128)(2,1)S(1)}, bf16[1024,128]{1,0:T(8,128)(2,1)S(1)}, u32[]{:S(2)}, u32[]{:S(2)}) collective-permute-start(bf16[1024,128]{1,0:T(8,128)(2,1)S(1)} %attend.10), channel_id=1, source_target_pairs={{0,8},{2,10},{3,11},{4,12},{5,13},{7,15},{8,0},{9,1},{10,2},{11,3}... | collective-permute-start | bytes 786440 | tf_op jit(solution)/shard_map/ppermute | solution.py:388
  121.5 10.8 %collective-permute-start.15 = (bf16[96,1024]{1,0:T(8,128)(2,1)S(1)}, bf16[96,1024]{1,0:T(8,128)(2,1)S(1)}, u32[]{:S(2)}, u32[]{:S(2)}) collective-permute-start(bf16[96,1024]{1,0:T(8,128)(2,1)S(1)} %last_head.1), channel_id=1, source_target_pairs={{0,1},{1,2},{2,3},{3,4},{4,5},{5,6},{6,7},{7,0},{8,9},{9,10},{10,1... | collective-permute-start | bytes 589832 | tf_op jit(solution)/shard_map/ppermute | solution.py:390
